TPU v7x, 32 devices: a whole 2x2x4 slice. The times are simulated.
32 devices in a mesh: dp: 16 (over z, x, core), tensor: 2 (over y).
Axes of the slice: x: 2, y: 2, z: 4, core: 2. Of those that a mesh axis runs over, the one named last changes fastest.
Arguments:
- tokens: bfloat16 [8192, 1152], P(('dp', 'tensor')), may hold values from -6 to 6
- cotangent: bfloat16 [8192, 1152], P(('dp', 'tensor')), may hold values from -6 to 6
- lengths: int32 [16, 2], P('dp'), may hold values from 128 to 384, as said below
- grid_width: int32 [16, 2], P('dp'), may hold values from 4 to 32
- timestep: int32 [16, 2], P('dp'), may hold values from 0 to 999
- class_id: int32 [16, 2], P('dp'), may hold values from 0 to 999
- class_table: bfloat16 [1000, 1152], replicated, may hold values from -6 to 6
- ada_weight: float32 [1152, 6, 1152], P('dp', None, 'tensor'), may hold values from -0.1875 to 0.1875
- ada_m: float32 [1152, 6, 1152], P('dp', None, 'tensor'), may hold values from -1.5 to 1.5
- ada_v: float32 [1152, 6, 1152], P('dp', None, 'tensor'), may hold values from 0.04308992 to 0.172032
- ada_bias: float32 [6, 1152], replicated, may hold values from -3 to 3
- bias_m: float32 [6, 1152], replicated, may hold values from -1.5 to 1.5
- bias_v: float32 [6, 1152], replicated, may hold values from 0.04308992 to 0.172032
- qkv_weight: float32 [1152, 3, 1152], P('dp', None, 'tensor'), may hold values from -0.1875 to 0.1875
- qkv_m: float32 [1152, 3, 1152], P('dp', None, 'tensor'), may hold values from -1.5 to 1.5
- qkv_v: float32 [1152, 3, 1152], P('dp', None, 'tensor'), may hold values from 0.04308992 to 0.172032
- out_weight: float32 [1152, 1152], P('dp', 'tensor'), may hold values from -1.5 to 1.5
- out_m: float32 [1152, 1152], P('dp', 'tensor'), may hold values from -1.5 to 1.5
- out_v: float32 [1152, 1152], P('dp', 'tensor'), may hold values from 0.04308992 to 0.172032
- gateup_weight: float32 [1152, 2, 3072], P('dp', None, 'tensor'), may hold values from -0.1875 to 0.1875
- gateup_m: float32 [1152, 2, 3072], P('dp', None, 'tensor'), may hold values from -1.5 to 1.5
- gateup_v: float32 [1152, 2, 3072], P('dp', None, 'tensor'), may hold values from 0.04308992 to 0.172032
- down_weight: float32 [1152, 3072], P('dp', 'tensor'), may hold values from -0.109375 to 0.109375
- down_m: float32 [1152, 3072], P('dp', 'tensor'), may hold values from -1.5 to 1.5
- down_v: float32 [1152, 3072], P('dp', 'tensor'), may hold values from 0.04308992 to 0.172032
- qk_gain: float32 [2, 72], replicated, may hold values from 0.25 to 1.75
- gain_m: float32 [2, 72], replicated, may hold values from -3 to 3
- gain_v: float32 [2, 72], replicated, may hold values from 0.172032 to 0.69632
Outputs:
- out_tokens: bfloat16 [8192, 1152], P(('dp', 'tensor'))
- input_grad: bfloat16 [8192, 1152], P(('dp', 'tensor'))
- grad_norm: float32 [], replicated
- new_ada_weight: float32 [1152, 6, 1152], P('dp', None, 'tensor')
- new_ada_m: float32 [1152, 6, 1152], P('dp', None, 'tensor')
- new_ada_v: float32 [1152, 6, 1152], P('dp', None, 'tensor')
- new_ada_bias: float32 [6, 1152], replicated
- new_bias_m: float32 [6, 1152], replicated
- new_bias_v: float32 [6, 1152], replicated
- new_qkv_weight: float32 [1152, 3, 1152], P('dp', None, 'tensor')
- new_qkv_m: float32 [1152, 3, 1152], P('dp', None, 'tensor')
- new_qkv_v: float32 [1152, 3, 1152], P('dp', None, 'tensor')
- new_out_weight: float32 [1152, 1152], P('dp', 'tensor')
- new_out_m: float32 [1152, 1152], P('dp', 'tensor')
- new_out_v: float32 [1152, 1152], P('dp', 'tensor')
- new_gateup_weight: float32 [1152, 2, 3072], P('dp', None, 'tensor')
- new_gateup_m: float32 [1152, 2, 3072], P('dp', None, 'tensor')
- new_gateup_v: float32 [1152, 2, 3072], P('dp', None, 'tensor')
- new_down_weight: float32 [1152, 3072], P('dp', 'tensor')
- new_down_m: float32 [1152, 3072], P('dp', 'tensor')
- new_down_v: float32 [1152, 3072], P('dp', 'tensor')
- new_qk_gain: float32 [2, 72], replicated
- new_gain_m: float32 [2, 72], replicated
- new_gain_v: float32 [2, 72], replicated
Inputs may be any that keep to these rules, and one draw needn't show every extreme that they name: Each row holds the lengths of one group's items in row order; they sum to 512, each is at most 384, and some row holds an item of exactly 384. `grid_width`: an item's patches fill its grid row by row.
All inputs are finite; a program needn't handle non-finite values.
Results may differ from a plain program's by a relative error of at most 0.015.
Values may be sent and summed in bfloat16 or wider, within the bound.
No kernel may reach another device: no remote copies, remote signals or barrier semaphores. Data moves between devices by JAX's collectives and lax.ppermute only.
A program may use at most 192 MiB of HBM per device.

v0:
```python
from functools import partial
import math

import jax
import jax.numpy as jnp
from jax import lax
from jax.sharding import PartitionSpec as P

D = 1152
HD = 72
FF = 3072
STEP = 10


EPSILON = 1e-06
NEG_FILL = -1e30
PRECISE = lax.Precision.HIGHEST
BETA_FIRST = 0.9
BETA_SECOND = 0.95
ADAM_EPSILON = 1e-08
DECAY_RATE = 0.01
SMALL_RATE = 0.5


def rms_scaled(values):
    return values * lax.rsqrt(jnp.mean(values * values, axis=-1, keepdims=True) + EPSILON)


def modulate_in(base_rows, scale_rows, shift_rows):
    return rms_scaled(base_rows) * (1.0 + scale_rows) + shift_rows


def time_embed(step_ids, width):
    half_width = width // 2
    frequency = jnp.exp(-math.log(10000.0) * jnp.arange(half_width, dtype=jnp.float32) / half_width)
    angles = step_ids.astype(jnp.float32)[..., None] * frequency
    return jnp.concatenate([jnp.cos(angles), jnp.sin(angles)], axis=-1)


def layout(item_lengths, item_widths, row_index):
    ends_at = jnp.cumsum(item_lengths)
    starts_at = ends_at - item_lengths
    segment = jnp.sum((row_index[:, None] >= ends_at[None, :]).astype(jnp.int32), axis=1)
    member = segment[:, None] == jnp.arange(item_lengths.shape[0], dtype=jnp.int32)[None, :]
    offset = jnp.sum(jnp.where(member, starts_at[None, :], 0), axis=1)
    grid_span = jnp.sum(jnp.where(member, item_widths[None, :], 0), axis=1)
    inside = row_index - offset
    return (segment, inside // grid_span, inside % grid_span)


def rope_tables(grid_row, grid_col, head_size):
    quarter = head_size // 4
    frequency = jnp.exp(-math.log(10000.0) * jnp.arange(quarter, dtype=jnp.float32) / quarter)
    row_angle = grid_row.astype(jnp.float32)[:, None] * frequency[None, :]
    col_angle = grid_col.astype(jnp.float32)[:, None] * frequency[None, :]
    return (jnp.cos(row_angle), jnp.sin(row_angle), jnp.cos(col_angle), jnp.sin(col_angle))


def turn_half(part, cosine, sine):
    quarter = part.shape[-1] // 2
    first_part = part[..., :quarter]
    second_part = part[..., quarter:]
    cosine = cosine[:, None, :]
    sine = sine[:, None, :]
    return jnp.concatenate(
        [first_part * cosine - second_part * sine, first_part * sine + second_part * cosine],
        axis=-1,
    )


def rotate(values, tables):
    half_size = values.shape[-1] // 2
    return jnp.concatenate(
        [
            turn_half(values[..., :half_size], tables[0], tables[1]),
            turn_half(values[..., half_size:], tables[2], tables[3]),
        ],
        axis=-1,
    )


def qk_prepare(raw_query, raw_key, gains, tables):
    head_size = gains.shape[1]
    row_count = raw_query.shape[0]
    head_count = raw_query.shape[1] // head_size
    query_norm = rms_scaled(raw_query.reshape(row_count, head_count, head_size)) * gains[0]
    key_norm = rms_scaled(raw_key.reshape(row_count, head_count, head_size)) * gains[1]
    return (rotate(query_norm, tables), rotate(key_norm, tables))


def block_geometry(total_rows):
    query_block = min(512, total_rows)
    return (query_block, total_rows, total_rows // query_block)


def window_start(block_index, query_block, key_window, total_rows):
    return jnp.clip(block_index * query_block - query_block, 0, total_rows - key_window)


def masked_scores(query_low, key_low, segment, block_index, query_block, key_window):
    total_rows = query_low.shape[0]
    scale = query_low.shape[2] ** (-0.5)
    query_start = block_index * query_block
    key_start = window_start(block_index, query_block, key_window, total_rows)
    queries = lax.dynamic_slice_in_dim(query_low, query_start, query_block, 0)
    seg_query = lax.dynamic_slice_in_dim(segment, query_start, query_block, 0)
    scores = (
        jnp.einsum("qhe,khe->hqk", queries, key_low, preferred_element_type=jnp.float32) * scale
    )
    allowed = (seg_query[:, None] == segment[None, :])[None]
    return (jnp.where(allowed, scores, NEG_FILL), queries, key_low, query_start, key_start)


def attend(query_low, key_low, value_low, segment):
    total_rows = query_low.shape[0]
    query_block, key_window, block_count = block_geometry(total_rows)

    def one_block(block_index):
        scores, queries, keyset, query_start, key_start = masked_scores(
            query_low, key_low, segment, block_index, query_block, key_window
        )
        peak = jnp.max(scores, axis=-1, keepdims=True)
        expo = jnp.exp(scores - peak)
        total_exp = jnp.sum(expo, axis=-1, keepdims=True)
        probs = (expo / total_exp).astype(jnp.bfloat16)
        result = jnp.einsum("hqk,khe->qhe", probs, value_low, preferred_element_type=jnp.float32)
        return (result, (peak + jnp.log(total_exp))[..., 0])

    outputs, log_sums = lax.map(one_block, jnp.arange(block_count, dtype=jnp.int32))
    return (outputs.reshape(total_rows, query_low.shape[1], query_low.shape[2]), log_sums)


def attend_back(query_low, key_low, value_low, d_attn, log_sums, segment):
    total_rows = query_low.shape[0]
    query_block, key_window, block_count = block_geometry(total_rows)
    scale = query_low.shape[2] ** (-0.5)
    zeros_like = jnp.zeros(query_low.shape, jnp.float32)

    def one_block(carry, block_index):
        d_keys, d_values = carry
        scores, queries, keyset, query_start, key_start = masked_scores(
            query_low, key_low, segment, block_index, query_block, key_window
        )
        grads_block = lax.dynamic_slice_in_dim(d_attn, query_start, query_block, 0)
        probs = jnp.exp(scores - log_sums[block_index][:, :, None])
        low_probs = probs.astype(jnp.bfloat16)
        d_probs = jnp.einsum(
            "qhe,khe->hqk", grads_block, value_low, preferred_element_type=jnp.float32
        )
        row_dot = jnp.sum(probs * d_probs, axis=-1, keepdims=True)
        d_scores = (probs * (d_probs - row_dot)).astype(jnp.bfloat16)
        d_query = (
            jnp.einsum("hqk,khe->qhe", d_scores, keyset, preferred_element_type=jnp.float32) * scale
        )
        d_key_part = (
            jnp.einsum("hqk,qhe->khe", d_scores, queries, preferred_element_type=jnp.float32)
            * scale
        )
        d_value_part = jnp.einsum(
            "hqk,qhe->khe", low_probs, grads_block, preferred_element_type=jnp.float32
        )
        d_keys = d_keys + d_key_part
        d_values = d_values + d_value_part
        return ((d_keys, d_values), d_query)

    (d_keys, d_values), d_queries = lax.scan(
        one_block, (zeros_like, zeros_like), jnp.arange(block_count, dtype=jnp.int32)
    )
    return (d_queries.reshape(query_low.shape), d_keys, d_values)


def reduce_grads(values):
    return (
        lax.psum_scatter(values[0], "dp", scatter_dimension=0, tiled=True),
        lax.psum_scatter(values[1], "dp", scatter_dimension=0, tiled=True),
        lax.psum_scatter(values[2], "dp", scatter_dimension=0, tiled=True),
        lax.psum_scatter(values[3], "dp", scatter_dimension=0, tiled=True),
        lax.psum_scatter(values[4], "dp", scatter_dimension=0, tiled=True),
    )


def adam_update(weight, first_moment, second_moment, gradient, rate, clip):
    clipped = gradient * clip
    new_first = BETA_FIRST * first_moment + (1.0 - BETA_FIRST) * clipped
    new_second = BETA_SECOND * second_moment + (1.0 - BETA_SECOND) * clipped * clipped
    unbiased_first = new_first / (1.0 - BETA_FIRST**STEP)
    unbiased_second = new_second / (1.0 - BETA_SECOND**STEP)
    new_weight = weight - rate * (
        unbiased_first / (jnp.sqrt(unbiased_second) + ADAM_EPSILON) + DECAY_RATE * weight
    )
    return (new_weight, new_first, new_second)


def local(
    tokens,
    cotangent,
    lengths,
    grid_width,
    timestep,
    class_id,
    class_table,
    ada_weight,
    ada_m,
    ada_v,
    ada_bias,
    bias_m,
    bias_v,
    qkv_weight,
    qkv_m,
    qkv_v,
    out_weight,
    out_m,
    out_v,
    gateup_weight,
    gateup_m,
    gateup_v,
    down_weight,
    down_m,
    down_v,
    qk_gain,
    gain_m,
    gain_v,
):
    tensor_count = lax.axis_size("tensor")
    data_count = lax.axis_size("dp")
    tensor_rank = lax.axis_index("tensor")
    local_rows = tokens.shape[0]
    model_width = tokens.shape[1]
    group_rows = local_rows * tensor_count
    column_share = model_width // tensor_count
    head_size = qk_gain.shape[1]
    item_count = lengths.shape[1]
    class_count = class_table.shape[0]
    full_ada, full_qkv, full_out, full_gateup, full_down = (
        lax.all_gather(ada_weight.astype(jnp.bfloat16), "dp", axis=0, tiled=True),
        lax.all_gather(qkv_weight.astype(jnp.bfloat16), "dp", axis=0, tiled=True),
        lax.all_gather(out_weight.astype(jnp.bfloat16), "dp", axis=0, tiled=True),
        lax.all_gather(gateup_weight.astype(jnp.bfloat16), "dp", axis=0, tiled=True),
        lax.all_gather(down_weight.astype(jnp.bfloat16), "dp", axis=0, tiled=True),
    )
    class_onehot = (
        class_id[0][:, None] == jnp.arange(class_count, dtype=jnp.int32)[None, :]
    ).astype(jnp.bfloat16)
    condition = jnp.dot(class_onehot, class_table, preferred_element_type=jnp.float32) + time_embed(
        timestep[0], model_width
    )
    silu_cond = jax.nn.silu(condition).astype(jnp.bfloat16)
    bias_share = lax.dynamic_slice_in_dim(ada_bias, tensor_rank * column_share, column_share, 1)
    mod_share = (
        jnp.einsum("id,dke->ike", silu_cond, full_ada, preferred_element_type=jnp.float32)
        + bias_share[None]
    )
    modulation = lax.all_gather(mod_share, "tensor", axis=2, tiled=True)
    segment_all, grid_row, grid_col = layout(
        lengths[0], grid_width[0], jnp.arange(group_rows, dtype=jnp.int32)
    )
    segment_mine = lax.dynamic_slice_in_dim(segment_all, tensor_rank * local_rows, local_rows, 0)
    member_rows = (
        segment_mine[:, None] == jnp.arange(item_count, dtype=jnp.int32)[None, :]
    ).astype(jnp.float32)
    mod_rows = jnp.dot(
        member_rows,
        modulation.reshape(item_count, 6 * model_width),
        precision=PRECISE,
        preferred_element_type=jnp.float32,
    ).reshape(local_rows, 6, model_width)
    shift_one, scale_one, gate_one, shift_two, scale_two, gate_two = [
        mod_rows[:, slot_index] for slot_index in range(6)
    ]
    tables = rope_tables(grid_row, grid_col, head_size)
    base_rows = tokens.astype(jnp.float32)
    attn_in = modulate_in(base_rows, scale_one, shift_one).astype(jnp.bfloat16)
    gathered = lax.all_gather(attn_in, "tensor", axis=0, tiled=True)
    qkv_raw = jnp.einsum("gd,dkc->kgc", gathered, full_qkv, preferred_element_type=jnp.float32)
    query_rot, key_rot = qk_prepare(qkv_raw[0], qkv_raw[1], qk_gain, tables)
    query_low = query_rot.astype(jnp.bfloat16)
    key_low = key_rot.astype(jnp.bfloat16)
    value_low = qkv_raw[2].reshape(group_rows, -1, head_size).astype(jnp.bfloat16)
    attn_vals, log_sums = attend(query_low, key_low, value_low, segment_all)
    attn_low = attn_vals.reshape(group_rows, column_share).astype(jnp.bfloat16)
    picked = attn_low
    branch = lax.psum_scatter(
        jnp.einsum("gc,dc->gd", picked, full_out, preferred_element_type=jnp.float32),
        "tensor",
        scatter_dimension=0,
        tiled=True,
    )
    attn_saved = (gathered, qkv_raw, query_low, key_low, value_low, attn_low, log_sums, branch)
    mid_rows = base_rows + gate_one * attn_saved[7]
    mlp_in = modulate_in(mid_rows, scale_two, shift_two).astype(jnp.bfloat16)
    gathered_mlp = lax.all_gather(mlp_in, "tensor", axis=0, tiled=True)
    gate_up = jnp.einsum(
        "gd,dkf->kgf", gathered_mlp, full_gateup, preferred_element_type=jnp.float32
    )
    hidden = (jax.nn.silu(gate_up[0]) * gate_up[1]).astype(jnp.bfloat16)
    picked = hidden
    branch_mlp = lax.psum_scatter(
        jnp.einsum("gf,df->gd", picked, full_down, preferred_element_type=jnp.float32),
        "tensor",
        scatter_dimension=0,
        tiled=True,
    )
    mlp_saved = (gathered_mlp, gate_up, hidden, branch_mlp)
    out_rows = mid_rows + gate_two * mlp_saved[3]
    gathered, qkv_raw, query_low, key_low, value_low, attn_low, log_sums, branch = attn_saved
    gathered_mlp, gate_up, hidden, branch_mlp = mlp_saved
    cot_rows = cotangent.astype(jnp.float32)
    d_gate_two = cot_rows * branch_mlp
    d_branch_mlp = (gate_two * cot_rows).astype(jnp.bfloat16)
    d_branch_all = lax.all_gather(d_branch_mlp, "tensor", axis=0, tiled=True)
    g_down = jnp.einsum("gd,gf->df", d_branch_all, hidden, preferred_element_type=jnp.float32)
    d_hidden = jnp.einsum("gd,df->gf", d_branch_all, full_down, preferred_element_type=jnp.float32)
    gate_vals = gate_up[0]
    up_vals = gate_up[1]
    sigmoid = jax.nn.sigmoid(gate_vals)
    d_gate = d_hidden * up_vals * sigmoid * (1.0 + gate_vals * (1.0 - sigmoid))
    d_up = d_hidden * gate_vals * sigmoid
    d_gateup_low = jnp.stack([d_gate, d_up]).astype(jnp.bfloat16)
    g_gateup = jnp.einsum(
        "gd,kgf->dkf", gathered_mlp, d_gateup_low, preferred_element_type=jnp.float32
    )
    picked = d_gateup_low
    d_mlp_in = lax.psum_scatter(
        jnp.einsum("kgf,dkf->gd", picked, full_gateup, preferred_element_type=jnp.float32),
        "tensor",
        scatter_dimension=0,
        tiled=True,
    )
    _, pull_two = jax.vjp(modulate_in, mid_rows, scale_two, shift_two)
    d_mid_norm, d_scale_two, d_shift_two = pull_two(d_mlp_in)
    d_mid = cot_rows + d_mid_norm
    d_gate_one = d_mid * branch
    d_branch_attn = (gate_one * d_mid).astype(jnp.bfloat16)
    d_attn_all = lax.all_gather(d_branch_attn, "tensor", axis=0, tiled=True)
    g_out = jnp.einsum("gd,gc->dc", d_attn_all, attn_low, preferred_element_type=jnp.float32)
    d_attn = jnp.einsum("gd,dc->gc", d_attn_all, full_out, preferred_element_type=jnp.float32)
    d_attn = d_attn.astype(jnp.bfloat16).reshape(query_low.shape)
    d_query_rot, d_key_rot, d_values = attend_back(
        query_low, key_low, value_low, d_attn, log_sums, segment_all
    )
    _, pull_qk = jax.vjp(partial(qk_prepare, tables=tables), qkv_raw[0], qkv_raw[1], qk_gain)
    d_query_raw, d_key_raw, g_gain = pull_qk((d_query_rot, d_key_rot))
    d_qkv_low = jnp.stack(
        [d_query_raw, d_key_raw, d_values.reshape(group_rows, column_share)]
    ).astype(jnp.bfloat16)
    g_qkv = jnp.einsum("gd,kgc->dkc", gathered, d_qkv_low, preferred_element_type=jnp.float32)
    picked = d_qkv_low
    d_attn_in = lax.psum_scatter(
        jnp.einsum("kgc,dkc->gd", picked, full_qkv, preferred_element_type=jnp.float32),
        "tensor",
        scatter_dimension=0,
        tiled=True,
    )
    _, pull_one = jax.vjp(modulate_in, base_rows, scale_one, shift_one)
    d_base_norm, d_scale_one, d_shift_one = pull_one(d_attn_in)
    input_grad = (d_mid + d_base_norm).astype(jnp.bfloat16)
    d_rows = jnp.stack(
        [d_shift_one, d_scale_one, d_gate_one, d_shift_two, d_scale_two, d_gate_two], axis=1
    )
    d_mod_part = jnp.einsum(
        "ri,rke->ike", member_rows, d_rows, precision=PRECISE, preferred_element_type=jnp.float32
    )
    d_mod = lax.psum_scatter(d_mod_part, "tensor", scatter_dimension=2, tiled=True)
    g_ada = jnp.einsum(
        "id,ike->dke",
        silu_cond.astype(jnp.float32),
        d_mod,
        precision=PRECISE,
        preferred_element_type=jnp.float32,
    )
    bias_total = jnp.sum(d_mod, axis=0)
    slot_mask = (jnp.arange(tensor_count, dtype=jnp.int32) == tensor_rank)[None, :, None]
    bias_slots = jnp.where(slot_mask, bias_total[:, None, :], 0.0).reshape(6, model_width)
    sum_ada, sum_qkv, sum_out, sum_gateup, sum_down = reduce_grads(
        (g_ada, g_qkv, g_out, g_gateup, g_down)
    )
    local_squares = (
        jnp.sum(sum_ada * sum_ada) + jnp.sum(sum_qkv * sum_qkv) + jnp.sum(sum_out * sum_out)
    )
    local_squares = local_squares + jnp.sum(sum_gateup * sum_gateup) + jnp.sum(sum_down * sum_down)
    total_squares, gain_total, bias_grad = lax.psum(
        (local_squares, g_gain, bias_slots), ("dp", "tensor")
    )
    grad_norm = jnp.sqrt(
        total_squares + jnp.sum(gain_total * gain_total) + jnp.sum(bias_grad * bias_grad)
    )
    tokens_all = local_rows * tensor_count * data_count
    params_all = 10 * D * D + 3 * D * FF + 6 * D + 2 * HD
    limit = 0.01 * math.sqrt(tokens_all * params_all)
    clip = limit / jnp.maximum(grad_norm, limit)
    matrix_rate = model_width ** (-0.5)
    new_ada = adam_update(ada_weight, ada_m, ada_v, sum_ada, matrix_rate, clip)
    new_bias = adam_update(ada_bias, bias_m, bias_v, bias_grad, SMALL_RATE, clip)
    new_qkv = adam_update(qkv_weight, qkv_m, qkv_v, sum_qkv, matrix_rate, clip)
    new_out = adam_update(out_weight, out_m, out_v, sum_out, (model_width // 64) ** (-0.5), clip)
    new_gateup = adam_update(gateup_weight, gateup_m, gateup_v, sum_gateup, matrix_rate, clip)
    new_down = adam_update(down_weight, down_m, down_v, sum_down, FF ** (-0.5), clip)
    new_gain = adam_update(qk_gain, gain_m, gain_v, gain_total, SMALL_RATE, clip)
    return (
        out_rows.astype(jnp.bfloat16),
        input_grad,
        grad_norm,
        new_ada[0],
        new_ada[1],
        new_ada[2],
        new_bias[0],
        new_bias[1],
        new_bias[2],
        new_qkv[0],
        new_qkv[1],
        new_qkv[2],
        new_out[0],
        new_out[1],
        new_out[2],
        new_gateup[0],
        new_gateup[1],
        new_gateup[2],
        new_down[0],
        new_down[1],
        new_down[2],
        new_gain[0],
        new_gain[1],
        new_gain[2],
    )


def solution(mesh):
    in_specs = (
        P(("dp", "tensor"), None),
        P(("dp", "tensor"), None),
        P("dp", None),
        P("dp", None),
        P("dp", None),
        P("dp", None),
        P(),
        P("dp", None, "tensor"),
        P("dp", None, "tensor"),
        P("dp", None, "tensor"),
        P(),
        P(),
        P(),
        P("dp", None, "tensor"),
        P("dp", None, "tensor"),
        P("dp", None, "tensor"),
        P("dp", "tensor"),
        P("dp", "tensor"),
        P("dp", "tensor"),
        P("dp", None, "tensor"),
        P("dp", None, "tensor"),
        P("dp", None, "tensor"),
        P("dp", "tensor"),
        P("dp", "tensor"),
        P("dp", "tensor"),
        P(),
        P(),
        P(),
    )
    out_specs = (
        P(("dp", "tensor"), None),
        P(("dp", "tensor"), None),
        P(),
        P("dp", None, "tensor"),
        P("dp", None, "tensor"),
        P("dp", None, "tensor"),
        P(),
        P(),
        P(),
        P("dp", None, "tensor"),
        P("dp", None, "tensor"),
        P("dp", None, "tensor"),
        P("dp", "tensor"),
        P("dp", "tensor"),
        P("dp", "tensor"),
        P("dp", None, "tensor"),
        P("dp", None, "tensor"),
        P("dp", None, "tensor"),
        P("dp", "tensor"),
        P("dp", "tensor"),
        P("dp", "tensor"),
        P(),
        P(),
        P(),
    )
    return jax.shard_map(local, mesh=mesh, in_specs=in_specs, out_specs=out_specs, check_vma=False)
```

profile of v0, /device:TPU:0, one launch (start us, length us, event | category | flops | bytes accessed | tf_op | source)
XLA Modules:
  0.0 1305.7 jit_solution(12392125756101383047)
XLA Ops:
  12.2 78.5 %all-gather.10.cloned.1.call-done = bf16[1152,6,576]{2,0,1:T(8,128)(2,1)} async-done(((bf16[72,6,576]{2,0,1:T(8,128)(2,1)}), bf16[1152,6,576]{2,0,1:T(8,128)(2,1)}) %all-gather.10.cloned.1.call-update) | async-done | bytes 7962640 | tf_op jit(solution)/shard_map/all_gather | solution.py:235
  95.8 16.1 %all_gather.31 = f32[2,6,1152]{1,0,2:T(2,128)S(1)} all-gather(f32[2,6,576]{1,0,2:T(2,128)S(1)} %copy.97), channel_id=1, replica_groups=mesh['dp'=16,'tensor'=2] {'tensor'}, dimensions={2}, use_global_device_ids=true | all-gather | bytes 82944 | tf_op jit(solution)/shard_map/all_gather | solution.py:253
  122.7 21.0 %all-gather.14.cloned.1.call-done = bf16[1152,3,576]{2,0,1:T(8,128)(2,1)} async-done(((bf16[72,3,576]{2,0,1:T(8,128)(2,1)}), bf16[1152,3,576]{2,0,1:T(8,128)(2,1)}) %all-gather.14.cloned.1.call-update) | async-done | bytes 3981328 | tf_op jit(solution)/shard_map/all_gather | solution.py:236
  143.7 23.4 %all-gather.12.cloned.1.call-done = bf16[512,1152]{1,0:T(8,128)(2,1)} async-done(((bf16[256,1152]{1,0:T(8,128)(2,1)}), bf16[512,1152]{1,0:T(8,128)(2,1)}) %all-gather.12.cloned.1.call-update) | async-done | bytes 1179664 | tf_op jit(solution)/shard_map/all_gather | solution.py:273
  183.8 25.1 %all-gather.16.cloned.1.call-done = bf16[1152,576]{1,0:T(8,128)(2,1)} async-done(((bf16[72,576]{1,0:T(8,128)(2,1)}), bf16[1152,576]{1,0:T(8,128)(2,1)}) %all-gather.16.cloned.1.call-update) | async-done | bytes 1327120 | tf_op jit(solution)/shard_map/all_gather | solution.py:237
  215.3 31.5 %reduce-scatter.15.cloned.1.call-done = f32[256,1152]{1,0:T(8,128)} async-done(((f32[512,1152]{1,0:T(8,128)}), f32[256,1152]{1,0:T(8,128)}) %reduce-scatter.15.cloned.1.call-update) | async-done | bytes 1179664 | tf_op jit(solution)/shard_map/reduce_scatter | solution.py:282
  254.7 61.0 %all-gather.20.cloned.1.call-done = bf16[1152,2,1536]{2,0,1:T(8,128)(2,1)} async-done(((bf16[72,2,1536]{2,0,1:T(8,128)(2,1)}), bf16[1152,2,1536]{2,0,1:T(8,128)(2,1)}) %all-gather.20.cloned.1.call-update) | async-done | bytes 7077904 | tf_op jit(solution)/shard_map/all_gather | solution.py:238
  315.7 23.7 %all-gather.18.cloned.1.call-done = bf16[512,1152]{1,0:T(8,128)(2,1)} async-done(((bf16[256,1152]{1,0:T(8,128)(2,1)}), bf16[512,1152]{1,0:T(8,128)(2,1)}) %all-gather.18.cloned.1.call-update) | async-done | bytes 1179664 | tf_op jit(solution)/shard_map/all_gather | solution.py:291
  339.4 10.3 convolution_bitcast_fusion
  349.6 39.8 %all-gather.22.cloned.1.call-done = bf16[1152,1536]{1,0:T(8,128)(2,1)} async-done(((bf16[72,1536]{1,0:T(8,128)(2,1)}), bf16[1152,1536]{1,0:T(8,128)(2,1)}) %all-gather.22.cloned.1.call-update) | async-done | bytes 3538960 | tf_op jit(solution)/shard_map/all_gather | solution.py:239
  389.4 23.5 %all-gather.24.cloned.1.call-done = bf16[512,1152]{1,0:T(8,128)(2,1)} async-done(((bf16[256,1152]{1,0:T(8,128)(2,1)}), bf16[512,1152]{1,0:T(8,128)(2,1)}) %all-gather.24.cloned.1.call-update) | async-done | bytes 1179664 | tf_op jit(solution)/shard_map/all_gather | solution.py:310
  412.9 8.6 fusion.10
  437.3 28.7 %reduce-scatter.19.cloned.1.call-done = f32[256,1152]{1,0:T(8,128)} async-done(((f32[512,1152]{1,0:T(8,128)}), f32[256,1152]{1,0:T(8,128)}) %reduce-scatter.19.cloned.1.call-update) | async-done | bytes 1179664 | tf_op jit(solution)/shard_map/reduce_scatter | solution.py:323
  468.2 34.8 %reduce-scatter.17.cloned.1.call-done = f32[256,1152]{1,0:T(8,128)} async-done(((f32[512,1152]{1,0:T(8,128)}), f32[256,1152]{1,0:T(8,128)}) %reduce-scatter.17.cloned.1.call-update) | async-done | bytes 1179664 | tf_op jit(solution)/shard_map/reduce_scatter | solution.py:297
  509.2 21.9 %all-gather.26.cloned.1.call-done = bf16[512,1152]{1,0:T(8,128)(2,1)} async-done(((bf16[256,1152]{1,0:T(8,128)(2,1)}), bf16[512,1152]{1,0:T(8,128)(2,1)}) %all-gather.26.cloned.1.call-update) | async-done | bytes 1179664 | tf_op jit(solution)/shard_map/all_gather | solution.py:334
  555.8 34.7 %reduce-scatter.21.cloned.1.call-done = f32[256,1152]{1,0:T(8,128)} async-done(((f32[512,1152]{1,0:T(8,128)}), f32[256,1152]{1,0:T(8,128)}) %reduce-scatter.21.cloned.1.call-update) | async-done | bytes 1179664 | tf_op jit(solution)/shard_map/reduce_scatter | solution.py:348
  629.6 9.1 fusion.6
  641.8 12.0 fusion.7
  654.0 37.4 %reduce-scatter.33.cloned.1.call-done = f32[72,576]{1,0:T(8,128)} async-done(((f32[1152,576]{1,0:T(8,128)}), f32[72,576]{1,0:T(8,128)}) %reduce-scatter.33.cloned.1.call-update) | async-done | bytes 165904
  694.6 89.6 %reduce-scatter.29.cloned.1.call-done = f32[72,1536]{1,0:T(8,128)} async-done(((f32[1152,1536]{1,0:T(8,128)}), f32[72,1536]{1,0:T(8,128)}) %reduce-scatter.29.cloned.1.call-update) | async-done | bytes 442384 | tf_op jit(solution)/shard_map/reduce_scatter | solution.py:178
  788.5 104.9 %reduce-scatter.25.cloned.1.call-done = f32[72,3,576]{2,0,1:T(8,128)} async-done(((f32[1152,3,576]{2,0,1:T(8,128)}), f32[72,3,576]{2,0,1:T(8,128)}) %reduce-scatter.25.cloned.1.call-update) | async-done | bytes 497680 | tf_op jit(solution)/shard_map/reduce_scatter | solution.py:175
  895.2 147.4 %reduce-scatter.27.cloned.1.call-done = f32[72,2,1536]{2,0,1:T(8,128)} async-done(((f32[1152,2,1536]{2,0,1:T(8,128)}), f32[72,2,1536]{2,0,1:T(8,128)}) %reduce-scatter.27.cloned.1.call-update) | async-done | bytes 884752 | tf_op jit(solution)/shard_map/reduce_scatter | solution.py:177
  1044.6 185.2 %reduce-scatter.23.cloned.1.call-done = f32[72,6,576]{2,0,1:T(8,128)} async-done(((f32[1152,6,576]{2,0,1:T(8,128)}), f32[72,6,576]{2,0,1:T(8,128)}) %reduce-scatter.23.cloned.1.call-update) | async-done | bytes 995344 | tf_op jit(solution)/shard_map/reduce_scatter | solution.py:174
  1237.7 39.8 %all-reduce.15 = (f32[]{:T(128)}, f32[2,72]{1,0:T(2,128)S(1)}, f32[6,1152]{1,0:T(8,128)S(1)}) all-reduce(f32[]{:T(128)S(6)} %add.365, f32[2,72]{1,0:T(2,128)S(1)} %pad_add_fusion.6, f32[6,1152]{1,0:T(8,128)S(1)} %broadcast_select_fusion), channel_id=1, replica_groups=mesh['dp'=16,'tensor'=2] {'dp','tensor'}, use_global_device_ids=true, to_apply=%region_30.31 | all-reduce | flops 7057 | bytes 56456 | tf_op jit(solution)/shard_map/psum | solution.py:381
  (344 shorter events, 175.8 us)
Async XLA Ops:
  7.2 83.5 %all-gather.10.cloned.1.call-start = ((), (), s32[]{:S(2)}) async-start(), calls=%async_computation.10 | async-start | bytes 9400320 | tf_op jit(solution)/shard_map/all_gather | solution.py:235
  9.6 134.1 %all-gather.14.cloned.1.call-start = ((), (), s32[]{:S(2)}) async-start(), calls=%async_computation.12 | async-start | bytes 4700160 | tf_op jit(solution)/shard_map/all_gather | solution.py:236
  10.4 156.7 %all-gather.12.cloned.1.call-start = ((), (), s32[]{:S(2)}) async-start(), calls=%async_computation.11 | async-start | bytes 1769472 | tf_op jit(solution)/shard_map/all_gather | solution.py:273
  10.8 102.1 %copy-start.77 = (s32[256]{0:T(256)}, s32[256]{0:T(256)S(1)}, u32[]{:S(2)}) copy-start(s32[256]{0:T(256)S(1)} %dynamic_slice.23) | copy-start | bytes 3076
  12.2 83.3 %copy-start.71 = (bf16[2,1152,1]{1,0,2:T(2,128)(2,1)}, bf16[2,1152,1]{1,0,2:T(2,128)(2,1)S(1)}, u32[]{:S(2)}) copy-start(bf16[2,1152,1]{1,0,2:T(2,128)(2,1)S(1)} %fusion.58) | copy-start | bytes 13828
  120.1 88.8 %all-gather.16.cloned.1.call-start = ((), (), s32[]{:S(2)}) async-start(), calls=%async_computation.13 | async-start | bytes 1566720 | tf_op jit(solution)/shard_map/all_gather | solution.py:237
  120.8 126.1 %reduce-scatter.15.cloned.1.call-start = ((), (), s32[]{:S(2)}) async-start(), calls=%async_computation.14 | async-start | bytes 3538944 | tf_op jit(solution)/shard_map/reduce_scatter | solution.py:282
  122.7 52.1 %copy-start.25 = (f32[512,18]{0,1:T(8,128)}, f32[512,18]{0,1:T(8,128)S(1)}, u32[]{:S(2)}) copy-start(f32[512,18]{0,1:T(8,128)S(1)} %get-tuple-element.247) | copy-start | bytes 110596
  122.7 52.1 %copy-start.27 = (f32[512,18]{0,1:T(8,128)}, f32[512,18]{0,1:T(8,128)S(1)}, u32[]{:S(2)}) copy-start(f32[512,18]{0,1:T(8,128)S(1)} %get-tuple-element.248) | copy-start | bytes 110596
  213.1 102.6 %all-gather.20.cloned.1.call-start = ((), (), s32[]{:S(2)}) async-start(), calls=%async_computation.16 | async-start | bytes 7520256 | tf_op jit(solution)/shard_map/all_gather | solution.py:238
  215.3 124.1 %all-gather.18.cloned.1.call-start = ((), (), s32[]{:S(2)}) async-start(), calls=%async_computation.15 | async-start | bytes 1769472 | tf_op jit(solution)/shard_map/all_gather | solution.py:291
  252.7 136.7 %all-gather.22.cloned.1.call-start = ((), (), s32[]{:S(2)}) async-start(), calls=%async_computation.17 | async-start | bytes 3760128 | tf_op jit(solution)/shard_map/all_gather | solution.py:239
  253.5 159.4 %all-gather.24.cloned.1.call-start = ((), (), s32[]{:S(2)}) async-start(), calls=%async_computation.19 | async-start | bytes 1769472 | tf_op jit(solution)/shard_map/all_gather | solution.py:310
  254.2 211.8 %reduce-scatter.19.cloned.1.call-start = ((), (), s32[]{:S(2)}) async-start(), calls=%async_computation.20 | async-start | bytes 3538944 | tf_op jit(solution)/shard_map/reduce_scatter | solution.py:323
  431.1 72.0 %reduce-scatter.17.cloned.1.call-start = ((), (), s32[]{:S(2)}) async-start(), calls=%async_computation.18 | async-start | bytes 3538944 | tf_op jit(solution)/shard_map/reduce_scatter | solution.py:297
  437.2 93.9 %all-gather.26.cloned.1.call-start = ((), (), s32[]{:S(2)}) async-start(), calls=%async_computation.21 | async-start | bytes 1769472 | tf_op jit(solution)/shard_map/all_gather | solution.py:334
  508.2 82.3 %reduce-scatter.21.cloned.1.call-start = ((), (), s32[]{:S(2)}) async-start(), calls=%async_computation.22 | async-start | bytes 3538944 | tf_op jit(solution)/shard_map/reduce_scatter | solution.py:348
  555.5 83.5 %reduce-scatter.31.cloned.1.call-start = ((), (), s32[]{:S(2)}) async-start(), calls=%async_computation.27 | async-start | bytes 884736
  608.0 83.4 %reduce-scatter.33.cloned.1.call-start = ((), (), s32[]{:S(2)}) async-start(), calls=%async_computation.28 | async-start | bytes 3133440
  611.9 172.3 %reduce-scatter.29.cloned.1.call-start = ((), (), s32[]{:S(2)}) async-start(), calls=%async_computation.26 | async-start | bytes 7520256 | tf_op jit(solution)/shard_map/reduce_scatter | solution.py:178
  619.6 273.7 %reduce-scatter.25.cloned.1.call-start = ((), (), s32[]{:S(2)}) async-start(), calls=%async_computation.24 | async-start | bytes 9400320 | tf_op jit(solution)/shard_map/reduce_scatter | solution.py:175
  628.3 414.3 %reduce-scatter.27.cloned.1.call-start = ((), (), s32[]{:S(2)}) async-start(), calls=%async_computation.25 | async-start | bytes 15040512 | tf_op jit(solution)/shard_map/reduce_scatter | solution.py:177
  638.7 591.1 %reduce-scatter.23.cloned.1.call-start = ((), (), s32[]{:S(2)}) async-start(), calls=%async_computation.23 | async-start | bytes 18800640 | tf_op jit(solution)/shard_map/reduce_scatter | solution.py:174
  788.5 446.7 %copy-start.11 = (f32[256,1152]{1,0:T(8,128)S(1)}, f32[256,1152]{1,0:T(8,128)}, u32[]{:S(2)}) copy-start(f32[256,1152]{1,0:T(8,128)} %get-tuple-element.202) | copy-start | bytes 3538948
  (91 other events, 268.4 us)
Sparse Core Ops, SparseCore 0:
  10.8 79.8 all-gather.9
  93.5 50.2 all-gather.13
  145.9 21.2 all-gather.11
  169.7 39.1 all-gather.15
  213.2 33.6 reduce-scatter.14
  249.6 66.0 all-gather.19
  317.8 21.5 all-gather.17
  342.2 47.1 all-gather.21
  391.5 21.3 all-gather.23
  431.2 34.7 reduce-scatter.18
  468.3 34.7 reduce-scatter.16
  508.3 22.7 all-gather.25
  555.6 34.7 reduce-scatter.20
  608.1 15.3 reduce-scatter.30
  627.3 64.0 reduce-scatter.32
  695.2 88.8 reduce-scatter.28
  788.1 105.2 reduce-scatter.24
  897.4 145.1 reduce-scatter.26
  1046.8 182.9 reduce-scatter.22
where the time goes:
time: 1310 us
  waiting for transfers between devices  1010 us (77%)
  matrix products  111 us (8%)
  other arithmetic  57.3 us (4%)
  blocking collectives  55.9 us (4%)
  local copies, waits for them, and re-layouts  44 us (3%)
  between operations  21.9 us (2%)
    reduce_scatter x1, waiting for transfers between devices, reduce_grads(): lax.psum_scatter(values[0], 'dp', scatter_dimension=0, tiled=True)  185 us
    reduce_scatter x1, waiting for transfers between devices, reduce_grads(): lax.psum_scatter(values[3], 'dp', scatter_dimension=0, tiled=True)  147 us
    reduce_scatter x1, waiting for transfers between devices, reduce_grads(): lax.psum_scatter(values[1], 'dp', scatter_dimension=0, tiled=True)  105 us
    reduce_scatter x1, waiting for transfers between devices, reduce_grads(): lax.psum_scatter(values[4], 'dp', scatter_dimension=0, tiled=True)  89.6 us
    all_gather x1, waiting for transfers between devices, local(): lax.all_gather(ada_weight.astype(jnp.bfloat16), 'dp', axis=0, tiled=True)  78.5 us
    all_gather x1, waiting for transfers between devices, local(): lax.all_gather(gateup_weight.astype(jnp.bfloat16), 'dp', axis=0, tiled=True)  61 us
    unnamed x202, local copies, waits for them, and re-layouts  42 us
    psum x1, blocking collectives, local(): lax.psum((local_squares, g_gain, bias_slots), ('dp', 'tensor'))  39.8 us
  transfers between devices with their start and end apart: 19, of which 18 were waited for; matrix products, arithmetic and copies ran while one was open for 8% of the time, Pallas kernels for 0%

commit v1 on v0

v1 whole, which is shorter than its diff:
```python
from functools import partial
import math

import jax
import jax.numpy as jnp
from jax import lax
from jax.experimental import pallas as pl
from jax.experimental.pallas import tpu as pltpu
from jax.sharding import PartitionSpec as P

D = 1152
HD = 72
FF = 3072
STEP = 10


EPSILON = 1e-06
NEG_FILL = -1e30
PRECISE = lax.Precision.HIGHEST
BETA_FIRST = 0.9
BETA_SECOND = 0.95
ADAM_EPSILON = 1e-08
DECAY_RATE = 0.01
SMALL_RATE = 0.5


def rms_scaled(values):
    return values * lax.rsqrt(jnp.mean(values * values, axis=-1, keepdims=True) + EPSILON)


def modulate_in(base_rows, scale_rows, shift_rows):
    return rms_scaled(base_rows) * (1.0 + scale_rows) + shift_rows


def time_embed(step_ids, width):
    half_width = width // 2
    frequency = jnp.exp(-math.log(10000.0) * jnp.arange(half_width, dtype=jnp.float32) / half_width)
    angles = step_ids.astype(jnp.float32)[..., None] * frequency
    return jnp.concatenate([jnp.cos(angles), jnp.sin(angles)], axis=-1)


def layout(item_lengths, item_widths, row_index):
    ends_at = jnp.cumsum(item_lengths)
    starts_at = ends_at - item_lengths
    segment = jnp.sum((row_index[:, None] >= ends_at[None, :]).astype(jnp.int32), axis=1)
    member = segment[:, None] == jnp.arange(item_lengths.shape[0], dtype=jnp.int32)[None, :]
    offset = jnp.sum(jnp.where(member, starts_at[None, :], 0), axis=1)
    grid_span = jnp.sum(jnp.where(member, item_widths[None, :], 0), axis=1)
    inside = row_index - offset
    return (segment, inside // grid_span, inside % grid_span)


def rope_tables(grid_row, grid_col, head_size):
    quarter = head_size // 4
    frequency = jnp.exp(-math.log(10000.0) * jnp.arange(quarter, dtype=jnp.float32) / quarter)
    row_angle = grid_row.astype(jnp.float32)[:, None] * frequency[None, :]
    col_angle = grid_col.astype(jnp.float32)[:, None] * frequency[None, :]
    return (jnp.cos(row_angle), jnp.sin(row_angle), jnp.cos(col_angle), jnp.sin(col_angle))


def turn_half(part, cosine, sine):
    quarter = part.shape[-1] // 2
    first_part = part[..., :quarter]
    second_part = part[..., quarter:]
    cosine = cosine[:, None, :]
    sine = sine[:, None, :]
    return jnp.concatenate(
        [first_part * cosine - second_part * sine, first_part * sine + second_part * cosine],
        axis=-1,
    )


def rotate(values, tables):
    half_size = values.shape[-1] // 2
    return jnp.concatenate(
        [
            turn_half(values[..., :half_size], tables[0], tables[1]),
            turn_half(values[..., half_size:], tables[2], tables[3]),
        ],
        axis=-1,
    )


def qk_prepare(raw_query, raw_key, gains, tables):
    head_size = gains.shape[1]
    row_count = raw_query.shape[0]
    head_count = raw_query.shape[1] // head_size
    query_norm = rms_scaled(raw_query.reshape(row_count, head_count, head_size)) * gains[0]
    key_norm = rms_scaled(raw_key.reshape(row_count, head_count, head_size)) * gains[1]
    return (rotate(query_norm, tables), rotate(key_norm, tables))


def block_geometry(total_rows):
    query_block = min(512, total_rows)
    return (query_block, total_rows, total_rows // query_block)


def window_start(block_index, query_block, key_window, total_rows):
    return jnp.clip(block_index * query_block - query_block, 0, total_rows - key_window)


def masked_scores(query_low, key_low, segment, block_index, query_block, key_window):
    total_rows = query_low.shape[0]
    scale = query_low.shape[2] ** (-0.5)
    query_start = block_index * query_block
    key_start = window_start(block_index, query_block, key_window, total_rows)
    queries = lax.dynamic_slice_in_dim(query_low, query_start, query_block, 0)
    seg_query = lax.dynamic_slice_in_dim(segment, query_start, query_block, 0)
    scores = (
        jnp.einsum("qhe,khe->hqk", queries, key_low, preferred_element_type=jnp.float32) * scale
    )
    allowed = (seg_query[:, None] == segment[None, :])[None]
    return (jnp.where(allowed, scores, NEG_FILL), queries, key_low, query_start, key_start)


def attend(query_low, key_low, value_low, segment):
    total_rows = query_low.shape[0]
    query_block, key_window, block_count = block_geometry(total_rows)

    def one_block(block_index):
        scores, queries, keyset, query_start, key_start = masked_scores(
            query_low, key_low, segment, block_index, query_block, key_window
        )
        peak = jnp.max(scores, axis=-1, keepdims=True)
        expo = jnp.exp(scores - peak)
        total_exp = jnp.sum(expo, axis=-1, keepdims=True)
        probs = (expo / total_exp).astype(jnp.bfloat16)
        result = jnp.einsum("hqk,khe->qhe", probs, value_low, preferred_element_type=jnp.float32)
        return (result, (peak + jnp.log(total_exp))[..., 0])

    outputs, log_sums = lax.map(one_block, jnp.arange(block_count, dtype=jnp.int32))
    return (outputs.reshape(total_rows, query_low.shape[1], query_low.shape[2]), log_sums)


def attend_back(query_low, key_low, value_low, d_attn, log_sums, segment):
    total_rows = query_low.shape[0]
    query_block, key_window, block_count = block_geometry(total_rows)
    scale = query_low.shape[2] ** (-0.5)
    zeros_like = jnp.zeros(query_low.shape, jnp.float32)

    def one_block(carry, block_index):
        d_keys, d_values = carry
        scores, queries, keyset, query_start, key_start = masked_scores(
            query_low, key_low, segment, block_index, query_block, key_window
        )
        grads_block = lax.dynamic_slice_in_dim(d_attn, query_start, query_block, 0)
        probs = jnp.exp(scores - log_sums[block_index][:, :, None])
        low_probs = probs.astype(jnp.bfloat16)
        d_probs = jnp.einsum(
            "qhe,khe->hqk", grads_block, value_low, preferred_element_type=jnp.float32
        )
        row_dot = jnp.sum(probs * d_probs, axis=-1, keepdims=True)
        d_scores = (probs * (d_probs - row_dot)).astype(jnp.bfloat16)
        d_query = (
            jnp.einsum("hqk,khe->qhe", d_scores, keyset, preferred_element_type=jnp.float32) * scale
        )
        d_key_part = (
            jnp.einsum("hqk,qhe->khe", d_scores, queries, preferred_element_type=jnp.float32)
            * scale
        )
        d_value_part = jnp.einsum(
            "hqk,qhe->khe", low_probs, grads_block, preferred_element_type=jnp.float32
        )
        d_keys = d_keys + d_key_part
        d_values = d_values + d_value_part
        return ((d_keys, d_values), d_query)

    (d_keys, d_values), d_queries = lax.scan(
        one_block, (zeros_like, zeros_like), jnp.arange(block_count, dtype=jnp.int32)
    )
    return (d_queries.reshape(query_low.shape), d_keys, d_values)


def adam_update(weight, first_moment, second_moment, gradient, rate, clip):
    clipped = gradient * clip
    new_first = BETA_FIRST * first_moment + (1.0 - BETA_FIRST) * clipped
    new_second = BETA_SECOND * second_moment + (1.0 - BETA_SECOND) * clipped * clipped
    unbiased_first = new_first / (1.0 - BETA_FIRST**STEP)
    unbiased_second = new_second / (1.0 - BETA_SECOND**STEP)
    new_weight = weight - rate * (
        unbiased_first / (jnp.sqrt(unbiased_second) + ADAM_EPSILON) + DECAY_RATE * weight
    )
    return (new_weight, new_first, new_second)


ZSIDE = 4
CORES = 2


def place_of(rank, count):
    xside = count // (ZSIDE * CORES)
    return (rank // (xside * CORES), (rank // CORES) % xside, rank % CORES)


def shift_pairs(count, dim, amount):
    xside = count // (ZSIDE * CORES)
    pairs = []
    for rank in range(count):
        z, x, core = place_of(rank, count)
        if dim == "z":
            z = (z + amount) % ZSIDE
        elif dim == "x":
            x = (x + amount) % xside
        else:
            core = (core + amount) % CORES
        pairs.append((rank, (z * xside + x) * CORES + core))
    return pairs


def send(values, dim, amount):
    count = lax.axis_size("dp")
    return lax.ppermute(values, "dp", shift_pairs(count, dim, amount))


def tensor_send(values, amount):
    count = lax.axis_size("tensor")
    return lax.ppermute(values, "tensor", [(r, (r + amount) % count) for r in range(count)])


def block_order(rank, count):
    xside = count // (ZSIDE * CORES)
    z, x, core = place_of(rank, count)
    flips = jnp.arange(CORES, dtype=jnp.int32)[:, None, None]
    turns = jnp.arange(xside, dtype=jnp.int32)[None, :, None]
    hops = jnp.arange(ZSIDE, dtype=jnp.int32)[None, None, :]
    their_z = (z - hops) % ZSIDE
    their_x = (x - turns) % xside
    their_core = (core + flips) % CORES
    return ((their_z * xside + their_x) * CORES + their_core).reshape(count)


def gather_pieces(shard):
    xside = lax.axis_size("dp") // (ZSIDE * CORES)
    near = jnp.concatenate([shard] + [send(shard, "z", hop) for hop in range(1, ZSIDE)], axis=0)
    mine = [near] + [send(near, "x", turn) for turn in range(1, xside)]
    other = [send(piece, "core", 1) for piece in mine]
    return mine + other


def gather_rows(shard):
    xside = lax.axis_size("dp") // (ZSIDE * CORES)
    near = jnp.concatenate([shard] + [send(shard, "z", hop) for hop in range(1, ZSIDE)], axis=0)
    mine = jnp.concatenate([near] + [send(near, "x", turn) for turn in range(1, xside)], axis=0)
    return jnp.concatenate([mine, send(mine, "core", 1)], axis=0)


def reduce_rows(mine, other):
    xside = lax.axis_size("dp") // (ZSIDE * CORES)
    kind = mine.dtype
    came = send(other, "core", 1)
    rows = mine.shape[0] // xside
    parts = []
    for turn in range(xside):
        cut = slice(turn * rows, (turn + 1) * rows)
        parts.append(mine[cut].astype(jnp.float32) + came[cut].astype(jnp.float32))
    came_x = [send(parts[turn].astype(kind), "x", -turn) for turn in range(1, xside)]
    rows = rows // ZSIDE
    cuts = []
    for hop in range(ZSIDE):
        cut = slice(hop * rows, (hop + 1) * rows)
        cuts.append(sum([piece[cut].astype(jnp.float32) for piece in came_x], parts[0][cut]))
    total = cuts[0]
    for hop in range(1, ZSIDE):
        total = total + send(cuts[hop].astype(kind), "z", -hop).astype(jnp.float32)
    return total


def tensor_gather(values):
    count = lax.axis_size("tensor")
    return jnp.concatenate([values] + [tensor_send(values, hop) for hop in range(1, count)], axis=0)


def tensor_reduce(values):
    count = lax.axis_size("tensor")
    rows = values.shape[0] // count
    total = values[:rows].astype(jnp.float32)
    for hop in range(1, count):
        came = tensor_send(values[hop * rows : (hop + 1) * rows], -hop)
        total = total + came.astype(jnp.float32)
    return total


def tensor_total(values):
    count = lax.axis_size("tensor")
    if count == 2:
        half = values.shape[0] // 2
        came = tensor_send(values, 1)
        came = jnp.concatenate([came[half:], came[:half]], axis=0)
        return values.astype(jnp.float32) + came.astype(jnp.float32)
    return tensor_gather(tensor_reduce(values).astype(values.dtype)).astype(jnp.float32)


def everywhere_sum(values):
    for axis in ("dp", "tensor"):
        count = lax.axis_size(axis)
        step = 1
        while step < count:
            values = values + lax.ppermute(values, axis, [(r, r ^ step) for r in range(count)])
            step *= 2
    return values


def mlp_kernel(pieces, has_start, rows_ref, rows_t_ref, grad_ref, grad_t_ref, *refs):
    weights = refs[:pieces]
    refs = refs[pieces:]
    if has_start:
        start_out, start_in = refs[:2]
        refs = refs[2:]
    out_ref, in_ref, mine_ref, other_ref, held, out_acc, in_acc = refs
    step = pl.program_id(0)
    share = held.shape[0] // pieces
    for index in range(pieces):
        held[index * share : (index + 1) * share, :] = weights[index][...]
    width = held.shape[1] // 3
    gate_w = held[:, :width]
    up_w = held[:, width : 2 * width]
    down_w = held[:, 2 * width :]

    @pl.when(step == 0)
    def _():
        if has_start:
            out_acc[...] = start_out[...]
            in_acc[...] = start_in[...]
        else:
            out_acc[...] = jnp.zeros_like(out_acc)
            in_acc[...] = jnp.zeros_like(in_acc)

    across = (((1,), (1,)), ((), ()))
    gate = jnp.dot(rows_ref[...], gate_w, preferred_element_type=jnp.float32)
    up = jnp.dot(rows_ref[...], up_w, preferred_element_type=jnp.float32)
    d_hidden = jnp.dot(grad_ref[...], down_w, preferred_element_type=jnp.float32)
    sigmoid = 1.0 / (1.0 + jnp.exp(-gate))
    silu = gate * sigmoid
    hidden = (silu * up).astype(jnp.bfloat16)
    d_gate = (d_hidden * up * sigmoid * (1.0 + gate * (1.0 - sigmoid))).astype(jnp.bfloat16)
    d_up = (d_hidden * silu).astype(jnp.bfloat16)
    out_acc[...] += lax.dot_general(hidden, down_w, across, preferred_element_type=jnp.float32)
    in_acc[...] += lax.dot_general(
        d_gate, gate_w, across, preferred_element_type=jnp.float32
    ) + lax.dot_general(d_up, up_w, across, preferred_element_type=jnp.float32)
    half = mine_ref.shape[0]
    for target, begin in ((mine_ref, 0), (other_ref, half)):
        rows_t = rows_t_ref[begin : begin + half, :]
        grad_t = grad_t_ref[begin : begin + half, :]
        target[:, :width] = jnp.dot(rows_t, d_gate, preferred_element_type=jnp.float32).astype(
            target.dtype
        )
        target[:, width : 2 * width] = jnp.dot(
            rows_t, d_up, preferred_element_type=jnp.float32
        ).astype(target.dtype)
        target[:, 2 * width :] = jnp.dot(
            grad_t, hidden, preferred_element_type=jnp.float32
        ).astype(target.dtype)

    @pl.when(step == pl.num_programs(0) - 1)
    def _():
        out_ref[...] = out_acc[...].astype(out_ref.dtype)
        in_ref[...] = in_acc[...].astype(in_ref.dtype)


def mlp_part(rows, rows_t, grad, grad_t, pieces, start, blocks, last):
    count, width = rows.shape
    columns = pieces[0].shape[1]
    block = columns // blocks
    whole = pl.BlockSpec((count, width), lambda i: (0, 0))
    whole_t = pl.BlockSpec((width, count), lambda i: (0, 0))
    kind = jnp.bfloat16 if last else jnp.float32
    half = jax.ShapeDtypeStruct((width // 2, columns), jnp.bfloat16)
    starts = [] if start is None else list(start)
    flops = 18 * count * width * (columns // 3)
    return pl.pallas_call(
        partial(mlp_kernel, len(pieces), len(starts) > 0),
        grid=(blocks,),
        in_specs=[whole, whole_t, whole, whole_t]
        + [pl.BlockSpec((p.shape[0], block), lambda i: (0, i)) for p in pieces]
        + [whole] * len(starts),
        out_specs=[whole, whole]
        + [pl.BlockSpec((width // 2, block), lambda i: (0, i))] * 2,
        out_shape=[jax.ShapeDtypeStruct((count, width), kind)] * 2 + [half, half],
        scratch_shapes=[
            pltpu.VMEM((width, block), jnp.bfloat16),
            pltpu.VMEM((count, width), jnp.float32),
            pltpu.VMEM((count, width), jnp.float32),
        ],
        cost_estimate=pl.CostEstimate(
            flops=flops, bytes_accessed=8 * width * columns, transcendentals=count * columns // 3
        ),
        compiler_params=pltpu.CompilerParams(vmem_limit_bytes=60 * 1024 * 1024),
    )(rows, rows_t, grad, grad_t, *pieces, *starts)


def mlp_plain(rows, grad, pieces, start, blocks, last):
    weights = jnp.concatenate(pieces, axis=0)
    width = weights.shape[0]
    block = weights.shape[1] // (3 * blocks)
    split = weights.reshape(width, blocks, 3, block)
    gate_w, up_w, down_w = [split[:, :, slot].reshape(width, blocks * block) for slot in range(3)]
    gate = jnp.dot(rows, gate_w, preferred_element_type=jnp.float32)
    up = jnp.dot(rows, up_w, preferred_element_type=jnp.float32)
    d_hidden = jnp.dot(grad, down_w, preferred_element_type=jnp.float32)
    sigmoid = jax.nn.sigmoid(gate)
    hidden = (gate * sigmoid * up).astype(jnp.bfloat16)
    d_gate = (d_hidden * up * sigmoid * (1.0 + gate * (1.0 - sigmoid))).astype(jnp.bfloat16)
    d_up = (d_hidden * gate * sigmoid).astype(jnp.bfloat16)
    out_sum = jnp.dot(hidden, down_w.T, preferred_element_type=jnp.float32)
    in_sum = jnp.dot(d_gate, gate_w.T, preferred_element_type=jnp.float32) + jnp.dot(
        d_up, up_w.T, preferred_element_type=jnp.float32
    )
    if start is not None:
        out_sum = out_sum + start[0]
        in_sum = in_sum + start[1]
    kind = jnp.bfloat16 if last else jnp.float32
    grads = [
        jnp.einsum("gd,gf->df", left, right, preferred_element_type=jnp.float32)
        .astype(jnp.bfloat16)
        .reshape(width, blocks, block)
        for left, right in ((rows, d_gate), (rows, d_up), (grad, hidden))
    ]
    packed = jnp.stack(grads, axis=2).reshape(width, 3 * blocks * block)
    return (out_sum.astype(kind), in_sum.astype(kind), packed[: width // 2], packed[width // 2 :])


def pad_columns(values, columns):
    return jnp.pad(values, ((0, 0), (0, columns - values.shape[1])))


def padded(columns):
    return -(-columns // 128) * 128


def local(
    tokens,
    cotangent,
    lengths,
    grid_width,
    timestep,
    class_id,
    class_table,
    ada_weight,
    ada_m,
    ada_v,
    ada_bias,
    bias_m,
    bias_v,
    qkv_weight,
    qkv_m,
    qkv_v,
    out_weight,
    out_m,
    out_v,
    gateup_weight,
    gateup_m,
    gateup_v,
    down_weight,
    down_m,
    down_v,
    qk_gain,
    gain_m,
    gain_v,
):
    tensor_count = lax.axis_size("tensor")
    data_count = lax.axis_size("dp")
    tensor_rank = lax.axis_index("tensor")
    data_rank = lax.axis_index("dp")
    local_rows, model_width = tokens.shape
    group_rows = local_rows * tensor_count
    column_share = model_width // tensor_count
    row_share = ada_weight.shape[0]
    head_size = qk_gain.shape[1]
    item_count = lengths.shape[1]
    class_count = class_table.shape[0]
    hidden_share = down_weight.shape[1]
    bf16 = jnp.bfloat16

    qkv_columns = padded(3 * column_share)
    out_columns = padded(column_share)
    attn_shard = jnp.concatenate(
        [
            pad_columns(qkv_weight.astype(bf16).reshape(row_share, -1), qkv_columns),
            pad_columns(out_weight.astype(bf16), out_columns),
        ],
        axis=1,
    )
    blocks = max(1, hidden_share // 512)
    block = hidden_share // (2 * blocks)
    mlp_split = jnp.stack(
        [
            part.astype(bf16).reshape(row_share, 2, blocks, block)
            for part in (gateup_weight[:, 0], gateup_weight[:, 1], down_weight)
        ],
        axis=3,
    )
    mlp_shards = [mlp_split[:, half].reshape(row_share, 3 * blocks * block) for half in range(2)]

    order = block_order(data_rank, data_count)
    column_of = (order[:, None] * row_share + jnp.arange(row_share, dtype=jnp.int32)).reshape(-1)
    to_held = (jnp.arange(model_width, dtype=jnp.int32)[:, None] == column_of[None, :]).astype(bf16)

    def hold(values):
        return jnp.dot(values, to_held, preferred_element_type=jnp.float32).astype(bf16)

    def unhold(values):
        return lax.dot_general(
            values, to_held, (((1,), (1,)), ((), ())), preferred_element_type=jnp.float32
        ).astype(bf16)

    ids = gather_rows(jnp.stack([class_id[0], timestep[0]])[None])
    item_ids = ids[:, 0].reshape(-1)
    item_steps = ids[:, 1].reshape(-1)
    class_onehot = (
        item_ids[:, None] == jnp.arange(class_count, dtype=jnp.int32)[None, :]
    ).astype(bf16)
    condition = jnp.dot(class_onehot, class_table, preferred_element_type=jnp.float32) + time_embed(
        item_steps, model_width
    )
    silu_all = jax.nn.silu(condition).astype(bf16)
    silu_own = lax.dynamic_slice_in_dim(silu_all, data_rank * row_share, row_share, 1)
    mod_part = jnp.dot(
        silu_own,
        ada_weight.astype(bf16).reshape(row_share, 6 * column_share),
        preferred_element_type=jnp.float32,
    )
    half_items = data_count * item_count // 2
    mod_share = reduce_rows(mod_part[:half_items], mod_part[half_items:])
    bias_share = lax.dynamic_slice_in_dim(ada_bias, tensor_rank * column_share, column_share, 1)
    mod_share = mod_share.reshape(item_count, 6, column_share) + bias_share[None]
    if tensor_count == 2:
        mod_other = tensor_send(mod_share, 1)
        lower = jnp.where(tensor_rank == 0, mod_share, mod_other)
        upper = jnp.where(tensor_rank == 0, mod_other, mod_share)
        modulation = jnp.concatenate([lower, upper], axis=2)
    else:
        modulation = lax.all_gather(mod_share, "tensor", axis=2, tiled=True)
    modulation = jnp.dot(
        modulation.reshape(item_count * 6, model_width),
        to_held.astype(jnp.float32),
        precision=PRECISE,
        preferred_element_type=jnp.float32,
    ).reshape(item_count, 6, model_width)

    tokens_all = hold(tensor_gather(tokens))
    cot_all = hold(tensor_gather(cotangent))
    base_rows = tokens_all.astype(jnp.float32)
    cot_rows = cot_all.astype(jnp.float32)
    row_blocks = (tensor_rank - jnp.arange(tensor_count, dtype=jnp.int32)) % tensor_count
    row_index = (
        row_blocks[:, None] * local_rows + jnp.arange(local_rows, dtype=jnp.int32)[None, :]
    ).reshape(-1)
    segment, grid_row, grid_col = layout(lengths[0], grid_width[0], row_index)
    tables = rope_tables(grid_row, grid_col, head_size)

    def mod_rows(slot, count):
        picked = modulation[0, slot][None, :]
        for item in range(1, item_count):
            picked = jnp.where(
                segment[:count, None] == item, modulation[item, slot][None, :], picked
            )
        return picked

    def mod_sums(values):
        own = segment[:local_rows]
        return jnp.stack(
            [
                jnp.sum(jnp.where(own[:, None] == item, values, 0.0), axis=0)
                for item in range(item_count)
            ]
        )

    attn_pieces = gather_pieces(attn_shard)
    mlp_pieces = [gather_pieces(shard) for shard in mlp_shards]
    attn_full = jnp.concatenate(attn_pieces, axis=0)
    full_qkv = attn_full[:, : 3 * column_share]
    full_out = attn_full[:, qkv_columns : qkv_columns + column_share]

    attn_in = modulate_in(base_rows, mod_rows(1, group_rows), mod_rows(0, group_rows)).astype(bf16)
    qkv_raw = jnp.dot(attn_in, full_qkv, preferred_element_type=jnp.float32)
    raw_query, raw_key, raw_value = [
        qkv_raw[:, slot * column_share : (slot + 1) * column_share] for slot in range(3)
    ]
    query_rot, key_rot = qk_prepare(raw_query, raw_key, qk_gain, tables)
    query_low = query_rot.astype(bf16)
    key_low = key_rot.astype(bf16)
    value_low = raw_value.reshape(group_rows, -1, head_size).astype(bf16)
    attn_vals, log_sums = attend(query_low, key_low, value_low, segment)
    attn_low = attn_vals.reshape(group_rows, column_share).astype(bf16)
    branch = tensor_total(
        jnp.einsum("gc,dc->gd", attn_low, full_out, preferred_element_type=jnp.float32).astype(bf16)
    )
    mid_rows = base_rows + mod_rows(2, group_rows) * branch
    scale_two = mod_rows(4, group_rows)
    mlp_in = modulate_in(mid_rows, scale_two, mod_rows(3, group_rows)).astype(bf16)
    gate_two = mod_rows(5, group_rows)
    d_branch_mlp = (gate_two * cot_rows).astype(bf16)

    if group_rows <= 512:
        mlp_in_t = mlp_in.T
        d_branch_t = d_branch_mlp.T
        first = mlp_part(
            mlp_in, mlp_in_t, d_branch_mlp, d_branch_t, mlp_pieces[0], None, blocks, False
        )
        second = mlp_part(
            mlp_in, mlp_in_t, d_branch_mlp, d_branch_t, mlp_pieces[1], first[:2], blocks, True
        )
    else:
        first = mlp_plain(mlp_in, d_branch_mlp, mlp_pieces[0], None, blocks, False)
        second = mlp_plain(mlp_in, d_branch_mlp, mlp_pieces[1], first[:2], blocks, True)
    d_mlp_in = tensor_total(second[1])
    branch_mlp = tensor_reduce(second[0])
    out_rows = mid_rows[:local_rows] + gate_two[:local_rows] * branch_mlp
    out_tokens = unhold(out_rows.astype(bf16))
    sum_mlp = [reduce_rows(part[2], part[3]) for part in (first, second)]

    d_mid_norm, d_scale_two, d_shift_two = jax.vjp(
        modulate_in, mid_rows, scale_two, jnp.zeros_like(mid_rows)
    )[1](d_mlp_in)
    d_mid = cot_rows + d_mid_norm
    d_branch_attn = (mod_rows(2, group_rows) * d_mid).astype(bf16)
    half_width = model_width // 2
    g_out = [
        jnp.einsum("gd,gc->dc", part, attn_low, preferred_element_type=jnp.float32).astype(bf16)
        for part in (d_branch_attn[:, :half_width], d_branch_attn[:, half_width:])
    ]
    sum_out = reduce_rows(g_out[0], g_out[1])
    d_attn = jnp.einsum("gd,dc->gc", d_branch_attn, full_out, preferred_element_type=jnp.float32)
    d_attn = d_attn.astype(bf16).reshape(query_low.shape)
    d_query_rot, d_key_rot, d_values = attend_back(
        query_low, key_low, value_low, d_attn, log_sums, segment
    )
    _, pull_qk = jax.vjp(partial(qk_prepare, tables=tables), raw_query, raw_key, qk_gain)
    d_query_raw, d_key_raw, g_gain = pull_qk((d_query_rot, d_key_rot))
    d_qkv_low = jnp.concatenate(
        [d_query_raw, d_key_raw, d_values.reshape(group_rows, column_share)], axis=1
    ).astype(bf16)
    d_attn_part = jnp.einsum("gc,dc->gd", d_qkv_low, full_qkv, preferred_element_type=jnp.float32)
    d_attn_in = tensor_reduce(d_attn_part.astype(bf16))
    g_qkv = [
        jnp.einsum("gd,gc->dc", part, d_qkv_low, preferred_element_type=jnp.float32).astype(bf16)
        for part in (attn_in[:, :half_width], attn_in[:, half_width:])
    ]
    sum_qkv = reduce_rows(g_qkv[0], g_qkv[1])

    own_scale = mod_rows(1, local_rows)
    d_base_norm, d_scale_one, d_shift_one = jax.vjp(
        modulate_in, base_rows[:local_rows], own_scale, jnp.zeros_like(own_scale)
    )[1](d_attn_in)
    input_grad = unhold((d_mid[:local_rows] + d_base_norm).astype(bf16))
    d_mod_part = jnp.stack(
        [
            mod_sums(d_shift_one),
            mod_sums(d_scale_one),
            mod_sums(d_mid[:local_rows] * branch[:local_rows]),
            mod_sums(d_shift_two[:local_rows]),
            mod_sums(d_scale_two[:local_rows]),
            mod_sums(cot_rows[:local_rows] * branch_mlp),
        ],
        axis=1,
    )
    d_mod_part = lax.dot_general(
        d_mod_part.reshape(item_count * 6, model_width),
        to_held.astype(jnp.float32),
        (((1,), (1,)), ((), ())),
        precision=PRECISE,
        preferred_element_type=jnp.float32,
    ).reshape(item_count, 6, model_width)
    if tensor_count == 2:
        lower, upper = d_mod_part[:, :, :column_share], d_mod_part[:, :, column_share:]
        theirs = jnp.where(tensor_rank == 0, upper, lower)
        d_mod = jnp.where(tensor_rank == 0, lower, upper) + tensor_send(theirs, 1)
    else:
        d_mod = lax.psum_scatter(d_mod_part, "tensor", scatter_dimension=2, tiled=True)
    d_mod_all = gather_rows(d_mod.reshape(item_count, 6 * column_share))
    sum_ada = lax.dot_general(
        silu_own.astype(jnp.float32),
        d_mod_all,
        (((0,), (0,)), ((), ())),
        precision=PRECISE,
        preferred_element_type=jnp.float32,
    )
    bias_share = jnp.sum(d_mod_all, axis=0).reshape(6, column_share)
    if tensor_count == 2:
        bias_other = tensor_send(bias_share, 1)
        lower = jnp.where(tensor_rank == 0, bias_share, bias_other)
        upper = jnp.where(tensor_rank == 0, bias_other, bias_share)
        bias_grad = jnp.concatenate([lower, upper], axis=1)
    else:
        bias_grad = lax.all_gather(bias_share, "tensor", axis=1, tiled=True)

    local_squares = jnp.sum(sum_ada * sum_ada) + jnp.sum(sum_qkv * sum_qkv)
    local_squares = local_squares + jnp.sum(sum_out * sum_out)
    for part in sum_mlp:
        local_squares = local_squares + jnp.sum(part * part)
    packet = jnp.concatenate(
        [
            g_gain.reshape(-1),
            local_squares[None],
            jnp.zeros((256 - 2 * head_size - 1,), jnp.float32),
        ]
    ).reshape(2, 128)
    packet = everywhere_sum(packet).reshape(-1)
    gain_total = packet[: 2 * head_size].reshape(2, head_size)
    grad_norm = jnp.sqrt(
        packet[2 * head_size] + jnp.sum(gain_total * gain_total) + jnp.sum(bias_grad * bias_grad)
    )
    tokens_all_count = local_rows * tensor_count * data_count
    params_all = 10 * D * D + 3 * D * FF + 6 * D + 2 * HD
    limit = 0.01 * math.sqrt(tokens_all_count * params_all)
    clip = limit / jnp.maximum(grad_norm, limit)
    matrix_rate = model_width ** (-0.5)

    g_ada = sum_ada.reshape(ada_weight.shape)
    g_qkv_sum = sum_qkv.reshape(qkv_weight.shape)
    mlp_sum = jnp.stack(
        [part.reshape(row_share, blocks, 3, block) for part in sum_mlp], axis=1
    )
    g_gateup = jnp.stack(
        [mlp_sum[:, :, :, slot].reshape(row_share, hidden_share) for slot in range(2)], axis=1
    )
    g_down = mlp_sum[:, :, :, 2].reshape(row_share, hidden_share)

    new_ada = adam_update(ada_weight, ada_m, ada_v, g_ada, matrix_rate, clip)
    new_bias = adam_update(ada_bias, bias_m, bias_v, bias_grad, SMALL_RATE, clip)
    new_qkv = adam_update(qkv_weight, qkv_m, qkv_v, g_qkv_sum, matrix_rate, clip)
    new_out = adam_update(out_weight, out_m, out_v, sum_out, (model_width // 64) ** (-0.5), clip)
    new_gateup = adam_update(gateup_weight, gateup_m, gateup_v, g_gateup, matrix_rate, clip)
    new_down = adam_update(down_weight, down_m, down_v, g_down, FF ** (-0.5), clip)
    new_gain = adam_update(qk_gain, gain_m, gain_v, gain_total, SMALL_RATE, clip)
    return (
        out_tokens,
        input_grad,
        grad_norm,
        new_ada[0],
        new_ada[1],
        new_ada[2],
        new_bias[0],
        new_bias[1],
        new_bias[2],
        new_qkv[0],
        new_qkv[1],
        new_qkv[2],
        new_out[0],
        new_out[1],
        new_out[2],
        new_gateup[0],
        new_gateup[1],
        new_gateup[2],
        new_down[0],
        new_down[1],
        new_down[2],
        new_gain[0],
        new_gain[1],
        new_gain[2],
    )


def solution(mesh):
    in_specs = (
        P(("dp", "tensor"), None),
        P(("dp", "tensor"), None),
        P("dp", None),
        P("dp", None),
        P("dp", None),
        P("dp", None),
        P(),
        P("dp", None, "tensor"),
        P("dp", None, "tensor"),
        P("dp", None, "tensor"),
        P(),
        P(),
        P(),
        P("dp", None, "tensor"),
        P("dp", None, "tensor"),
        P("dp", None, "tensor"),
        P("dp", "tensor"),
        P("dp", "tensor"),
        P("dp", "tensor"),
        P("dp", None, "tensor"),
        P("dp", None, "tensor"),
        P("dp", None, "tensor"),
        P("dp", "tensor"),
        P("dp", "tensor"),
        P("dp", "tensor"),
        P(),
        P(),
        P(),
    )
    out_specs = (
        P(("dp", "tensor"), None),
        P(("dp", "tensor"), None),
        P(),
        P("dp", None, "tensor"),
        P("dp", None, "tensor"),
        P("dp", None, "tensor"),
        P(),
        P(),
        P(),
        P("dp", None, "tensor"),
        P("dp", None, "tensor"),
        P("dp", None, "tensor"),
        P("dp", "tensor"),
        P("dp", "tensor"),
        P("dp", "tensor"),
        P("dp", None, "tensor"),
        P("dp", None, "tensor"),
        P("dp", None, "tensor"),
        P("dp", "tensor"),
        P("dp", "tensor"),
        P("dp", "tensor"),
        P(),
        P(),
        P(),
    )
    return jax.shard_map(local, mesh=mesh, in_specs=in_specs, out_specs=out_specs, check_vma=False)
```

time: 1310 us -> 636 us (0.49)
  waiting for transfers between devices: 1010 us -> 290 us
  starting transfers between devices: 2.04 us -> 77.1 us
  matrix products: 111 us -> 51.2 us
  blocking collectives: 55.9 us -> 0 us
  local copies, waits for them, and re-layouts: 44 us -> 89.7 us
  Pallas kernels: 0 us -> 33.4 us
  other arithmetic: 57.3 us -> 74.8 us
    reduce_scatter x8 -> x0, waiting for transfers between devices: 657 us -> none  [the longest x1 185 us: reduce_grads(): lax.psum_scatter(values[0], 'dp', scatter_dimension=0, tiled=True)]
    all_gather x9 -> x0, waiting for transfers between devices: 318 us -> none  [the longest x1 78.5 us: local(): lax.all_gather(ada_weight.astype(jnp.bfloat16), 'dp', axis=0, tiled=True)]
    ppermute x0 -> x67, waiting for transfers between devices: none -> 290 us  [the longest x53 203 us: send(): return lax.ppermute(values, 'dp', shift_pairs(count, dim, amount))]
    ppermute x0 -> x67, starting transfers between devices: none -> 77.1 us  [the longest x53 65.9 us: send(): return lax.ppermute(values, 'dp', shift_pairs(count, dim, amount))]
    dot_general x16, matrix products: 98.3 us -> 40.6 us  [the longest x2 8.6 us: hold(): jnp.dot(values, to_held, preferred_element_type=jnp.float32).astype(bf16)]
    psum x1 -> x0, blocking collectives: 39.8 us -> none  [local(): lax.psum((local_squares, g_gain, bias_slots), ('dp', 'tensor'))]
    unnamed x21 -> x0, waiting for transfers between devices: 38.4 us -> none
    pallas_call x0 -> x2, Pallas kernels: none -> 33.4 us  [mlp_part(): pl.pallas_call(partial(mlp_kernel, len(pieces), len(starts) > 0), grid=(b...]
  transfers between devices with their start and end apart: 19 -> 67, of which waited for: 18 -> 33; matrix products, arithmetic and copies ran while one was open for 8% -> 27% of each run, Pallas kernels for 0% -> 3%
where the time goes in v1:
time: 636 us; the launch traced here: 626 us
  waiting for transfers between devices  290 us (46%)
  local copies, waits for them, and re-layouts  89.7 us (14%)
  starting transfers between devices  77.1 us (12%)
  other arithmetic  74.8 us (12%)
  matrix products  51.2 us (8%)
  Pallas kernels  33.4 us (5%)
  between operations  9.71 us (2%)
    ppermute x53, waiting for transfers between devices, send(): return lax.ppermute(values, 'dp', shift_pairs(count, dim, amount))  203 us
    ppermute x9, waiting for transfers between devices, tensor_send(): lax.ppermute(values, 'tensor', [(r, (r + amount) % count) for r in range(...  84.7 us
    ppermute x53, starting transfers between devices, send(): return lax.ppermute(values, 'dp', shift_pairs(count, dim, amount))  65.9 us
    unnamed x333, local copies, waits for them, and re-layouts  34.4 us
    pallas_call x2, Pallas kernels, mlp_part(): pl.pallas_call(partial(mlp_kernel, len(pieces), len(starts) > 0), grid=(b...  33.4 us
  transfers between devices with their start and end apart: 67, of which 33 were waited for; matrix products, arithmetic and copies ran while one was open for 27% of the time, Pallas kernels for 3%

profile of v1, /device:TPU:0, one launch (start us, length us, event | category | flops | bytes accessed | tf_op | source)
XLA Modules:
  0.0 626.0 jit_solution(425372961687546727)
XLA Ops:
  1.5 5.1 collective-permute-start.3
  41.0 3.8 collective-permute-start.22
  54.1 11.8 %collective-permute-done.20 = bf16[72,2304]{1,0:T(8,128)(2,1)S(1)} collective-permute-done((bf16[72,2304]{1,0:T(8,128)(2,1)S(1)}, bf16[72,2304]{1,0:T(8,128)(2,1)S(1)}, u32[]{:S(2)}, u32[]{:S(2)}) %collective-permute-start.20) | collective-permute-done | bytes 331808 | tf_op jit(solution)/shard_map/ppermute | solution.py:212
  66.7 14.7 %collective-permute-done.21 = bf16[72,2304]{1,0:T(8,128)(2,1)S(1)} collective-permute-done((bf16[72,2304]{1,0:T(8,128)(2,1)S(1)}, bf16[72,2304]{1,0:T(8,128)(2,1)S(1)}, u32[]{:S(2)}, u32[]{:S(2)}) %collective-permute-start.21) | collective-permute-done | bytes 331808 | tf_op jit(solution)/shard_map/ppermute | solution.py:212
  100.2 9.6 %collective-permute-start.8 = (f32[2,3456]{1,0:T(2,128)S(1)}, f32[2,3456]{1,0:T(2,128)S(1)}, u32[]{:S(2)}, u32[]{:S(2)}) collective-permute-start(f32[2,3456]{1,0:T(2,128)S(1)} %get-tuple-element.320), channel_id=1, source_target_pairs={{0,24},{2,26},{4,28},{6,30},{8,0},{10,2},{12,4},{14,6},{16,8},{18,... | collective-permute-start | bytes 82952 | tf_op jit(solution)/shard_map/ppermute | solution.py:212
  110.6 4.4 collective-permute-start.10
  115.0 3.9 collective-permute-start.9
  132.1 53.5 %collective-permute-done.15 = bf16[288,2432]{1,0:T(8,128)(2,1)S(1)} collective-permute-done((bf16[288,2432]{1,0:T(8,128)(2,1)S(1)}, bf16[288,2432]{1,0:T(8,128)(2,1)S(1)}, u32[]{:S(2)}, u32[]{:S(2)}) %collective-permute-start.15) | collective-permute-done | bytes 1400864 | tf_op jit(solution)/shard_map/ppermute | solution.py:212
  206.6 26.2 %collective-permute-done.18 = bf16[512,1152]{0,1:T(8,128)(2,1)S(1)} collective-permute-done((bf16[512,1152]{0,1:T(8,128)(2,1)S(1)}, bf16[512,1152]{0,1:T(8,128)(2,1)S(1)}, u32[]{:S(2)}, u32[]{:S(2)}) %collective-permute-start.18) | collective-permute-done | bytes 1179680 | tf_op jit(solution)/shard_map/ppermute | solution.py:217
  232.9 11.7 %collective-permute-done.19 = bf16[256,1152]{1,0:T(8,128)(2,1)S(1)} collective-permute-done((bf16[256,1152]{1,0:T(8,128)(2,1)S(1)}, bf16[256,1152]{1,0:T(8,128)(2,1)S(1)}, u32[]{:S(2)}, u32[]{:S(2)}) %collective-permute-start.19) | collective-permute-done | bytes 589856 | tf_op jit(solution)/shard_map/ppermute | solution.py:217
  244.7 5.2 multiply_reduce_fusion.2
  261.9 16.4 %shard_map.451 = (f32[512,1152]{1,0:T(8,128)}, f32[512,1152]{1,0:T(8,128)}, bf16[576,2304]{1,0:T(8,128)(2,1)}, bf16[576,2304]{1,0:T(8,128)(2,1)}) custom-call(bf16[512,1152]{1,0:T(8,128)(2,1)} %copy.258.rows_ref, bf16[1152,512]{1,0:T(8,128)(2,1)} %bitcast.94, bf16[512,1152]{1,0:T(8,128)(2,1)} %copy.259.grad_ref, bf16[1152,512]{1,0:T(8,128)(2,1)} %fusion.37.grad_t_ref, ...), custom_call_target="tpu_custom_call" | custom-call | flops 8153726976 | bytes 21233664 | tf_op jit(solution)/shard_map/pallas_call | solution.py:371
  278.2 17.0 %shard_map.452 = (bf16[512,1152]{1,0:T(8,128)(2,1)}, bf16[512,1152]{1,0:T(8,128)(2,1)}, bf16[576,2304]{1,0:T(8,128)(2,1)}, bf16[576,2304]{1,0:T(8,128)(2,1)}) custom-call(bf16[512,1152]{1,0:T(8,128)(2,1)} %copy.258.rows_ref, bf16[1152,512]{1,0:T(8,128)(2,1)} %bitcast.95, bf16[512,1152]{1,0:T(8,128)(2,1)} %copy.259.grad_ref, ...), custom_call_target="tpu_custom_call" | custom-call | flops 8153726976 | bytes 21233664 | tf_op jit(solution)/shard_map/pallas_call | solution.py:371
  307.5 30.1 %collective-permute-done.32 = bf16[256,1152]{0,1:T(8,128)(2,1)S(1)} collective-permute-done((bf16[256,1152]{0,1:T(8,128)(2,1)S(1)}, bf16[256,1152]{0,1:T(8,128)(2,1)S(1)}, u32[]{:S(2)}, u32[]{:S(2)}) %collective-permute-start.32) | collective-permute-done | bytes 589856 | tf_op jit(solution)/shard_map/ppermute | solution.py:217
  337.6 3.9 fusion.32
  344.7 6.2 fusion.35
  381.4 11.0 %collective-permute-done.34 = bf16[256,1152]{0,1:T(8,128)(2,1)S(1)} collective-permute-done((bf16[256,1152]{0,1:T(8,128)(2,1)S(1)}, bf16[256,1152]{0,1:T(8,128)(2,1)S(1)}, u32[]{:S(2)}, u32[]{:S(2)}) %collective-permute-start.34) | collective-permute-done | bytes 589856 | tf_op jit(solution)/shard_map/ppermute | solution.py:217
  417.9 4.2 fusion.33
  449.8 25.0 %collective-permute-done.57 = bf16[288,2304]{1,0:T(8,128)(2,1)S(1)} collective-permute-done((bf16[288,2304]{1,0:T(8,128)(2,1)S(1)}, bf16[288,2304]{1,0:T(8,128)(2,1)S(1)}, u32[]{:S(2)}, u32[]{:S(2)}) %collective-permute-start.57) | collective-permute-done | bytes 1327136 | tf_op jit(solution)/shard_map/ppermute | solution.py:212
  477.8 25.4 %collective-permute-done.52 = bf16[288,2304]{1,0:T(8,128)(2,1)S(1)} collective-permute-done((bf16[288,2304]{1,0:T(8,128)(2,1)S(1)}, bf16[288,2304]{1,0:T(8,128)(2,1)S(1)}, u32[]{:S(2)}, u32[]{:S(2)}) %collective-permute-start.52) | collective-permute-done | bytes 1327136 | tf_op jit(solution)/shard_map/ppermute | solution.py:212
  505.6 18.8 %collective-permute-done.42 = bf16[288,1728]{1,0:T(8,128)(2,1)S(1)} collective-permute-done((bf16[288,1728]{1,0:T(8,128)(2,1)S(1)}, bf16[288,1728]{1,0:T(8,128)(2,1)S(1)}, u32[]{:S(2)}, u32[]{:S(2)}) %collective-permute-start.42) | collective-permute-done | bytes 995360 | tf_op jit(solution)/shard_map/ppermute | solution.py:212
  532.3 4.7 collective-permute-done.55
  537.0 23.5 %collective-permute-done.54 = bf16[72,2304]{1,0:T(8,128)(2,1)S(1)} collective-permute-done((bf16[72,2304]{1,0:T(8,128)(2,1)S(1)}, bf16[72,2304]{1,0:T(8,128)(2,1)S(1)}, u32[]{:S(2)}, u32[]{:S(2)}) %collective-permute-start.54) | collective-permute-done | bytes 331808 | tf_op jit(solution)/shard_map/ppermute | solution.py:212
  562.2 8.5 %collective-permute-done.44 = bf16[72,1728]{1,0:T(8,128)(2,1)S(1)} collective-permute-done((bf16[72,1728]{1,0:T(8,128)(2,1)S(1)}, bf16[72,1728]{1,0:T(8,128)(2,1)S(1)}, u32[]{:S(2)}, u32[]{:S(2)}) %collective-permute-start.44) | collective-permute-done | bytes 248864 | tf_op jit(solution)/shard_map/ppermute | solution.py:212
  (677 shorter events, 271.6 us)
Async XLA Ops:
  1.5 39.5 %collective-permute-start.3 = (s32[1,2,2]{2,1,0:T(2,128)S(1)}, s32[1,2,2]{2,1,0:T(2,128)S(1)}, u32[]{:S(2)}, u32[]{:S(2)}) collective-permute-start(s32[1,2,2]{2,1,0:T(2,128)S(1)} %add_bitcast_fusion.1), channel_id=1, source_target_pairs={{0,24},{2,26},{4,28},{6,30},{8,0},{10,2},{12,4},{14,6},{16,8},{18,... | collective-permute-start | bytes 56 | tf_op jit(solution)/shard_map/ppermute | solution.py:212
  6.6 38.2 %collective-permute-start.1 = (s32[1,2,2]{2,1,0:T(2,128)S(1)}, s32[1,2,2]{2,1,0:T(2,128)}, u32[]{:S(2)}, u32[]{:S(2)}) collective-permute-start(s32[1,2,2]{2,1,0:T(2,128)S(1)} %add_bitcast_fusion.1), channel_id=1, source_target_pairs={{0,8},{2,10},{4,12},{6,14},{8,16},{10,18},{12,20},{14,22},{16,24},... | collective-permute-start | bytes 56 | tf_op jit(solution)/shard_map/ppermute | solution.py:212
  15.9 76.8 %collective-permute-start.28 = (bf16[72,2304]{1,0:T(8,128)(2,1)}, bf16[72,2304]{1,0:T(8,128)(2,1)}, u32[]{:S(2)}, u32[]{:S(2)}) collective-permute-start(bf16[72,2304]{1,0:T(8,128)(2,1)} %reshape_squeeze.9), channel_id=1, source_target_pairs={{0,24},{2,26},{4,28},{6,30},{8,0},{10,2},{12,4},{14,6},{16,8},{18,... | collective-permute-start | bytes 995336 | tf_op jit(solution)/shard_map/ppermute | solution.py:212
  18.7 70.7 %collective-permute-start.27 = (bf16[72,2304]{1,0:T(8,128)(2,1)}, bf16[72,2304]{1,0:T(8,128)(2,1)}, u32[]{:S(2)}, u32[]{:S(2)}) collective-permute-start(bf16[72,2304]{1,0:T(8,128)(2,1)} %reshape_squeeze.9), channel_id=1, source_target_pairs={{0,16},{2,18},{4,20},{6,22},{8,24},{10,26},{12,28},{14,30},{16,0},... | collective-permute-start | bytes 995336 | tf_op jit(solution)/shard_map/ppermute | solution.py:212
  41.0 45.6 %collective-permute-start.26 = (bf16[72,2304]{1,0:T(8,128)(2,1)}, bf16[72,2304]{1,0:T(8,128)(2,1)}, u32[]{:S(2)}, u32[]{:S(2)}) collective-permute-start(bf16[72,2304]{1,0:T(8,128)(2,1)} %reshape_squeeze.9), channel_id=1, source_target_pairs={{0,8},{2,10},{4,12},{6,14},{8,16},{10,18},{12,20},{14,22},{16,24},... | collective-permute-start | bytes 995336 | tf_op jit(solution)/shard_map/ppermute | solution.py:212
  41.0 41.2 %collective-permute-start.22 = (bf16[72,2304]{1,0:T(8,128)(2,1)}, bf16[72,2304]{1,0:T(8,128)(2,1)}, u32[]{:S(2)}, u32[]{:S(2)}) collective-permute-start(bf16[72,2304]{1,0:T(8,128)(2,1)} %reshape_squeeze.8), channel_id=1, source_target_pairs={{0,24},{2,26},{4,28},{6,30},{8,0},{10,2},{12,4},{14,6},{16,8},{18,... | collective-permute-start | bytes 995336 | tf_op jit(solution)/shard_map/ppermute | solution.py:212
  89.5 39.2 %collective-permute-start = (bf16[256,1152]{1,0:T(8,128)(2,1)}, bf16[256,1152]{1,0:T(8,128)(2,1)}, u32[]{:S(2)}, u32[]{:S(2)}) collective-permute-start(bf16[256,1152]{1,0:T(8,128)(2,1)} %param.28), channel_id=1, source_target_pairs={{0,1},{1,0},{2,3},{3,2},{4,5},{5,4},{6,7},{7,6},{8,9},{9,8},{10,11... | collective-permute-start | bytes 1769480 | tf_op jit(solution)/shard_map/ppermute | solution.py:217
  97.5 108.5 %collective-permute-start.29 = (bf16[288,2304]{1,0:T(8,128)(2,1)}, bf16[288,2304]{1,0:T(8,128)(2,1)}, u32[]{:S(2)}, u32[]{:S(2)}) collective-permute-start(bf16[288,2304]{1,0:T(8,128)(2,1)} %constant_dynamic-update-slice_fusion.14.refs_0_), channel_id=1, source_target_pairs={{0,4},{2,6},{4,0},{6,2},{8,12},{10,14},{12,8},{14,10},{16,20},{18,... | collective-permute-start | bytes 3981320 | tf_op jit(solution)/shard_map/ppermute | solution.py:212
  119.8 86.7 %collective-permute-start.23 = (bf16[288,2304]{1,0:T(8,128)(2,1)}, bf16[288,2304]{1,0:T(8,128)(2,1)}, u32[]{:S(2)}, u32[]{:S(2)}) collective-permute-start(bf16[288,2304]{1,0:T(8,128)(2,1)} %constant_dynamic-update-slice_fusion.10.refs_0_), channel_id=1, source_target_pairs={{0,4},{2,6},{4,0},{6,2},{8,12},{10,14},{12,8},{14,10},{16,20},{18,... | collective-permute-start | bytes 3981320 | tf_op jit(solution)/shard_map/ppermute | solution.py:212
  121.3 64.3 %collective-permute-start.15 = (bf16[288,2432]{1,0:T(8,128)(2,1)S(1)}, bf16[288,2432]{1,0:T(8,128)(2,1)S(1)}, u32[]{:S(2)}, u32[]{:S(2)}) collective-permute-start(bf16[288,2432]{1,0:T(8,128)(2,1)S(1)} %pad_maximum_fusion.1), channel_id=1, source_target_pairs={{0,4},{2,6},{4,0},{6,2},{8,12},{10,14},{12,8},{14,10},{16,20},{18,... | collective-permute-start | bytes 4202504 | tf_op jit(solution)/shard_map/ppermute | solution.py:212
  126.1 60.9 %collective-permute-start.16 = (bf16[288,2432]{1,0:T(8,128)(2,1)S(1)}, bf16[288,2432]{1,0:T(8,128)(2,1)S(1)}, u32[]{:S(2)}, u32[]{:S(2)}) collective-permute-start(bf16[288,2432]{1,0:T(8,128)(2,1)S(1)} %pad_maximum_fusion.1), channel_id=1, source_target_pairs={{0,2},{2,0},{4,6},{6,4},{8,10},{10,8},{12,14},{14,12},{16,18},{18,... | collective-permute-start | bytes 4202504 | tf_op jit(solution)/shard_map/ppermute | solution.py:212
  204.5 40.1 %collective-permute-start.19 = (bf16[256,1152]{1,0:T(8,128)(2,1)S(1)}, bf16[256,1152]{1,0:T(8,128)(2,1)S(1)}, u32[]{:S(2)}, u32[]{:S(2)}) collective-permute-start(bf16[256,1152]{1,0:T(8,128)(2,1)S(1)} %copy-done.71), channel_id=1, source_target_pairs={{0,1},{1,0},{2,3},{3,2},{4,5},{5,4},{6,7},{7,6},{8,9},{9,8},{10,11... | collective-permute-start | bytes 1769480 | tf_op jit(solution)/shard_map/ppermute | solution.py:217
  206.0 55.9 %collective-permute-start.30 = (bf16[288,2304]{1,0:T(8,128)(2,1)}, bf16[288,2304]{1,0:T(8,128)(2,1)}, u32[]{:S(2)}, u32[]{:S(2)}) collective-permute-start(bf16[288,2304]{1,0:T(8,128)(2,1)} %constant_dynamic-update-slice_fusion.14.refs_0_), channel_id=1, source_target_pairs={{0,2},{2,0},{4,6},{6,4},{8,10},{10,8},{12,14},{14,12},{16,18},{18,... | collective-permute-start | bytes 3981320 | tf_op jit(solution)/shard_map/ppermute | solution.py:212
  206.0 72.2 %collective-permute-start.24 = (bf16[288,2304]{1,0:T(8,128)(2,1)}, bf16[288,2304]{1,0:T(8,128)(2,1)}, u32[]{:S(2)}, u32[]{:S(2)}) collective-permute-start(bf16[288,2304]{1,0:T(8,128)(2,1)} %constant_dynamic-update-slice_fusion.10.refs_0_), channel_id=1, source_target_pairs={{0,2},{2,0},{4,6},{6,4},{8,10},{10,8},{12,14},{14,12},{16,18},{18,... | collective-permute-start | bytes 3981320 | tf_op jit(solution)/shard_map/ppermute | solution.py:212
  206.5 55.3 %collective-permute-start.31 = (bf16[288,2304]{1,0:T(8,128)(2,1)}, bf16[288,2304]{1,0:T(8,128)(2,1)}, u32[]{:S(2)}, u32[]{:S(2)}) collective-permute-start(bf16[288,2304]{1,0:T(8,128)(2,1)} %collective-permute-done.29.refs_1_), channel_id=1, source_target_pairs={{0,2},{2,0},{4,6},{6,4},{8,10},{10,8},{12,14},{14,12},{16,18},{18,... | collective-permute-start | bytes 3981320 | tf_op jit(solution)/shard_map/ppermute | solution.py:212
  232.8 45.4 %collective-permute-start.25 = (bf16[288,2304]{1,0:T(8,128)(2,1)}, bf16[288,2304]{1,0:T(8,128)(2,1)}, u32[]{:S(2)}, u32[]{:S(2)}) collective-permute-start(bf16[288,2304]{1,0:T(8,128)(2,1)} %collective-permute-done.23.refs_1_), channel_id=1, source_target_pairs={{0,2},{2,0},{4,6},{6,4},{8,10},{10,8},{12,14},{14,12},{16,18},{18,... | collective-permute-start | bytes 3981320 | tf_op jit(solution)/shard_map/ppermute | solution.py:212
  297.6 43.9 %collective-permute-start.33 = (bf16[512,1152]{0,1:T(8,128)(2,1)}, bf16[512,1152]{0,1:T(8,128)(2,1)}, u32[]{:S(2)}, u32[]{:S(2)}) collective-permute-start(bf16[512,1152]{0,1:T(8,128)(2,1)} %copy.262), channel_id=1, source_target_pairs={{0,1},{1,0},{2,3},{3,2},{4,5},{5,4},{6,7},{7,6},{8,9},{9,8},{10,11... | collective-permute-start | bytes 3538952 | tf_op jit(solution)/shard_map/ppermute | solution.py:217
  307.4 132.1 %collective-permute-start.56 = (bf16[576,2304]{1,0:T(8,128)(2,1)}, bf16[576,2304]{1,0:T(8,128)(2,1)}, u32[]{:S(2)}, u32[]{:S(2)}) collective-permute-start(bf16[576,2304]{1,0:T(8,128)(2,1)} %get-tuple-element.90), channel_id=1, source_target_pairs={{0,2},{2,0},{4,6},{6,4},{8,10},{10,8},{12,14},{14,12},{16,18},{18,... | collective-permute-start | bytes 7962632 | tf_op jit(solution)/shard_map/ppermute | solution.py:212
  447.2 56.0 %collective-permute-start.52 = (bf16[288,2304]{1,0:T(8,128)(2,1)S(1)}, bf16[288,2304]{1,0:T(8,128)(2,1)S(1)}, u32[]{:S(2)}, u32[]{:S(2)}) collective-permute-start(bf16[288,2304]{1,0:T(8,128)(2,1)S(1)} %get-tuple-element.261), channel_id=1, source_target_pairs={{0,4},{2,6},{4,0},{6,2},{8,12},{10,14},{12,8},{14,10},{16,20},{18,... | collective-permute-start | bytes 3981320 | tf_op jit(solution)/shard_map/ppermute | solution.py:212
  447.8 76.6 %collective-permute-start.42 = (bf16[288,1728]{1,0:T(8,128)(2,1)S(1)}, bf16[288,1728]{1,0:T(8,128)(2,1)S(1)}, u32[]{:S(2)}, u32[]{:S(2)}) collective-permute-start(bf16[288,1728]{1,0:T(8,128)(2,1)S(1)} %get-tuple-element.263), channel_id=1, source_target_pairs={{0,4},{2,6},{4,0},{6,2},{8,12},{10,14},{12,8},{14,10},{16,20},{18,... | collective-permute-start | bytes 2985992 | tf_op jit(solution)/shard_map/ppermute | solution.py:212
  475.0 49.5 %collective-permute-start.58 = (bf16[72,2304]{1,0:T(8,128)(2,1)S(1)}, bf16[72,2304]{1,0:T(8,128)(2,1)S(1)}, u32[]{:S(2)}, u32[]{:S(2)}) collective-permute-start(bf16[72,2304]{1,0:T(8,128)(2,1)S(1)} %get-tuple-element.265), channel_id=1, source_target_pairs={{0,24},{2,26},{4,28},{6,30},{8,0},{10,2},{12,4},{14,6},{16,8},{18,... | collective-permute-start | bytes 995336 | tf_op jit(solution)/shard_map/ppermute | solution.py:212
  477.2 50.2 %collective-permute-start.60 = (bf16[72,2304]{1,0:T(8,128)(2,1)S(1)}, bf16[72,2304]{1,0:T(8,128)(2,1)S(1)}, u32[]{:S(2)}, u32[]{:S(2)}) collective-permute-start(bf16[72,2304]{1,0:T(8,128)(2,1)S(1)} %get-tuple-element.266), channel_id=1, source_target_pairs={{0,8},{2,10},{4,12},{6,14},{8,16},{10,18},{12,20},{14,22},{16,24},... | collective-permute-start | bytes 995336 | tf_op jit(solution)/shard_map/ppermute | solution.py:212
  477.2 51.3 %collective-permute-start.59 = (bf16[72,2304]{1,0:T(8,128)(2,1)S(1)}, bf16[72,2304]{1,0:T(8,128)(2,1)S(1)}, u32[]{:S(2)}, u32[]{:S(2)}) collective-permute-start(bf16[72,2304]{1,0:T(8,128)(2,1)S(1)} %get-tuple-element.267), channel_id=1, source_target_pairs={{0,16},{2,18},{4,20},{6,22},{8,24},{10,26},{12,28},{14,30},{16,0},... | collective-permute-start | bytes 995336 | tf_op jit(solution)/shard_map/ppermute | solution.py:212
  531.2 39.5 %collective-permute-start.44 = (bf16[72,1728]{1,0:T(8,128)(2,1)S(1)}, bf16[72,1728]{1,0:T(8,128)(2,1)S(1)}, u32[]{:S(2)}, u32[]{:S(2)}) collective-permute-start(bf16[72,1728]{1,0:T(8,128)(2,1)S(1)} %get-tuple-element.275), channel_id=1, source_target_pairs={{0,16},{2,18},{4,20},{6,22},{8,24},{10,26},{12,28},{14,30},{16,0},... | collective-permute-start | bytes 746504 | tf_op jit(solution)/shard_map/ppermute | solution.py:212
  (199 other events, 2794.2 us)

commit v2 on v1

--- a/solution.py
+++ b/solution.py
@@ -5,6 +5,7 @@
 import jax.numpy as jnp
 from jax import lax
 from jax.experimental import pallas as pl
+from jax.experimental.layout import Layout, with_layout_constraint
 from jax.experimental.pallas import tpu as pltpu
 from jax.sharding import PartitionSpec as P
 
@@ -229,14 +230,6 @@
     return ((their_z * xside + their_x) * CORES + their_core).reshape(count)
 
 
-def gather_pieces(shard):
-    xside = lax.axis_size("dp") // (ZSIDE * CORES)
-    near = jnp.concatenate([shard] + [send(shard, "z", hop) for hop in range(1, ZSIDE)], axis=0)
-    mine = [near] + [send(near, "x", turn) for turn in range(1, xside)]
-    other = [send(piece, "core", 1) for piece in mine]
-    return mine + other
-
-
 def gather_rows(shard):
     xside = lax.axis_size("dp") // (ZSIDE * CORES)
     near = jnp.concatenate([shard] + [send(shard, "z", hop) for hop in range(1, ZSIDE)], axis=0)
@@ -244,21 +237,79 @@
     return jnp.concatenate([mine, send(mine, "core", 1)], axis=0)
 
 
-def reduce_rows(mine, other):
+def by_rows(values):
+    return with_layout_constraint(values, Layout(tuple(range(values.ndim))))
+
+
+def gated(value, gate):
+    return lax.optimization_barrier((value, gate))
+
+
+def fold_core(mine, other):
     xside = lax.axis_size("dp") // (ZSIDE * CORES)
-    kind = mine.dtype
     came = send(other, "core", 1)
     rows = mine.shape[0] // xside
     parts = []
     for turn in range(xside):
         cut = slice(turn * rows, (turn + 1) * rows)
-        parts.append(mine[cut].astype(jnp.float32) + came[cut].astype(jnp.float32))
-    came_x = [send(parts[turn].astype(kind), "x", -turn) for turn in range(1, xside)]
-    rows = rows // ZSIDE
+        added = mine[cut].astype(jnp.float32) + came[cut].astype(jnp.float32)
+        parts.append(added.astype(mine.dtype))
+    return parts
+
+
+def fold_x(parts):
+    came = [send(parts[turn], "x", -turn) for turn in range(1, len(parts))]
+    rows = parts[0].shape[0] // ZSIDE
     cuts = []
     for hop in range(ZSIDE):
         cut = slice(hop * rows, (hop + 1) * rows)
-        cuts.append(sum([piece[cut].astype(jnp.float32) for piece in came_x], parts[0][cut]))
+        added = parts[0][cut].astype(jnp.float32)
+        for piece in came:
+            added = added + piece[cut].astype(jnp.float32)
+        cuts.append(added.astype(parts[0].dtype))
+    return cuts
+
+
+def fold_z(cuts):
+    total = cuts[0].astype(jnp.float32)
+    for hop in range(1, ZSIDE):
+        total = total + send(cuts[hop], "z", -hop).astype(jnp.float32)
+    return total
+
+
+def reduce_rows(mine, other):
+    return fold_z(fold_x(fold_core(mine, other)))
+
+
+def split_core(gradient):
+    count = lax.axis_size("dp")
+    xside = count // (ZSIDE * CORES)
+    z, x, core = place_of(lax.axis_index("dp"), count)
+    rows = gradient.shape[0] // count
+    blocks = gradient.reshape(ZSIDE, xside, CORES, rows, -1)
+    halves = []
+    for side in (core, 1 - core):
+        half = lax.dynamic_index_in_dim(blocks, side, 2, keepdims=False)
+        turns = [(x - turn) % xside for turn in range(xside)]
+        cut = [lax.dynamic_index_in_dim(half, turn, 1, keepdims=False) for turn in turns]
+        halves.append(cut)
+    return halves
+
+
+def fold_rows(gradient):
+    z = place_of(lax.axis_index("dp"), lax.axis_size("dp"))[0]
+    kind = gradient.dtype
+    mine, other = split_core(gradient)
+    parts = []
+    for own, theirs in zip(mine, other):
+        came = send(theirs, "core", 1)
+        parts.append((own.astype(jnp.float32) + came.astype(jnp.float32)).astype(kind))
+    total = parts[0].astype(jnp.float32)
+    for turn in range(1, len(parts)):
+        total = total + send(parts[turn], "x", -turn).astype(jnp.float32)
+    cuts = [
+        lax.dynamic_index_in_dim(total, (z - hop) % ZSIDE, 0, keepdims=False) for hop in range(ZSIDE)
+    ]
     total = cuts[0]
     for hop in range(1, ZSIDE):
         total = total + send(cuts[hop].astype(kind), "z", -hop).astype(jnp.float32)
@@ -300,17 +351,9 @@
     return values
 
 
-def mlp_kernel(pieces, has_start, rows_ref, rows_t_ref, grad_ref, grad_t_ref, *refs):
-    weights = refs[:pieces]
-    refs = refs[pieces:]
-    if has_start:
-        start_out, start_in = refs[:2]
-        refs = refs[2:]
-    out_ref, in_ref, mine_ref, other_ref, held, out_acc, in_acc = refs
+def mlp_kernel(rows_ref, rows_t_ref, grad_ref, grad_t_ref, held, *refs):
+    out_ref, in_ref, target, out_acc, in_acc = refs
     step = pl.program_id(0)
-    share = held.shape[0] // pieces
-    for index in range(pieces):
-        held[index * share : (index + 1) * share, :] = weights[index][...]
     width = held.shape[1] // 3
     gate_w = held[:, :width]
     up_w = held[:, width : 2 * width]
@@ -318,12 +361,8 @@
 
     @pl.when(step == 0)
     def _():
-        if has_start:
-            out_acc[...] = start_out[...]
-            in_acc[...] = start_in[...]
-        else:
-            out_acc[...] = jnp.zeros_like(out_acc)
-            in_acc[...] = jnp.zeros_like(in_acc)
+        out_acc[...] = jnp.zeros_like(out_acc)
+        in_acc[...] = jnp.zeros_like(in_acc)
 
     across = (((1,), (1,)), ((), ()))
     gate = jnp.dot(rows_ref[...], gate_w, preferred_element_type=jnp.float32)
@@ -338,19 +377,14 @@
     in_acc[...] += lax.dot_general(
         d_gate, gate_w, across, preferred_element_type=jnp.float32
     ) + lax.dot_general(d_up, up_w, across, preferred_element_type=jnp.float32)
-    half = mine_ref.shape[0]
-    for target, begin in ((mine_ref, 0), (other_ref, half)):
-        rows_t = rows_t_ref[begin : begin + half, :]
-        grad_t = grad_t_ref[begin : begin + half, :]
-        target[:, :width] = jnp.dot(rows_t, d_gate, preferred_element_type=jnp.float32).astype(
-            target.dtype
-        )
-        target[:, width : 2 * width] = jnp.dot(
-            rows_t, d_up, preferred_element_type=jnp.float32
-        ).astype(target.dtype)
-        target[:, 2 * width :] = jnp.dot(
-            grad_t, hidden, preferred_element_type=jnp.float32
-        ).astype(target.dtype)
+    rows_t = rows_t_ref[...]
+    for at, left, right in (
+        (0, rows_t, d_gate),
+        (width, rows_t, d_up),
+        (2 * width, grad_t_ref[...], hidden),
+    ):
+        product = jnp.dot(left, right, preferred_element_type=jnp.float32)
+        target[:, at : at + width] = product.astype(target.dtype)
 
     @pl.when(step == pl.num_programs(0) - 1)
     def _():
@@ -358,39 +392,31 @@
         in_ref[...] = in_acc[...].astype(in_ref.dtype)
 
 
-def mlp_part(rows, rows_t, grad, grad_t, pieces, start, blocks, last):
+def mlp_part(rows, grad, weights, blocks):
     count, width = rows.shape
-    columns = pieces[0].shape[1]
+    columns = weights.shape[1]
     block = columns // blocks
     whole = pl.BlockSpec((count, width), lambda i: (0, 0))
     whole_t = pl.BlockSpec((width, count), lambda i: (0, 0))
-    kind = jnp.bfloat16 if last else jnp.float32
-    half = jax.ShapeDtypeStruct((width // 2, columns), jnp.bfloat16)
-    starts = [] if start is None else list(start)
-    flops = 18 * count * width * (columns // 3)
+    across = pl.BlockSpec((width, block), lambda i: (0, i))
     return pl.pallas_call(
-        partial(mlp_kernel, len(pieces), len(starts) > 0),
+        mlp_kernel,
         grid=(blocks,),
-        in_specs=[whole, whole_t, whole, whole_t]
-        + [pl.BlockSpec((p.shape[0], block), lambda i: (0, i)) for p in pieces]
-        + [whole] * len(starts),
-        out_specs=[whole, whole]
-        + [pl.BlockSpec((width // 2, block), lambda i: (0, i))] * 2,
-        out_shape=[jax.ShapeDtypeStruct((count, width), kind)] * 2 + [half, half],
-        scratch_shapes=[
-            pltpu.VMEM((width, block), jnp.bfloat16),
-            pltpu.VMEM((count, width), jnp.float32),
-            pltpu.VMEM((count, width), jnp.float32),
-        ],
+        in_specs=[whole, whole_t, whole, whole_t, across],
+        out_specs=[whole, whole, across],
+        out_shape=[jax.ShapeDtypeStruct((count, width), jnp.bfloat16)] * 2
+        + [jax.ShapeDtypeStruct((width, columns), jnp.bfloat16)],
+        scratch_shapes=[pltpu.VMEM((count, width), jnp.float32)] * 2,
         cost_estimate=pl.CostEstimate(
-            flops=flops, bytes_accessed=8 * width * columns, transcendentals=count * columns // 3
+            flops=6 * count * width * columns,
+            bytes_accessed=4 * width * columns,
+            transcendentals=count * columns // 3,
         ),
         compiler_params=pltpu.CompilerParams(vmem_limit_bytes=60 * 1024 * 1024),
-    )(rows, rows_t, grad, grad_t, *pieces, *starts)
-
-
-def mlp_plain(rows, grad, pieces, start, blocks, last):
-    weights = jnp.concatenate(pieces, axis=0)
+    )(rows, rows.T, grad, grad.T, weights)
+
+
+def mlp_plain(rows, grad, weights, blocks):
     width = weights.shape[0]
     block = weights.shape[1] // (3 * blocks)
     split = weights.reshape(width, blocks, 3, block)
@@ -406,10 +432,6 @@
     in_sum = jnp.dot(d_gate, gate_w.T, preferred_element_type=jnp.float32) + jnp.dot(
         d_up, up_w.T, preferred_element_type=jnp.float32
     )
-    if start is not None:
-        out_sum = out_sum + start[0]
-        in_sum = in_sum + start[1]
-    kind = jnp.bfloat16 if last else jnp.float32
     grads = [
         jnp.einsum("gd,gf->df", left, right, preferred_element_type=jnp.float32)
         .astype(jnp.bfloat16)
@@ -417,11 +439,88 @@
         for left, right in ((rows, d_gate), (rows, d_up), (grad, hidden))
     ]
     packed = jnp.stack(grads, axis=2).reshape(width, 3 * blocks * block)
-    return (out_sum.astype(kind), in_sum.astype(kind), packed[: width // 2], packed[width // 2 :])
-
-
-def pad_columns(values, columns):
-    return jnp.pad(values, ((0, 0), (0, columns - values.shape[1])))
+    return (out_sum.astype(jnp.bfloat16), in_sum.astype(jnp.bfloat16), packed)
+
+
+def pack_kernel(stride, block, qkv_ref, out_ref, gateup_ref, down_ref, attn_low, mlp_low):
+    columns = out_ref.shape[1]
+    attn_low[...] = jnp.zeros_like(attn_low)
+    for slot in range(3):
+        attn_low[:, slot * stride : slot * stride + columns] = qkv_ref[slot].astype(jnp.bfloat16)
+    attn_low[:, 3 * stride : 3 * stride + columns] = out_ref[...].astype(jnp.bfloat16)
+    for begin in range(0, down_ref.shape[1], block):
+        cut = slice(begin, begin + block)
+        at = 3 * begin
+        mlp_low[:, at : at + block] = gateup_ref[0, :, cut].astype(jnp.bfloat16)
+        mlp_low[:, at + block : at + 2 * block] = gateup_ref[1, :, cut].astype(jnp.bfloat16)
+        mlp_low[:, at + 2 * block : at + 3 * block] = down_ref[:, cut].astype(jnp.bfloat16)
+
+
+def pack(qkv, out, gateup, down, stride, block):
+    rows, hidden = down.shape
+    low = lambda columns: jax.ShapeDtypeStruct((rows, columns), jnp.bfloat16)
+    return pl.pallas_call(
+        partial(pack_kernel, stride, block), out_shape=[low(4 * stride), low(3 * hidden)]
+    )(qkv, out, gateup, down)
+
+
+def mod_kernel(stride, rows_ref, ada_ref, target):
+    columns = ada_ref.shape[2]
+    target[...] = jnp.zeros_like(target)
+    for slot in range(ada_ref.shape[0]):
+        target[:, slot * stride : slot * stride + columns] = jnp.dot(
+            rows_ref[...], ada_ref[slot].astype(jnp.bfloat16), preferred_element_type=jnp.float32
+        )
+
+
+def mod_product(rows, ada, stride):
+    return pl.pallas_call(
+        partial(mod_kernel, stride),
+        out_shape=jax.ShapeDtypeStruct((rows.shape[0], ada.shape[0] * stride), jnp.float32),
+    )(rows, ada)
+
+
+def adam_kernel(stride, block, rates, clip_ref, *refs):
+    clip = clip_ref[0, 0]
+    ada_g, qkv_g, out_g, mlp_g, bias_g, gain_g = refs[:6]
+    states, targets = refs[6:27], refs[27:]
+    ada, bias, qkv, out, gateup, down, gain = [
+        (states[3 * i : 3 * i + 3], targets[3 * i : 3 * i + 3], rates[i]) for i in range(7)
+    ]
+
+    def step(group, index, gradient):
+        held, put, rate = group
+        result = adam_update(*[ref[index] for ref in held], gradient, rate, clip)
+        for ref, value in zip(put, result):
+            ref[index] = value
+
+    columns = out[0][0].shape[1]
+    for group, source in ((ada, ada_g), (qkv, qkv_g)):
+        for slot in range(group[0][0].shape[0]):
+            step(group, slot, source[:, slot * stride : slot * stride + columns])
+    step(out, slice(None), out_g[:, :columns])
+    for begin in range(0, down[0][0].shape[1], block):
+        cut = slice(begin, begin + block)
+        at = 3 * begin
+        for slot, group, index in (
+            (0, gateup, (0, slice(None), cut)),
+            (1, gateup, (1, slice(None), cut)),
+            (2, down, (slice(None), cut)),
+        ):
+            gradient = mlp_g[:, at + slot * block : at + (slot + 1) * block]
+            step(group, index, gradient.astype(jnp.float32))
+    step(bias, slice(None), bias_g[...])
+    step(gain, slice(None), gain_g[...])
+
+
+def adam_all(clip, grads, states, stride, block, rates):
+    vmem = pl.BlockSpec(memory_space=pltpu.VMEM)
+    return pl.pallas_call(
+        partial(adam_kernel, stride, block, rates),
+        in_specs=[pl.BlockSpec(memory_space=pltpu.SMEM)] + [vmem] * (len(grads) + len(states)),
+        out_shape=[jax.ShapeDtypeStruct(x.shape, x.dtype) for x in states],
+        compiler_params=pltpu.CompilerParams(vmem_limit_bytes=60 * 1024 * 1024),
+    )(clip.reshape(1, 1), *grads, *states)
 
 
 def padded(columns):
@@ -472,39 +571,16 @@
     hidden_share = down_weight.shape[1]
     bf16 = jnp.bfloat16
 
-    qkv_columns = padded(3 * column_share)
-    out_columns = padded(column_share)
-    attn_shard = jnp.concatenate(
-        [
-            pad_columns(qkv_weight.astype(bf16).reshape(row_share, -1), qkv_columns),
-            pad_columns(out_weight.astype(bf16), out_columns),
-        ],
-        axis=1,
-    )
-    blocks = max(1, hidden_share // 512)
-    block = hidden_share // (2 * blocks)
-    mlp_split = jnp.stack(
-        [
-            part.astype(bf16).reshape(row_share, 2, blocks, block)
-            for part in (gateup_weight[:, 0], gateup_weight[:, 1], down_weight)
-        ],
-        axis=3,
-    )
-    mlp_shards = [mlp_split[:, half].reshape(row_share, 3 * blocks * block) for half in range(2)]
-
-    order = block_order(data_rank, data_count)
-    column_of = (order[:, None] * row_share + jnp.arange(row_share, dtype=jnp.int32)).reshape(-1)
-    to_held = (jnp.arange(model_width, dtype=jnp.int32)[:, None] == column_of[None, :]).astype(bf16)
-
-    def hold(values):
-        return jnp.dot(values, to_held, preferred_element_type=jnp.float32).astype(bf16)
-
-    def unhold(values):
-        return lax.dot_general(
-            values, to_held, (((1,), (1,)), ((), ())), preferred_element_type=jnp.float32
-        ).astype(bf16)
+    stride = padded(column_share)
+    block = 256 if hidden_share % 512 == 0 else hidden_share
+    blocks = hidden_share // block
+    swap = lambda values: jnp.transpose(values, (1, 0, 2))
+    attn_shard, mlp_shard = pack(
+        swap(qkv_weight), out_weight, swap(gateup_weight), down_weight, stride, block
+    )
 
     ids = gather_rows(jnp.stack([class_id[0], timestep[0]])[None])
+    ids, attn_shard = gated(ids, attn_shard)
     item_ids = ids[:, 0].reshape(-1)
     item_steps = ids[:, 1].reshape(-1)
     class_onehot = (
@@ -515,15 +591,12 @@
     )
     silu_all = jax.nn.silu(condition).astype(bf16)
     silu_own = lax.dynamic_slice_in_dim(silu_all, data_rank * row_share, row_share, 1)
-    mod_part = jnp.dot(
-        silu_own,
-        ada_weight.astype(bf16).reshape(row_share, 6 * column_share),
-        preferred_element_type=jnp.float32,
-    )
+    mod_part = mod_product(silu_own, swap(ada_weight), stride)
     half_items = data_count * item_count // 2
     mod_share = reduce_rows(mod_part[:half_items], mod_part[half_items:])
+    mod_share = mod_share.reshape(item_count, 6, stride)[:, :, :column_share]
     bias_share = lax.dynamic_slice_in_dim(ada_bias, tensor_rank * column_share, column_share, 1)
-    mod_share = mod_share.reshape(item_count, 6, column_share) + bias_share[None]
+    mod_share = mod_share + bias_share[None]
     if tensor_count == 2:
         mod_other = tensor_send(mod_share, 1)
         lower = jnp.where(tensor_rank == 0, mod_share, mod_other)
@@ -531,17 +604,9 @@
         modulation = jnp.concatenate([lower, upper], axis=2)
     else:
         modulation = lax.all_gather(mod_share, "tensor", axis=2, tiled=True)
-    modulation = jnp.dot(
-        modulation.reshape(item_count * 6, model_width),
-        to_held.astype(jnp.float32),
-        precision=PRECISE,
-        preferred_element_type=jnp.float32,
-    ).reshape(item_count, 6, model_width)
-
-    tokens_all = hold(tensor_gather(tokens))
-    cot_all = hold(tensor_gather(cotangent))
+    tokens_all = tensor_gather(tokens)
+    cot_all = tensor_gather(cotangent)
     base_rows = tokens_all.astype(jnp.float32)
-    cot_rows = cot_all.astype(jnp.float32)
     row_blocks = (tensor_rank - jnp.arange(tensor_count, dtype=jnp.int32)) % tensor_count
     row_index = (
         row_blocks[:, None] * local_rows + jnp.arange(local_rows, dtype=jnp.int32)[None, :]
@@ -566,16 +631,16 @@
             ]
         )
 
-    attn_pieces = gather_pieces(attn_shard)
-    mlp_pieces = [gather_pieces(shard) for shard in mlp_shards]
-    attn_full = jnp.concatenate(attn_pieces, axis=0)
-    full_qkv = attn_full[:, : 3 * column_share]
-    full_out = attn_full[:, qkv_columns : qkv_columns + column_share]
-
-    attn_in = modulate_in(base_rows, mod_rows(1, group_rows), mod_rows(0, group_rows)).astype(bf16)
+    full_attn = lax.all_gather(attn_shard, "dp", axis=0, tiled=True)
+    full_mlp = lax.all_gather(mlp_shard, "dp", axis=0, tiled=True)
+    full_qkv = full_attn[:, : 3 * stride]
+    full_out = full_attn[:, 3 * stride : 3 * stride + column_share]
+
+    attn_in = modulate_in(base_rows, mod_rows(1, group_rows), mod_rows(0, group_rows))
+    attn_in = by_rows(attn_in.astype(bf16))
     qkv_raw = jnp.dot(attn_in, full_qkv, preferred_element_type=jnp.float32)
     raw_query, raw_key, raw_value = [
-        qkv_raw[:, slot * column_share : (slot + 1) * column_share] for slot in range(3)
+        qkv_raw[:, slot * stride : slot * stride + column_share] for slot in range(3)
     ]
     query_rot, key_rot = qk_prepare(raw_query, raw_key, qk_gain, tables)
     query_low = query_rot.astype(bf16)
@@ -583,9 +648,10 @@
     value_low = raw_value.reshape(group_rows, -1, head_size).astype(bf16)
     attn_vals, log_sums = attend(query_low, key_low, value_low, segment)
     attn_low = attn_vals.reshape(group_rows, column_share).astype(bf16)
-    branch = tensor_total(
-        jnp.einsum("gc,dc->gd", attn_low, full_out, preferred_element_type=jnp.float32).astype(bf16)
-    )
+    branch = jnp.einsum("gc,dc->gd", attn_low, full_out, preferred_element_type=jnp.float32)
+    branch, cot_all = gated(by_rows(branch.astype(bf16)), cot_all)
+    cot_rows = cot_all.astype(jnp.float32)
+    branch = tensor_total(branch)
     mid_rows = base_rows + mod_rows(2, group_rows) * branch
     scale_two = mod_rows(4, group_rows)
     mlp_in = modulate_in(mid_rows, scale_two, mod_rows(3, group_rows)).astype(bf16)
@@ -593,34 +659,22 @@
     d_branch_mlp = (gate_two * cot_rows).astype(bf16)
 
     if group_rows <= 512:
-        mlp_in_t = mlp_in.T
-        d_branch_t = d_branch_mlp.T
-        first = mlp_part(
-            mlp_in, mlp_in_t, d_branch_mlp, d_branch_t, mlp_pieces[0], None, blocks, False
-        )
-        second = mlp_part(
-            mlp_in, mlp_in_t, d_branch_mlp, d_branch_t, mlp_pieces[1], first[:2], blocks, True
-        )
+        out_part, in_part, g_mlp = mlp_part(mlp_in, d_branch_mlp, full_mlp, blocks)
     else:
-        first = mlp_plain(mlp_in, d_branch_mlp, mlp_pieces[0], None, blocks, False)
-        second = mlp_plain(mlp_in, d_branch_mlp, mlp_pieces[1], first[:2], blocks, True)
-    d_mlp_in = tensor_total(second[1])
-    branch_mlp = tensor_reduce(second[0])
+        out_part, in_part, g_mlp = mlp_plain(mlp_in, d_branch_mlp, full_mlp, blocks)
+    sum_mlp = lax.psum_scatter(g_mlp, "dp", scatter_dimension=0, tiled=True)
+    d_mlp_in = tensor_total(in_part)
+    branch_mlp = tensor_reduce(out_part)
     out_rows = mid_rows[:local_rows] + gate_two[:local_rows] * branch_mlp
-    out_tokens = unhold(out_rows.astype(bf16))
-    sum_mlp = [reduce_rows(part[2], part[3]) for part in (first, second)]
+    out_tokens = out_rows.astype(bf16)
 
     d_mid_norm, d_scale_two, d_shift_two = jax.vjp(
         modulate_in, mid_rows, scale_two, jnp.zeros_like(mid_rows)
     )[1](d_mlp_in)
     d_mid = cot_rows + d_mid_norm
-    d_branch_attn = (mod_rows(2, group_rows) * d_mid).astype(bf16)
-    half_width = model_width // 2
-    g_out = [
-        jnp.einsum("gd,gc->dc", part, attn_low, preferred_element_type=jnp.float32).astype(bf16)
-        for part in (d_branch_attn[:, :half_width], d_branch_attn[:, half_width:])
-    ]
-    sum_out = reduce_rows(g_out[0], g_out[1])
+    d_branch_attn = by_rows((mod_rows(2, group_rows) * d_mid).astype(bf16))
+    g_out = jnp.einsum("gd,gc->dc", d_branch_attn, attn_low, preferred_element_type=jnp.float32)
+    sum_out = fold_rows(g_out.astype(bf16))
     d_attn = jnp.einsum("gd,dc->gc", d_branch_attn, full_out, preferred_element_type=jnp.float32)
     d_attn = d_attn.astype(bf16).reshape(query_low.shape)
     d_query_rot, d_key_rot, d_values = attend_back(
@@ -628,22 +682,20 @@
     )
     _, pull_qk = jax.vjp(partial(qk_prepare, tables=tables), raw_query, raw_key, qk_gain)
     d_query_raw, d_key_raw, g_gain = pull_qk((d_query_rot, d_key_rot))
+    spare = jnp.zeros((group_rows, stride - column_share), jnp.float32)
     d_qkv_low = jnp.concatenate(
-        [d_query_raw, d_key_raw, d_values.reshape(group_rows, column_share)], axis=1
+        [d_query_raw, spare, d_key_raw, spare, d_values.reshape(group_rows, -1), spare], axis=1
     ).astype(bf16)
     d_attn_part = jnp.einsum("gc,dc->gd", d_qkv_low, full_qkv, preferred_element_type=jnp.float32)
-    d_attn_in = tensor_reduce(d_attn_part.astype(bf16))
-    g_qkv = [
-        jnp.einsum("gd,gc->dc", part, d_qkv_low, preferred_element_type=jnp.float32).astype(bf16)
-        for part in (attn_in[:, :half_width], attn_in[:, half_width:])
-    ]
-    sum_qkv = reduce_rows(g_qkv[0], g_qkv[1])
+    d_attn_in = tensor_reduce(by_rows(d_attn_part.astype(bf16)))
+    g_qkv = jnp.einsum("gd,gc->dc", attn_in, d_qkv_low, preferred_element_type=jnp.float32)
+    sum_qkv = fold_rows(g_qkv.astype(bf16))
 
     own_scale = mod_rows(1, local_rows)
     d_base_norm, d_scale_one, d_shift_one = jax.vjp(
         modulate_in, base_rows[:local_rows], own_scale, jnp.zeros_like(own_scale)
     )[1](d_attn_in)
-    input_grad = unhold((d_mid[:local_rows] + d_base_norm).astype(bf16))
+    input_grad = (d_mid[:local_rows] + d_base_norm).astype(bf16)
     d_mod_part = jnp.stack(
         [
             mod_sums(d_shift_one),
@@ -655,20 +707,14 @@
         ],
         axis=1,
     )
-    d_mod_part = lax.dot_general(
-        d_mod_part.reshape(item_count * 6, model_width),
-        to_held.astype(jnp.float32),
-        (((1,), (1,)), ((), ())),
-        precision=PRECISE,
-        preferred_element_type=jnp.float32,
-    ).reshape(item_count, 6, model_width)
     if tensor_count == 2:
         lower, upper = d_mod_part[:, :, :column_share], d_mod_part[:, :, column_share:]
         theirs = jnp.where(tensor_rank == 0, upper, lower)
         d_mod = jnp.where(tensor_rank == 0, lower, upper) + tensor_send(theirs, 1)
     else:
         d_mod = lax.psum_scatter(d_mod_part, "tensor", scatter_dimension=2, tiled=True)
-    d_mod_all = gather_rows(d_mod.reshape(item_count, 6 * column_share))
+    d_mod = jnp.pad(d_mod, ((0, 0), (0, 0), (0, stride - column_share)))
+    d_mod_all = gather_rows(d_mod.reshape(item_count, 6 * stride))
     sum_ada = lax.dot_general(
         silu_own.astype(jnp.float32),
         d_mod_all,
@@ -676,7 +722,7 @@
         precision=PRECISE,
         preferred_element_type=jnp.float32,
     )
-    bias_share = jnp.sum(d_mod_all, axis=0).reshape(6, column_share)
+    bias_share = jnp.sum(d_mod_all, axis=0).reshape(6, stride)[:, :column_share]
     if tensor_count == 2:
         bias_other = tensor_send(bias_share, 1)
         lower = jnp.where(tensor_rank == 0, bias_share, bias_other)
@@ -687,8 +733,7 @@
 
     local_squares = jnp.sum(sum_ada * sum_ada) + jnp.sum(sum_qkv * sum_qkv)
     local_squares = local_squares + jnp.sum(sum_out * sum_out)
-    for part in sum_mlp:
-        local_squares = local_squares + jnp.sum(part * part)
+    local_squares = local_squares + jnp.sum(jnp.square(sum_mlp.astype(jnp.float32)))
     packet = jnp.concatenate(
         [
             g_gain.reshape(-1),
@@ -707,48 +752,27 @@
     clip = limit / jnp.maximum(grad_norm, limit)
     matrix_rate = model_width ** (-0.5)
 
-    g_ada = sum_ada.reshape(ada_weight.shape)
-    g_qkv_sum = sum_qkv.reshape(qkv_weight.shape)
-    mlp_sum = jnp.stack(
-        [part.reshape(row_share, blocks, 3, block) for part in sum_mlp], axis=1
-    )
-    g_gateup = jnp.stack(
-        [mlp_sum[:, :, :, slot].reshape(row_share, hidden_share) for slot in range(2)], axis=1
-    )
-    g_down = mlp_sum[:, :, :, 2].reshape(row_share, hidden_share)
-
-    new_ada = adam_update(ada_weight, ada_m, ada_v, g_ada, matrix_rate, clip)
-    new_bias = adam_update(ada_bias, bias_m, bias_v, bias_grad, SMALL_RATE, clip)
-    new_qkv = adam_update(qkv_weight, qkv_m, qkv_v, g_qkv_sum, matrix_rate, clip)
-    new_out = adam_update(out_weight, out_m, out_v, sum_out, (model_width // 64) ** (-0.5), clip)
-    new_gateup = adam_update(gateup_weight, gateup_m, gateup_v, g_gateup, matrix_rate, clip)
-    new_down = adam_update(down_weight, down_m, down_v, g_down, FF ** (-0.5), clip)
-    new_gain = adam_update(qk_gain, gain_m, gain_v, gain_total, SMALL_RATE, clip)
+    out_rate = (model_width // 64) ** (-0.5)
+    rates = (matrix_rate, SMALL_RATE, matrix_rate, out_rate, matrix_rate, FF ** (-0.5), SMALL_RATE)
+    states = []
+    for group in (
+        (ada_weight, ada_m, ada_v),
+        (ada_bias, bias_m, bias_v),
+        (qkv_weight, qkv_m, qkv_v),
+        (out_weight, out_m, out_v),
+        (gateup_weight, gateup_m, gateup_v),
+        (down_weight, down_m, down_v),
+        (qk_gain, gain_m, gain_v),
+    ):
+        states += [swap(x) if x.ndim == 3 else x for x in group]
+    grads = [sum_ada, sum_qkv, sum_out, sum_mlp, bias_grad, gain_total]
+    updated = adam_all(clip, grads, states, stride, block, rates)
+    updated = [swap(x) if x.ndim == 3 else x for x in updated]
     return (
         out_tokens,
         input_grad,
         grad_norm,
-        new_ada[0],
-        new_ada[1],
-        new_ada[2],
-        new_bias[0],
-        new_bias[1],
-        new_bias[2],
-        new_qkv[0],
-        new_qkv[1],
-        new_qkv[2],
-        new_out[0],
-        new_out[1],
-        new_out[2],
-        new_gateup[0],
-        new_gateup[1],
-        new_gateup[2],
-        new_down[0],
-        new_down[1],
-        new_down[2],
-        new_gain[0],
-        new_gain[1],
-        new_gain[2],
+        *updated,
     )
 
 

time: 636 us -> 427 us (0.67)
  waiting for transfers between devices: 290 us -> 170 us
  local copies, waits for them, and re-layouts: 89.7 us -> 46.8 us
  starting transfers between devices: 77.1 us -> 52.6 us
  matrix products: 51.2 us -> 32.6 us
  other arithmetic: 74.8 us -> 59.5 us
  between operations: 9.71 us -> 21.9 us
  Pallas kernels: 33.4 us -> 40 us
    ppermute x53 -> x27, waiting for transfers between devices: 203 us -> 59.1 us  [send(): return lax.ppermute(values, 'dp', shift_pairs(count, dim, amount))]
    all_gather x0 -> x2, waiting for transfers between devices: none -> 54.5 us  [the longest x1 27.7 us: local(): full_attn = lax.all_gather(attn_shard, 'dp', axis=0, tiled=True)]
    ppermute x9, waiting for transfers between devices: 84.7 us -> 49.2 us  [tensor_send(): lax.ppermute(values, 'tensor', [(r, (r + amount) % count) for r in range(...]
    ppermute x53 -> x27, starting transfers between devices: 65.9 us -> 32.4 us  [send(): return lax.ppermute(values, 'dp', shift_pairs(count, dim, amount))]
    dot_general x11 -> x2, matrix products: 29.6 us -> 5.43 us  [the longest x1 3.24 us: local(): jnp.einsum('gd,gc->dc', attn_in, d_qkv_low, preferred_element_type=jnp.fl...]
    unnamed x333 -> x251, local copies, waits for them, and re-layouts: 34.4 us -> 15.8 us
    convert_element_type x15 -> x5, other arithmetic: 24.7 us -> 7.79 us  [the longest x2 4.03 us: fold_rows(): (own.astype(jnp.float32) + came.astype(jnp.float32)).astype(kind)]
    another operation x9 -> x0, local copies, waits for them, and re-layouts: 12.7 us -> none  [the longest x3 6.87 us: local(): jnp.stack([part.reshape(row_share, blocks, 3, block) for part in sum_mlp]...]
  transfers between devices with their start and end apart: 67 -> 44, of which waited for: 33 -> 18; matrix products, arithmetic and copies ran while one was open for 27% -> 28% of each run, Pallas kernels for 3% -> 1%
where the time goes in v2:
time: 427 us; the launch traced here: 423 us
  waiting for transfers between devices  170 us (40%)
  other arithmetic  59.5 us (14%)
  starting transfers between devices  52.6 us (12%)
  local copies, waits for them, and re-layouts  46.8 us (11%)
  Pallas kernels  40 us (9%)
  matrix products  32.6 us (8%)
  between operations  21.9 us (5%)
    ppermute x27, waiting for transfers between devices, send(): return lax.ppermute(values, 'dp', shift_pairs(count, dim, amount))  59.1 us
    ppermute x9, waiting for transfers between devices, tensor_send(): lax.ppermute(values, 'tensor', [(r, (r + amount) % count) for r in range(...  49.2 us
    ppermute x27, starting transfers between devices, send(): return lax.ppermute(values, 'dp', shift_pairs(count, dim, amount))  32.4 us
    all_gather x1, waiting for transfers between devices, local(): full_attn = lax.all_gather(attn_shard, 'dp', axis=0, tiled=True)  27.7 us
    all_gather x1, waiting for transfers between devices, local(): full_mlp = lax.all_gather(mlp_shard, 'dp', axis=0, tiled=True)  26.8 us
    pallas_call x1, Pallas kernels, mlp_part(): pl.pallas_call(mlp_kernel, grid=(blocks,), in_specs=[whole, whole_t, whol...  25.5 us
    unnamed x251, local copies, waits for them, and re-layouts  15.8 us
    ppermute x9, starting transfers between devices, tensor_send(): lax.ppermute(values, 'tensor', [(r, (r + amount) % count) for r in range(...  11.1 us
  transfers between devices with their start and end apart: 44, of which 18 were waited for; matrix products, arithmetic and copies ran while one was open for 28% of the time, Pallas kernels for 1%

profile of v2, /device:TPU:0, one launch (start us, length us, event | category | flops | bytes accessed | tf_op | source)
XLA Modules:
  0.0 423.0 jit_solution(16011843954189450736)
XLA Ops:
  8.1 3.1 collective-permute-start.1
  37.6 4.6 %collective-permute-done.7 = f32[8,3840]{1,0:T(8,128)S(1)} collective-permute-done((f32[8,3840]{1,0:T(8,128)S(1)}, f32[8,3840]{1,0:T(8,128)S(1)}, u32[]{:S(2)}, u32[]{:S(2)}) %collective-permute-start.7) | collective-permute-done | bytes 122912 | tf_op jit(solution)/shard_map/ppermute | solution.py:213
  58.4 27.7 %all-gather.3.cloned.1.call-done = bf16[1152,2560]{1,0:T(8,128)(2,1)} async-done(((bf16[72,2560]{1,0:T(8,128)(2,1)}), bf16[1152,2560]{1,0:T(8,128)(2,1)}) %all-gather.3.cloned.1.call-update) | async-done | bytes 5898256 | tf_op jit(solution)/shard_map/all_gather | solution.py:634
  86.1 5.6 %fusion.8 = f32[512,1920]{1,0:T(8,128)S(1)} fusion(bf16[1152,2560]{1,0:T(8,128)(2,1)} %all-gather.3.cloned.1.call-done, f32[1152]{0:T(1024)S(1)} %get-tuple-element.253, f32[1152]{0:T(1024)S(1)} %get-tuple-element.254, f32[1152]{0:T(1024)S(1)} %get-tuple-element.255, f32[1152]{0:T(1024)S(1)} %get-tuple-element.256, f32[512]{0:T(512)S(1)} %add_rsqrt_fusion, ...), kind=kOutput, calls=%fused_computation.14 | convolution fusion | flops 2271412224 | bytes 9556480 | tf_op jit(solution)/shard_map/dot_general | solution.py:641
  106.4 3.2 convolution_convert_fusion.2
  111.3 26.6 %collective-permute-done.13 = bf16[512,1152]{1,0:T(8,128)(2,1)S(1)} collective-permute-done((bf16[512,1152]{1,0:T(8,128)(2,1)S(1)}, bf16[512,1152]{1,0:T(8,128)(2,1)S(1)}, u32[]{:S(2)}, u32[]{:S(2)}) %collective-permute-start.13) | collective-permute-done | bytes 1179680 | tf_op jit(solution)/shard_map/ppermute | solution.py:218
  138.0 3.8 multiply_reduce_fusion.2
  149.2 26.8 %all-gather.5.cloned.1.call-done.held = bf16[1152,4608]{1,0:T(8,128)(2,1)} async-done(((bf16[72,4608]{1,0:T(8,128)(2,1)}), bf16[1152,4608]{1,0:T(8,128)(2,1)}) %all-gather.5.cloned.1.call-update) | async-done | bytes 10616848 | tf_op jit(solution)/shard_map/all_gather | solution.py:635
  176.0 25.5 %shard_map.453 = (bf16[512,1152]{1,0:T(8,128)(2,1)}, bf16[512,1152]{1,0:T(8,128)(2,1)}, bf16[1152,4608]{1,0:T(8,128)(2,1)}) custom-call(bf16[512,1152]{1,0:T(8,128)(2,1)} %get-tuple-element.272.rows_ref, bf16[1152,512]{1,0:T(8,128)(2,1)} %copy.141.rows_t_ref, bf16[512,1152]{1,0:T(8,128)(2,1)} %get-tuple-element.351.grad_ref, ...), custom_call_target="tpu_custom_call" | custom-call | flops 16307453952 | bytes 21233664 | tf_op jit(solution)/shard_map/pallas_call | solution.py:402
  210.2 20.5 %collective-permute-done.15 = bf16[512,1152]{1,0:T(8,128)(2,1)} collective-permute-done((bf16[512,1152]{1,0:T(8,128)(2,1)}, bf16[512,1152]{1,0:T(8,128)(2,1)}, u32[]{:S(2)}, u32[]{:S(2)}) %collective-permute-start.15) | collective-permute-done | bytes 1179680 | tf_op jit(solution)/shard_map/ppermute | solution.py:218
  235.8 3.3 convolution_convert_fusion.3
  254.2 2.9 fusion.10
  259.6 3.2 convolution_convert_fusion
  275.6 4.3 %select_reduce_fusion.9 = (f32[1152]{0:T(1024)S(1)}, f32[1152]{0:T(1024)S(1)}, f32[256]{0:T(256)S(1)}, f32[1152]{0:T(1024)S(1)}, f32[1152]{0:T(1024)S(1)}, /*ind...) fusion(pred[256]{0:T(512)(128)(4,1)} %get-tuple-element.343, ...), kind=kLoop, calls=%fused_computation.76 | loop fusion | flops 8545280 | bytes 7707136 | tf_op jit(solution)/shard_map/reduce_sum | solution.py:629
  280.6 3.6 select_reduce_fusion.3
  285.1 2.9 fusion.17
  297.7 35.6 %collective-permute-done.31 = bf16[4,72,576]{2,1,0:T(8,128)(2,1)S(1)} collective-permute-done((bf16[4,72,576]{2,1,0:T(8,128)(2,1)S(1)}, bf16[4,72,576]{2,1,0:T(8,128)(2,1)S(1)}, u32[]{:S(2)}, u32[]{:S(2)}) %collective-permute-start.31) | collective-permute-done | bytes 331808 | tf_op jit(solution)/shard_map/ppermute | solution.py:213
  344.8 3.0 collective-permute-start.26
  355.0 11.1 %collective-permute-done.27 = bf16[72,1920]{1,0:T(8,128)(2,1)} collective-permute-done((bf16[72,1920]{1,0:T(8,128)(2,1)}, bf16[72,1920]{1,0:T(8,128)(2,1)}, u32[]{:S(2)}, u32[]{:S(2)}) %collective-permute-start.27) | collective-permute-done | bytes 276512 | tf_op jit(solution)/shard_map/ppermute | solution.py:213
  378.5 5.8 %collective-permute-start.37 = (f32[2,128]{1,0:T(2,128)S(1)}, f32[2,128]{1,0:T(2,128)S(1)}, u32[]{:S(2)}, u32[]{:S(2)}) collective-permute-start(f32[2,128]{1,0:T(2,128)S(1)} %fusion.90), channel_id=1, source_target_pairs={{0,8},{2,10},{4,12},{6,14},{8,0},{10,2},{12,4},{14,6},{16,24},{18,... | collective-permute-start | bytes 3080 | tf_op jit(solution)/shard_map/ppermute | solution.py:349
  384.3 3.0 copy_bitcast_fusion
  388.6 3.1 collective-permute-done.38
  399.2 9.7 %shard_map.454 = (f32[6,72,576]{2,1,0:T(8,128)}, f32[6,72,576]{2,1,0:T(8,128)}, f32[6,72,576]{2,1,0:T(8,128)}, f32[6,1152]{1,0:T(8,128)}, f32[6,1152]{1,0:T(8,12...) custom-call(f32[1,1]{1,0:T(1,128)} %bitcast.50.clip_ref, ...), custom_call_target="tpu_custom_call" | custom-call | tf_op jit(solution)/shard_map/pallas_call | solution.py:518
  409.0 2.9 copy.153
  (497 shorter events, 159.2 us)
Async XLA Ops:
  7.2 78.9 %all-gather.3.cloned.1.call-start = ((), (), s32[]{:S(2)}) async-start(), calls=%async_computation.1 | async-start | bytes 6266880 | tf_op jit(solution)/shard_map/all_gather | solution.py:634
  8.1 9.3 %collective-permute-start.1 = (s32[1,2,2]{2,1,0:T(2,128)S(1)}, s32[1,2,2]{2,1,0:T(2,128)S(1)}, u32[]{:S(2)}, u32[]{:S(2)}) collective-permute-start(s32[1,2,2]{2,1,0:T(2,128)S(1)} %add_bitcast_fusion.1), channel_id=1, source_target_pairs={{0,8},{2,10},{4,12},{6,14},{8,16},{10,18},{12,20},{14,22},{16,24},... | collective-permute-start | bytes 56 | tf_op jit(solution)/shard_map/ppermute | solution.py:213
  24.1 151.9 %all-gather.5.cloned.1.call-start = ((), (), s32[]{:S(2)}) async-start(), calls=%async_computation.2 | async-start | bytes 11280384 | tf_op jit(solution)/shard_map/all_gather | solution.py:635
  24.9 345.9 %reduce-scatter.2.cloned.1.call-start = ((), (), s32[]{:S(2)}) async-start(), calls=%async_computation.3 | async-start | bytes 11280384 | tf_op jit(solution)/shard_map/reduce_scatter | solution.py:665
  24.9 30.9 %collective-permute-start = (bf16[256,1152]{1,0:T(8,128)(2,1)S(1)}, bf16[256,1152]{1,0:T(8,128)(2,1)S(1)}, u32[]{:S(2)}, u32[]{:S(2)}) collective-permute-start(bf16[256,1152]{1,0:T(8,128)(2,1)S(1)} %copy-done.11), channel_id=1, source_target_pairs={{0,1},{1,0},{2,3},{3,2},{4,5},{5,4},{6,7},{7,6},{8,9},{9,8},{10,11... | collective-permute-start | bytes 1769480 | tf_op jit(solution)/shard_map/ppermute | solution.py:218
  26.5 29.7 %collective-permute-start.12 = (bf16[256,1152]{1,0:T(8,128)(2,1)}, bf16[256,1152]{1,0:T(8,128)(2,1)}, u32[]{:S(2)}, u32[]{:S(2)}) collective-permute-start(bf16[256,1152]{1,0:T(8,128)(2,1)} %param.29), channel_id=1, source_target_pairs={{0,1},{1,0},{2,3},{3,2},{4,5},{5,4},{6,7},{7,6},{8,9},{9,8},{10,11... | collective-permute-start | bytes 1769480 | tf_op jit(solution)/shard_map/ppermute | solution.py:218
  109.7 28.2 %collective-permute-start.13 = (bf16[512,1152]{1,0:T(8,128)(2,1)S(1)}, bf16[512,1152]{1,0:T(8,128)(2,1)S(1)}, u32[]{:S(2)}, u32[]{:S(2)}) collective-permute-start(bf16[512,1152]{1,0:T(8,128)(2,1)S(1)} %convolution_convert_fusion.2), channel_id=1, source_target_pairs={{0,1},{1,0},{2,3},{3,2},{4,5},{5,4},{6,7},{7,6},{8,9},{9,8},{10,11... | collective-permute-start | bytes 3538952 | tf_op jit(solution)/shard_map/ppermute | solution.py:218
  201.5 29.2 %collective-permute-start.15 = (bf16[512,1152]{1,0:T(8,128)(2,1)}, bf16[512,1152]{1,0:T(8,128)(2,1)}, u32[]{:S(2)}, u32[]{:S(2)}) collective-permute-start(bf16[512,1152]{1,0:T(8,128)(2,1)} %get-tuple-element.112), channel_id=1, source_target_pairs={{0,1},{1,0},{2,3},{3,2},{4,5},{5,4},{6,7},{7,6},{8,9},{9,8},{10,11... | collective-permute-start | bytes 3538952 | tf_op jit(solution)/shard_map/ppermute | solution.py:218
  209.5 66.0 %collective-permute-start.14 = (bf16[256,1152]{1,0:T(8,128)(2,1)}, bf16[256,1152]{1,0:T(8,128)(2,1)}, u32[]{:S(2)}, u32[]{:S(2)}) collective-permute-start(bf16[256,1152]{1,0:T(8,128)(2,1)} %slice.280), channel_id=1, source_target_pairs={{0,1},{1,0},{2,3},{3,2},{4,5},{5,4},{6,7},{7,6},{8,9},{9,8},{10,11... | collective-permute-start | bytes 1769480 | tf_op jit(solution)/shard_map/ppermute | solution.py:218
  258.0 17.5 %collective-permute-start.16 = (bf16[256,1152]{1,0:T(8,128)(2,1)}, bf16[256,1152]{1,0:T(8,128)(2,1)}, u32[]{:S(2)}, u32[]{:S(2)}) collective-permute-start(bf16[256,1152]{1,0:T(8,128)(2,1)} %slice.332), channel_id=1, source_target_pairs={{0,1},{1,0},{2,3},{3,2},{4,5},{5,4},{6,7},{7,6},{8,9},{9,8},{10,11... | collective-permute-start | bytes 1769480 | tf_op jit(solution)/shard_map/ppermute | solution.py:218
  265.6 19.5 %collective-permute-start.24 = (bf16[4,72,1920]{2,1,0:T(8,128)(2,1)}, bf16[4,72,1920]{2,1,0:T(8,128)(2,1)}, u32[]{:S(2)}, u32[]{:S(2)}) collective-permute-start(bf16[4,72,1920]{2,1,0:T(8,128)(2,1)} %get-tuple-element.277), channel_id=1, source_target_pairs={{0,2},{2,0},{4,6},{6,4},{8,10},{10,8},{12,14},{14,12},{16,18},{18,... | collective-permute-start | bytes 3317768 | tf_op jit(solution)/shard_map/ppermute | solution.py:213
  265.6 74.4 %collective-permute-start.23 = (bf16[4,72,1920]{2,1,0:T(8,128)(2,1)}, bf16[4,72,1920]{2,1,0:T(8,128)(2,1)}, u32[]{:S(2)}, u32[]{:S(2)}) collective-permute-start(bf16[4,72,1920]{2,1,0:T(8,128)(2,1)} %get-tuple-element.276), channel_id=1, source_target_pairs={{0,2},{2,0},{4,6},{6,4},{8,10},{10,8},{12,14},{14,12},{16,18},{18,... | collective-permute-start | bytes 3317768 | tf_op jit(solution)/shard_map/ppermute | solution.py:213
  273.0 19.0 %collective-permute-start.30 = (bf16[4,72,576]{2,1,0:T(8,128)(2,1)}, bf16[4,72,576]{2,1,0:T(8,128)(2,1)}, u32[]{:S(2)}, u32[]{:S(2)}) collective-permute-start(bf16[4,72,576]{2,1,0:T(8,128)(2,1)} %get-tuple-element.289), channel_id=1, source_target_pairs={{0,2},{2,0},{4,6},{6,4},{8,10},{10,8},{12,14},{14,12},{16,18},{18,... | collective-permute-start | bytes 995336 | tf_op jit(solution)/shard_map/ppermute | solution.py:213
  288.1 52.0 %collective-permute-start.25 = (bf16[4,72,1920]{2,1,0:T(8,128)(2,1)}, bf16[4,72,1920]{2,1,0:T(8,128)(2,1)}, u32[]{:S(2)}, u32[]{:S(2)}) collective-permute-start(bf16[4,72,1920]{2,1,0:T(8,128)(2,1)} %fusion.17), channel_id=1, source_target_pairs={{0,4},{2,6},{4,0},{6,2},{8,12},{10,14},{12,8},{14,10},{16,20},{18,... | collective-permute-start | bytes 3317768 | tf_op jit(solution)/shard_map/ppermute | solution.py:213
  295.5 37.8 %collective-permute-start.31 = (bf16[4,72,576]{2,1,0:T(8,128)(2,1)S(1)}, bf16[4,72,576]{2,1,0:T(8,128)(2,1)S(1)}, u32[]{:S(2)}, u32[]{:S(2)}) collective-permute-start(bf16[4,72,576]{2,1,0:T(8,128)(2,1)S(1)} %fusion.33), channel_id=1, source_target_pairs={{0,4},{2,6},{4,0},{6,2},{8,12},{10,14},{12,8},{14,10},{16,20},{18,... | collective-permute-start | bytes 995336 | tf_op jit(solution)/shard_map/ppermute | solution.py:213
  296.9 39.9 %collective-permute-start.21 = (f32[8,3840]{1,0:T(8,128)S(1)}, f32[8,3840]{1,0:T(8,128)S(1)}, u32[]{:S(2)}, u32[]{:S(2)}) collective-permute-start(f32[8,3840]{1,0:T(8,128)S(1)} %pad_maximum_fusion.4), channel_id=1, source_target_pairs={{0,4},{2,6},{4,0},{6,2},{8,12},{10,14},{12,8},{14,10},{16,20},{18,... | collective-permute-start | bytes 368648 | tf_op jit(solution)/shard_map/ppermute | solution.py:213
  334.2 9.4 %collective-permute-start.34 = (bf16[72,576]{1,0:T(8,128)(2,1)}, bf16[72,576]{1,0:T(8,128)(2,1)S(1)}, u32[]{:S(2)}, u32[]{:S(2)}) collective-permute-start(bf16[72,576]{1,0:T(8,128)(2,1)} %get-tuple-element.319), channel_id=1, source_target_pairs={{0,8},{2,10},{4,12},{6,14},{8,16},{10,18},{12,20},{14,22},{16,24},... | collective-permute-start | bytes 248840 | tf_op jit(solution)/shard_map/ppermute | solution.py:213
  334.2 10.6 %collective-permute-start.33 = (bf16[72,576]{1,0:T(8,128)(2,1)}, bf16[72,576]{1,0:T(8,128)(2,1)}, u32[]{:S(2)}, u32[]{:S(2)}) collective-permute-start(bf16[72,576]{1,0:T(8,128)(2,1)} %get-tuple-element.320), channel_id=1, source_target_pairs={{0,16},{2,18},{4,20},{6,22},{8,24},{10,26},{12,28},{14,30},{16,0},... | collective-permute-start | bytes 248840 | tf_op jit(solution)/shard_map/ppermute | solution.py:213
  336.9 11.0 %collective-permute-start.32 = (bf16[72,576]{1,0:T(8,128)(2,1)}, bf16[72,576]{1,0:T(8,128)(2,1)}, u32[]{:S(2)}, u32[]{:S(2)}) collective-permute-start(bf16[72,576]{1,0:T(8,128)(2,1)} %get-tuple-element.318), channel_id=1, source_target_pairs={{0,24},{2,26},{4,28},{6,30},{8,0},{10,2},{12,4},{14,6},{16,8},{18,... | collective-permute-start | bytes 248840 | tf_op jit(solution)/shard_map/ppermute | solution.py:213
  340.0 10.0 %collective-permute-start.22 = (f32[16,3840]{1,0:T(8,128)}, f32[16,3840]{1,0:T(8,128)S(1)}, u32[]{:S(2)}, u32[]{:S(2)}) collective-permute-start(f32[16,3840]{1,0:T(8,128)} %concatenate.71), channel_id=1, source_target_pairs={{0,2},{2,0},{4,6},{6,4},{8,10},{10,8},{12,14},{14,12},{16,18},{18,... | collective-permute-start | bytes 737288 | tf_op jit(solution)/shard_map/ppermute | solution.py:213
  343.3 11.7 %collective-permute-start.28 = (bf16[72,1920]{1,0:T(8,128)(2,1)}, bf16[72,1920]{1,0:T(8,128)(2,1)}, u32[]{:S(2)}, u32[]{:S(2)}) collective-permute-start(bf16[72,1920]{1,0:T(8,128)(2,1)} %get-tuple-element.285), channel_id=1, source_target_pairs={{0,8},{2,10},{4,12},{6,14},{8,16},{10,18},{12,20},{14,22},{16,24},... | collective-permute-start | bytes 829448 | tf_op jit(solution)/shard_map/ppermute | solution.py:213
  343.5 22.6 %collective-permute-start.27 = (bf16[72,1920]{1,0:T(8,128)(2,1)}, bf16[72,1920]{1,0:T(8,128)(2,1)}, u32[]{:S(2)}, u32[]{:S(2)}) collective-permute-start(bf16[72,1920]{1,0:T(8,128)(2,1)} %get-tuple-element.286), channel_id=1, source_target_pairs={{0,16},{2,18},{4,20},{6,22},{8,24},{10,26},{12,28},{14,30},{16,0},... | collective-permute-start | bytes 829448 | tf_op jit(solution)/shard_map/ppermute | solution.py:213
  344.8 21.4 %collective-permute-start.26 = (bf16[72,1920]{1,0:T(8,128)(2,1)}, bf16[72,1920]{1,0:T(8,128)(2,1)}, u32[]{:S(2)}, u32[]{:S(2)}) collective-permute-start(bf16[72,1920]{1,0:T(8,128)(2,1)} %get-tuple-element.284), channel_id=1, source_target_pairs={{0,24},{2,26},{4,28},{6,30},{8,0},{10,2},{12,4},{14,6},{16,8},{18,... | collective-permute-start | bytes 829448 | tf_op jit(solution)/shard_map/ppermute | solution.py:213
  375.1 13.5 %collective-permute-start.40 = (f32[6,576]{1,0:T(8,128)S(1)}, f32[6,576]{1,0:T(8,128)S(1)}, u32[]{:S(2)}, u32[]{:S(2)}) collective-permute-start(f32[6,576]{1,0:T(8,128)S(1)} %slice_add_fusion.7), channel_id=1, source_target_pairs={{0,1},{1,0},{2,3},{3,2},{4,5},{5,4},{6,7},{7,6},{8,9},{9,8},{10,11... | collective-permute-start | bytes 41480 | tf_op jit(solution)/shard_map/ppermute | solution.py:218
  (140 other events, 1212.0 us)
Sparse Core Ops, SparseCore 0:
  24.2 61.8 all-gather.2
  88.9 86.9 all-gather.4
  210.2 127.3 reduce-scatter.1

commit v3 on v2

--- a/solution.py
+++ b/solution.py
@@ -230,13 +230,20 @@
     return ((their_z * xside + their_x) * CORES + their_core).reshape(count)
 
 
-def gather_rows(shard):
+def near_rows(shard):
+    return jnp.concatenate([shard] + [send(shard, "z", hop) for hop in range(1, ZSIDE)], axis=0)
+
+
+def far_rows(near):
     xside = lax.axis_size("dp") // (ZSIDE * CORES)
-    near = jnp.concatenate([shard] + [send(shard, "z", hop) for hop in range(1, ZSIDE)], axis=0)
     mine = jnp.concatenate([near] + [send(near, "x", turn) for turn in range(1, xside)], axis=0)
     return jnp.concatenate([mine, send(mine, "core", 1)], axis=0)
 
 
+def gather_rows(shard):
+    return far_rows(near_rows(shard))
+
+
 def by_rows(values):
     return with_layout_constraint(values, Layout(tuple(range(values.ndim))))
 
@@ -246,28 +253,22 @@
 
 
 def fold_core(mine, other):
-    xside = lax.axis_size("dp") // (ZSIDE * CORES)
-    came = send(other, "core", 1)
-    rows = mine.shape[0] // xside
     parts = []
-    for turn in range(xside):
-        cut = slice(turn * rows, (turn + 1) * rows)
-        added = mine[cut].astype(jnp.float32) + came[cut].astype(jnp.float32)
-        parts.append(added.astype(mine.dtype))
+    for own, theirs in zip(mine, other):
+        came = send(theirs, "core", 1)
+        parts.append((own.astype(jnp.float32) + came.astype(jnp.float32)).astype(own.dtype))
     return parts
 
 
 def fold_x(parts):
-    came = [send(parts[turn], "x", -turn) for turn in range(1, len(parts))]
-    rows = parts[0].shape[0] // ZSIDE
-    cuts = []
-    for hop in range(ZSIDE):
-        cut = slice(hop * rows, (hop + 1) * rows)
-        added = parts[0][cut].astype(jnp.float32)
-        for piece in came:
-            added = added + piece[cut].astype(jnp.float32)
-        cuts.append(added.astype(parts[0].dtype))
-    return cuts
+    z = place_of(lax.axis_index("dp"), lax.axis_size("dp"))[0]
+    total = parts[0].astype(jnp.float32)
+    for turn in range(1, len(parts)):
+        total = total + send(parts[turn], "x", -turn).astype(jnp.float32)
+    total = total.astype(parts[0].dtype)
+    return [
+        lax.dynamic_index_in_dim(total, (z - hop) % ZSIDE, 0, keepdims=False) for hop in range(ZSIDE)
+    ]
 
 
 def fold_z(cuts):
@@ -278,7 +279,15 @@
 
 
 def reduce_rows(mine, other):
-    return fold_z(fold_x(fold_core(mine, other)))
+    xside = lax.axis_size("dp") // (ZSIDE * CORES)
+    total = mine + send(other, "core", 1)
+    for side, count in (("x", xside), ("z", ZSIDE)):
+        rows = total.shape[0] // count
+        cuts = [total[turn * rows : (turn + 1) * rows] for turn in range(count)]
+        total = cuts[0]
+        for turn in range(1, count):
+            total = total + send(cuts[turn], side, -turn)
+    return total
 
 
 def split_core(gradient):
@@ -296,26 +305,6 @@
     return halves
 
 
-def fold_rows(gradient):
-    z = place_of(lax.axis_index("dp"), lax.axis_size("dp"))[0]
-    kind = gradient.dtype
-    mine, other = split_core(gradient)
-    parts = []
-    for own, theirs in zip(mine, other):
-        came = send(theirs, "core", 1)
-        parts.append((own.astype(jnp.float32) + came.astype(jnp.float32)).astype(kind))
-    total = parts[0].astype(jnp.float32)
-    for turn in range(1, len(parts)):
-        total = total + send(parts[turn], "x", -turn).astype(jnp.float32)
-    cuts = [
-        lax.dynamic_index_in_dim(total, (z - hop) % ZSIDE, 0, keepdims=False) for hop in range(ZSIDE)
-    ]
-    total = cuts[0]
-    for hop in range(1, ZSIDE):
-        total = total + send(cuts[hop].astype(kind), "z", -hop).astype(jnp.float32)
-    return total
-
-
 def tensor_gather(values):
     count = lax.axis_size("tensor")
     return jnp.concatenate([values] + [tensor_send(values, hop) for hop in range(1, count)], axis=0)
@@ -351,8 +340,7 @@
     return values
 
 
-def mlp_kernel(rows_ref, rows_t_ref, grad_ref, grad_t_ref, held, *refs):
-    out_ref, in_ref, target, out_acc, in_acc = refs
+def mlp_kernel(rows_ref, grad_ref, held, out_ref, in_ref, act_ref, out_acc, in_acc):
     step = pl.program_id(0)
     width = held.shape[1] // 3
     gate_w = held[:, :width]
@@ -373,18 +361,13 @@
     hidden = (silu * up).astype(jnp.bfloat16)
     d_gate = (d_hidden * up * sigmoid * (1.0 + gate * (1.0 - sigmoid))).astype(jnp.bfloat16)
     d_up = (d_hidden * silu).astype(jnp.bfloat16)
+    act_ref[:, :width] = d_gate
+    act_ref[:, width : 2 * width] = d_up
+    act_ref[:, 2 * width :] = hidden
     out_acc[...] += lax.dot_general(hidden, down_w, across, preferred_element_type=jnp.float32)
     in_acc[...] += lax.dot_general(
         d_gate, gate_w, across, preferred_element_type=jnp.float32
     ) + lax.dot_general(d_up, up_w, across, preferred_element_type=jnp.float32)
-    rows_t = rows_t_ref[...]
-    for at, left, right in (
-        (0, rows_t, d_gate),
-        (width, rows_t, d_up),
-        (2 * width, grad_t_ref[...], hidden),
-    ):
-        product = jnp.dot(left, right, preferred_element_type=jnp.float32)
-        target[:, at : at + width] = product.astype(target.dtype)
 
     @pl.when(step == pl.num_programs(0) - 1)
     def _():
@@ -397,23 +380,57 @@
     columns = weights.shape[1]
     block = columns // blocks
     whole = pl.BlockSpec((count, width), lambda i: (0, 0))
-    whole_t = pl.BlockSpec((width, count), lambda i: (0, 0))
     across = pl.BlockSpec((width, block), lambda i: (0, i))
+    acts = pl.BlockSpec((count, block), lambda i: (0, i))
     return pl.pallas_call(
         mlp_kernel,
         grid=(blocks,),
-        in_specs=[whole, whole_t, whole, whole_t, across],
-        out_specs=[whole, whole, across],
+        in_specs=[whole, whole, across],
+        out_specs=[whole, whole, acts],
         out_shape=[jax.ShapeDtypeStruct((count, width), jnp.bfloat16)] * 2
-        + [jax.ShapeDtypeStruct((width, columns), jnp.bfloat16)],
+        + [jax.ShapeDtypeStruct((count, columns), jnp.bfloat16)],
         scratch_shapes=[pltpu.VMEM((count, width), jnp.float32)] * 2,
         cost_estimate=pl.CostEstimate(
-            flops=6 * count * width * columns,
-            bytes_accessed=4 * width * columns,
+            flops=4 * count * width * columns,
+            bytes_accessed=2 * width * columns,
             transcendentals=count * columns // 3,
         ),
         compiler_params=pltpu.CompilerParams(vmem_limit_bytes=60 * 1024 * 1024),
-    )(rows, rows.T, grad, grad.T, weights)
+    )(rows, grad, weights)
+
+
+def grad_kernel(rows_t_ref, grad_t_ref, *refs):
+    acts, target = refs[:-1], refs[-1]
+    width = target.shape[1] // 3
+    for at, left in ((0, rows_t_ref), (width, rows_t_ref), (2 * width, grad_t_ref)):
+        cut = slice(at, at + width)
+        begin = 0
+        product = None
+        for act_ref in acts:
+            rows = slice(begin, begin + act_ref.shape[0])
+            share = jnp.dot(left[:, rows], act_ref[:, cut], preferred_element_type=jnp.float32)
+            product = share if product is None else product + share
+            begin = rows.stop
+        target[:, cut] = product.astype(target.dtype)
+
+
+def grad_part(rows_t, grad_t, acts, blocks):
+    width, count = rows_t.shape
+    columns = acts[0].shape[1]
+    block = columns // blocks
+    whole = pl.BlockSpec((width, count), lambda i: (0, 0))
+    return pl.pallas_call(
+        grad_kernel,
+        grid=(blocks,),
+        in_specs=[whole, whole]
+        + [pl.BlockSpec((act.shape[0], block), lambda i: (0, i)) for act in acts],
+        out_specs=pl.BlockSpec((width, block), lambda i: (0, i)),
+        out_shape=jax.ShapeDtypeStruct((width, columns), jnp.bfloat16),
+        cost_estimate=pl.CostEstimate(
+            flops=2 * count * width * columns, bytes_accessed=2 * width * columns, transcendentals=0
+        ),
+        compiler_params=pltpu.CompilerParams(vmem_limit_bytes=60 * 1024 * 1024),
+    )(rows_t, grad_t, *acts)
 
 
 def mlp_plain(rows, grad, weights, blocks):
@@ -442,26 +459,35 @@
     return (out_sum.astype(jnp.bfloat16), in_sum.astype(jnp.bfloat16), packed)
 
 
-def pack_kernel(stride, block, qkv_ref, out_ref, gateup_ref, down_ref, attn_low, mlp_low):
+def pack_attn_kernel(qkv_ref, out_ref, target):
     columns = out_ref.shape[1]
-    attn_low[...] = jnp.zeros_like(attn_low)
     for slot in range(3):
-        attn_low[:, slot * stride : slot * stride + columns] = qkv_ref[slot].astype(jnp.bfloat16)
-    attn_low[:, 3 * stride : 3 * stride + columns] = out_ref[...].astype(jnp.bfloat16)
+        target[:, slot * columns : (slot + 1) * columns] = qkv_ref[slot].astype(target.dtype)
+    target[:, 3 * columns :] = out_ref[...].astype(target.dtype)
+
+
+def pack_attn(qkv, out):
+    rows, columns = out.shape
+    return pl.pallas_call(
+        pack_attn_kernel, out_shape=jax.ShapeDtypeStruct((rows, 4 * columns), jnp.bfloat16)
+    )(qkv, out)
+
+
+def pack_mlp_kernel(block, gateup_ref, down_ref, target):
     for begin in range(0, down_ref.shape[1], block):
         cut = slice(begin, begin + block)
         at = 3 * begin
-        mlp_low[:, at : at + block] = gateup_ref[0, :, cut].astype(jnp.bfloat16)
-        mlp_low[:, at + block : at + 2 * block] = gateup_ref[1, :, cut].astype(jnp.bfloat16)
-        mlp_low[:, at + 2 * block : at + 3 * block] = down_ref[:, cut].astype(jnp.bfloat16)
-
-
-def pack(qkv, out, gateup, down, stride, block):
+        target[:, at : at + block] = gateup_ref[0, :, cut].astype(target.dtype)
+        target[:, at + block : at + 2 * block] = gateup_ref[1, :, cut].astype(target.dtype)
+        target[:, at + 2 * block : at + 3 * block] = down_ref[:, cut].astype(target.dtype)
+
+
+def pack_mlp(gateup, down, block):
     rows, hidden = down.shape
-    low = lambda columns: jax.ShapeDtypeStruct((rows, columns), jnp.bfloat16)
     return pl.pallas_call(
-        partial(pack_kernel, stride, block), out_shape=[low(4 * stride), low(3 * hidden)]
-    )(qkv, out, gateup, down)
+        partial(pack_mlp_kernel, block),
+        out_shape=jax.ShapeDtypeStruct((rows, 3 * hidden), jnp.bfloat16),
+    )(gateup, down)
 
 
 def mod_kernel(stride, rows_ref, ada_ref, target):
@@ -480,43 +506,34 @@
     )(rows, ada)
 
 
-def adam_kernel(stride, block, rates, clip_ref, *refs):
+def adam_kernel(rates, clip_ref, *refs):
     clip = clip_ref[0, 0]
-    ada_g, qkv_g, out_g, mlp_g, bias_g, gain_g = refs[:6]
-    states, targets = refs[6:27], refs[27:]
-    ada, bias, qkv, out, gateup, down, gain = [
-        (states[3 * i : 3 * i + 3], targets[3 * i : 3 * i + 3], rates[i]) for i in range(7)
-    ]
-
-    def step(group, index, gradient):
-        held, put, rate = group
-        result = adam_update(*[ref[index] for ref in held], gradient, rate, clip)
-        for ref, value in zip(put, result):
-            ref[index] = value
-
-    columns = out[0][0].shape[1]
-    for group, source in ((ada, ada_g), (qkv, qkv_g)):
-        for slot in range(group[0][0].shape[0]):
-            step(group, slot, source[:, slot * stride : slot * stride + columns])
-    step(out, slice(None), out_g[:, :columns])
-    for begin in range(0, down[0][0].shape[1], block):
-        cut = slice(begin, begin + block)
-        at = 3 * begin
-        for slot, group, index in (
-            (0, gateup, (0, slice(None), cut)),
-            (1, gateup, (1, slice(None), cut)),
-            (2, down, (slice(None), cut)),
+    count = len(rates)
+    grads, states, targets = refs[:count], refs[count : 4 * count], refs[4 * count :]
+    for index, rate in enumerate(rates):
+        held = states[3 * index : 3 * index + 3]
+        put = targets[3 * index : 3 * index + 3]
+        paired = len(grads[index].shape) == 3 and grads[index].shape[1] == 2
+        rows = grads[index].shape[0 if paired else -2]
+        tall = 8 if rows % 8 == 0 else rows
+
+        def step(
+            at, carry, held=held, put=put, source=grads[index], rate=rate, tall=tall, paired=paired
         ):
-            gradient = mlp_g[:, at + slot * block : at + (slot + 1) * block]
-            step(group, index, gradient.astype(jnp.float32))
-    step(bias, slice(None), bias_g[...])
-    step(gain, slice(None), gain_g[...])
-
-
-def adam_all(clip, grads, states, stride, block, rates):
+            cut = pl.ds(at * tall, tall)
+            cell = (cut,) if paired or len(source.shape) == 2 else (slice(None), cut)
+            result = adam_update(*[ref[cell] for ref in held], source[cell], rate, clip)
+            for ref, value in zip(put, result):
+                ref[cell] = value
+            return carry
+
+        lax.fori_loop(0, rows // tall, step, 0)
+
+
+def adam_all(clip, grads, states, rates):
     vmem = pl.BlockSpec(memory_space=pltpu.VMEM)
     return pl.pallas_call(
-        partial(adam_kernel, stride, block, rates),
+        partial(adam_kernel, rates),
         in_specs=[pl.BlockSpec(memory_space=pltpu.SMEM)] + [vmem] * (len(grads) + len(states)),
         out_shape=[jax.ShapeDtypeStruct(x.shape, x.dtype) for x in states],
         compiler_params=pltpu.CompilerParams(vmem_limit_bytes=60 * 1024 * 1024),
@@ -575,12 +592,14 @@
     block = 256 if hidden_share % 512 == 0 else hidden_share
     blocks = hidden_share // block
     swap = lambda values: jnp.transpose(values, (1, 0, 2))
-    attn_shard, mlp_shard = pack(
-        swap(qkv_weight), out_weight, swap(gateup_weight), down_weight, stride, block
-    )
+    attn_shard = pack_attn(swap(qkv_weight), out_weight)
+    full_attn = lax.all_gather(attn_shard, "dp", axis=0, tiled=True)
+    mlp_shard = pack_mlp(swap(gateup_weight), down_weight, block)
+    full_mlp = lax.all_gather(mlp_shard, "dp", axis=0, tiled=True)
+    full_qkv = full_attn[:, : 3 * column_share]
+    full_out = full_attn[:, 3 * column_share :]
 
     ids = gather_rows(jnp.stack([class_id[0], timestep[0]])[None])
-    ids, attn_shard = gated(ids, attn_shard)
     item_ids = ids[:, 0].reshape(-1)
     item_steps = ids[:, 1].reshape(-1)
     class_onehot = (
@@ -604,8 +623,8 @@
         modulation = jnp.concatenate([lower, upper], axis=2)
     else:
         modulation = lax.all_gather(mod_share, "tensor", axis=2, tiled=True)
-    tokens_all = tensor_gather(tokens)
-    cot_all = tensor_gather(cotangent)
+    tokens_all = by_rows(tensor_gather(tokens))
+    cot_all = by_rows(tensor_gather(cotangent))
     base_rows = tokens_all.astype(jnp.float32)
     row_blocks = (tensor_rank - jnp.arange(tensor_count, dtype=jnp.int32)) % tensor_count
     row_index = (
@@ -631,16 +650,11 @@
             ]
         )
 
-    full_attn = lax.all_gather(attn_shard, "dp", axis=0, tiled=True)
-    full_mlp = lax.all_gather(mlp_shard, "dp", axis=0, tiled=True)
-    full_qkv = full_attn[:, : 3 * stride]
-    full_out = full_attn[:, 3 * stride : 3 * stride + column_share]
-
     attn_in = modulate_in(base_rows, mod_rows(1, group_rows), mod_rows(0, group_rows))
     attn_in = by_rows(attn_in.astype(bf16))
     qkv_raw = jnp.dot(attn_in, full_qkv, preferred_element_type=jnp.float32)
     raw_query, raw_key, raw_value = [
-        qkv_raw[:, slot * stride : slot * stride + column_share] for slot in range(3)
+        qkv_raw[:, slot * column_share : (slot + 1) * column_share] for slot in range(3)
     ]
     query_rot, key_rot = qk_prepare(raw_query, raw_key, qk_gain, tables)
     query_low = query_rot.astype(bf16)
@@ -651,30 +665,31 @@
     branch = jnp.einsum("gc,dc->gd", attn_low, full_out, preferred_element_type=jnp.float32)
     branch, cot_all = gated(by_rows(branch.astype(bf16)), cot_all)
     cot_rows = cot_all.astype(jnp.float32)
-    branch = tensor_total(branch)
-    mid_rows = base_rows + mod_rows(2, group_rows) * branch
+    branch = by_rows(tensor_total(branch))
+    mid_rows = by_rows(base_rows + mod_rows(2, group_rows) * branch)
     scale_two = mod_rows(4, group_rows)
-    mlp_in = modulate_in(mid_rows, scale_two, mod_rows(3, group_rows)).astype(bf16)
+    mlp_in = by_rows(modulate_in(mid_rows, scale_two, mod_rows(3, group_rows)).astype(bf16))
     gate_two = mod_rows(5, group_rows)
-    d_branch_mlp = (gate_two * cot_rows).astype(bf16)
+    d_branch_mlp = by_rows((gate_two * cot_rows).astype(bf16))
 
     if group_rows <= 512:
-        out_part, in_part, g_mlp = mlp_part(mlp_in, d_branch_mlp, full_mlp, blocks)
+        turned = (mlp_in.T, d_branch_mlp.T)
+        (mlp_in, d_branch_mlp), turned = gated((mlp_in, d_branch_mlp), turned)
+        out_part, in_part, acts = mlp_part(mlp_in, d_branch_mlp, full_mlp, blocks)
+        g_mlp = grad_part(*turned, (acts,), blocks)
     else:
         out_part, in_part, g_mlp = mlp_plain(mlp_in, d_branch_mlp, full_mlp, blocks)
     sum_mlp = lax.psum_scatter(g_mlp, "dp", scatter_dimension=0, tiled=True)
-    d_mlp_in = tensor_total(in_part)
-    branch_mlp = tensor_reduce(out_part)
+    d_mlp_in = by_rows(tensor_total(in_part))
+    branch_mlp = by_rows(tensor_reduce(out_part))
     out_rows = mid_rows[:local_rows] + gate_two[:local_rows] * branch_mlp
     out_tokens = out_rows.astype(bf16)
 
     d_mid_norm, d_scale_two, d_shift_two = jax.vjp(
         modulate_in, mid_rows, scale_two, jnp.zeros_like(mid_rows)
     )[1](d_mlp_in)
-    d_mid = cot_rows + d_mid_norm
+    d_mid = by_rows(cot_rows + d_mid_norm)
     d_branch_attn = by_rows((mod_rows(2, group_rows) * d_mid).astype(bf16))
-    g_out = jnp.einsum("gd,gc->dc", d_branch_attn, attn_low, preferred_element_type=jnp.float32)
-    sum_out = fold_rows(g_out.astype(bf16))
     d_attn = jnp.einsum("gd,dc->gc", d_branch_attn, full_out, preferred_element_type=jnp.float32)
     d_attn = d_attn.astype(bf16).reshape(query_low.shape)
     d_query_rot, d_key_rot, d_values = attend_back(
@@ -682,14 +697,22 @@
     )
     _, pull_qk = jax.vjp(partial(qk_prepare, tables=tables), raw_query, raw_key, qk_gain)
     d_query_raw, d_key_raw, g_gain = pull_qk((d_query_rot, d_key_rot))
-    spare = jnp.zeros((group_rows, stride - column_share), jnp.float32)
     d_qkv_low = jnp.concatenate(
-        [d_query_raw, spare, d_key_raw, spare, d_values.reshape(group_rows, -1), spare], axis=1
+        [d_query_raw, d_key_raw, d_values.reshape(group_rows, -1)], axis=1
     ).astype(bf16)
+    g_qkv = jnp.einsum("gd,gc->dc", attn_in, d_qkv_low, preferred_element_type=jnp.float32)
+    mine, other = split_core(by_rows(g_qkv.astype(bf16)))
+    other, d_qkv_low = gated(other, d_qkv_low)
     d_attn_part = jnp.einsum("gc,dc->gd", d_qkv_low, full_qkv, preferred_element_type=jnp.float32)
-    d_attn_in = tensor_reduce(by_rows(d_attn_part.astype(bf16)))
-    g_qkv = jnp.einsum("gd,gc->dc", attn_in, d_qkv_low, preferred_element_type=jnp.float32)
-    sum_qkv = fold_rows(g_qkv.astype(bf16))
+    turns, d_attn_part = gated(fold_core(mine, other), by_rows(d_attn_part.astype(bf16)))
+    d_attn_in = by_rows(tensor_reduce(d_attn_part))
+    turns, d_branch_attn = gated(turns, d_branch_attn)
+    g_out = jnp.einsum("gd,gc->dc", d_branch_attn, attn_low, preferred_element_type=jnp.float32)
+    out_turns = fold_core(*split_core(by_rows(g_out.astype(bf16))))
+    qkv_cuts = fold_x(turns)
+    qkv_cuts, (d_attn_in, out_turns) = gated(qkv_cuts, (d_attn_in, out_turns))
+    sum_qkv = fold_z(qkv_cuts)
+    out_cuts = fold_x(out_turns)
 
     own_scale = mod_rows(1, local_rows)
     d_base_norm, d_scale_one, d_shift_one = jax.vjp(
@@ -707,6 +730,8 @@
         ],
         axis=1,
     )
+    d_mod_part, out_cuts = gated(d_mod_part, out_cuts)
+    sum_out = fold_z(out_cuts)
     if tensor_count == 2:
         lower, upper = d_mod_part[:, :, :column_share], d_mod_part[:, :, column_share:]
         theirs = jnp.where(tensor_rank == 0, upper, lower)
@@ -714,7 +739,8 @@
     else:
         d_mod = lax.psum_scatter(d_mod_part, "tensor", scatter_dimension=2, tiled=True)
     d_mod = jnp.pad(d_mod, ((0, 0), (0, 0), (0, stride - column_share)))
-    d_mod_all = gather_rows(d_mod.reshape(item_count, 6 * stride))
+    d_mod_near = near_rows(d_mod.reshape(item_count, 6 * stride))
+    d_mod_all = far_rows(d_mod_near)
     sum_ada = lax.dot_general(
         silu_own.astype(jnp.float32),
         d_mod_all,
@@ -732,6 +758,7 @@
         bias_grad = lax.all_gather(bias_share, "tensor", axis=1, tiled=True)
 
     local_squares = jnp.sum(sum_ada * sum_ada) + jnp.sum(sum_qkv * sum_qkv)
+    local_squares = local_squares + jnp.sum(bias_share * bias_share) / data_count
     local_squares = local_squares + jnp.sum(sum_out * sum_out)
     local_squares = local_squares + jnp.sum(jnp.square(sum_mlp.astype(jnp.float32)))
     packet = jnp.concatenate(
@@ -744,7 +771,7 @@
     packet = everywhere_sum(packet).reshape(-1)
     gain_total = packet[: 2 * head_size].reshape(2, head_size)
     grad_norm = jnp.sqrt(
-        packet[2 * head_size] + jnp.sum(gain_total * gain_total) + jnp.sum(bias_grad * bias_grad)
+        packet[2 * head_size] + jnp.sum(gain_total * gain_total)
     )
     tokens_all_count = local_rows * tensor_count * data_count
     params_all = 10 * D * D + 3 * D * FF + 6 * D + 2 * HD
@@ -753,21 +780,41 @@
     matrix_rate = model_width ** (-0.5)
 
     out_rate = (model_width // 64) ** (-0.5)
-    rates = (matrix_rate, SMALL_RATE, matrix_rate, out_rate, matrix_rate, FF ** (-0.5), SMALL_RATE)
-    states = []
-    for group in (
-        (ada_weight, ada_m, ada_v),
-        (ada_bias, bias_m, bias_v),
-        (qkv_weight, qkv_m, qkv_v),
-        (out_weight, out_m, out_v),
-        (gateup_weight, gateup_m, gateup_v),
-        (down_weight, down_m, down_v),
-        (qk_gain, gain_m, gain_v),
-    ):
-        states += [swap(x) if x.ndim == 3 else x for x in group]
-    grads = [sum_ada, sum_qkv, sum_out, sum_mlp, bias_grad, gain_total]
-    updated = adam_all(clip, grads, states, stride, block, rates)
-    updated = [swap(x) if x.ndim == 3 else x for x in updated]
+    hidden_rate = FF ** (-0.5)
+    rates = (matrix_rate, SMALL_RATE, matrix_rate, out_rate, matrix_rate, hidden_rate, SMALL_RATE)
+    same = lambda values: values
+    views = (
+        ((ada_weight, ada_m, ada_v), swap, swap),
+        ((ada_bias, bias_m, bias_v), same, same),
+        ((qkv_weight, qkv_m, qkv_v), swap, swap),
+        ((out_weight, out_m, out_v), same, same),
+        ((gateup_weight, gateup_m, gateup_v), same, same),
+        ((down_weight, down_m, down_v), same, same),
+        ((qk_gain, gain_m, gain_v), same, same),
+    )
+    by_slot = lambda values, width: jnp.stack(
+        [values[:, at : at + column_share] for at in range(0, values.shape[1], width)]
+    )
+    mlp_split = sum_mlp.reshape(row_share, blocks, 3, block).astype(jnp.float32)
+    gateup_grad = jnp.stack(
+        [mlp_split[:, :, slot].reshape(row_share, hidden_share) for slot in range(2)], axis=1
+    )
+    grads = [
+        by_slot(sum_ada, stride),
+        bias_grad,
+        by_slot(sum_qkv, column_share),
+        sum_out,
+        gateup_grad,
+        mlp_split[:, :, 2].reshape(row_share, hidden_share),
+        gain_total,
+    ]
+    states = [view(x) for group, view, _ in views for x in group]
+    updated = adam_all(clip, grads, states, rates)
+    updated = [
+        back(updated[3 * index + slot])
+        for index, (_, _, back) in enumerate(views)
+        for slot in range(3)
+    ]
     return (
         out_tokens,
         input_grad,

time: 427 us -> 396 us (0.927)
  local copies, waits for them, and re-layouts: 46.8 us -> 32.5 us
  waiting for transfers between devices: 170 us -> 156 us
  starting transfers between devices: 52.6 us -> 43.5 us
  Pallas kernels: 40 us -> 48.6 us
    all_gather x1, waiting for transfers between devices: 27.7 us -> 10.6 us  [local(): full_attn = lax.all_gather(attn_shard, 'dp', axis=0, tiled=True)]
    convert_element_type x2 -> x6, other arithmetic: 4.03 us -> 13.8 us  [the longest x2 4.61 us: fold_core(): (own.astype(jnp.float32) + came.astype(jnp.float32)).astype(own.dtype)]
    pallas_call x3 -> x5, Pallas kernels: 37.7 us -> 46.4 us  [the longest x1 19 us: mlp_part(): pl.pallas_call(mlp_kernel, grid=(blocks,), in_specs=[whole, whole, across...]
    transpose x3 -> x0, local copies, waits for them, and re-layouts: 7.83 us -> none  [the longest x2 4.85 us: mlp_part(): return pl.pallas_call(mlp_kernel, grid=(blocks,), in_specs=[whole, whole_...]
    unnamed x251 -> x249, local copies, waits for them, and re-layouts: 15.8 us -> 9.24 us
    all_gather x1, waiting for transfers between devices: 26.8 us -> 32.4 us  [local(): full_mlp = lax.all_gather(mlp_shard, 'dp', axis=0, tiled=True)]
    another operation x7, local copies, waits for them, and re-layouts: 0.15 us -> 5.12 us  [local(): jnp.stack([mod_sums(d_shift_one), mod_sums(d_scale_one), mod_sums(d_mid[:...]
    another operation x0 -> x4, local copies, waits for them, and re-layouts: none -> 4.93 us  [the longest x2 4.8 us: by_rows(): return with_layout_constraint(values, Layout(tuple(range(values.ndim))))]
  transfers between devices with their start and end apart: 44 -> 44, of which waited for: 18 -> 23; matrix products, arithmetic and copies ran while one was open for 28% -> 29% of each run, Pallas kernels for 1% -> 4%
where the time goes in v3:
time: 396 us; the launch traced here: 392 us
  waiting for transfers between devices  156 us (39%)
  other arithmetic  60 us (15%)
  Pallas kernels  48.6 us (12%)
  starting transfers between devices  43.5 us (11%)
  local copies, waits for them, and re-layouts  32.5 us (8%)
  matrix products  30 us (8%)
  between operations  22 us (6%)
    ppermute x27, waiting for transfers between devices, send(): return lax.ppermute(values, 'dp', shift_pairs(count, dim, amount))  56.1 us
    ppermute x9, waiting for transfers between devices, tensor_send(): lax.ppermute(values, 'tensor', [(r, (r + amount) % count) for r in range(...  51.1 us
    all_gather x1, waiting for transfers between devices, local(): full_mlp = lax.all_gather(mlp_shard, 'dp', axis=0, tiled=True)  32.4 us
    ppermute x27, starting transfers between devices, send(): return lax.ppermute(values, 'dp', shift_pairs(count, dim, amount))  28.8 us
    pallas_call x1, Pallas kernels, mlp_part(): pl.pallas_call(mlp_kernel, grid=(blocks,), in_specs=[whole, whole, across...  19 us
    pallas_call x1, Pallas kernels, adam_all(): pl.pallas_call(partial(adam_kernel, rates), in_specs=[pl.BlockSpec(memory...  11.8 us
    pallas_call x1, Pallas kernels, grad_part(): pl.pallas_call(grad_kernel, grid=(blocks,), in_specs=[whole, whole] + [pl...  11.2 us
    all_gather x1, waiting for transfers between devices, local(): full_attn = lax.all_gather(attn_shard, 'dp', axis=0, tiled=True)  10.6 us
  transfers between devices with their start and end apart: 44, of which 23 were waited for; matrix products, arithmetic and copies ran while one was open for 29% of the time, Pallas kernels for 4%

profile of v3, /device:TPU:0, one launch (start us, length us, event | category | flops | bytes accessed | tf_op | source)
XLA Modules:
  0.0 392.3 jit_solution(4206441517532426458)
XLA Ops:
  12.9 3.1 collective-permute-start.1
  37.5 3.9 %collective-permute-done.7 = f32[8,3840]{1,0:T(8,128)S(1)} collective-permute-done((f32[8,3840]{1,0:T(8,128)S(1)}, f32[8,3840]{1,0:T(8,128)S(1)}, u32[]{:S(2)}, u32[]{:S(2)}) %collective-permute-start.7) | collective-permute-done | bytes 122912 | tf_op jit(solution)/shard_map/ppermute | solution.py:213
  42.1 3.8 collective-permute-start.8
  48.2 4.2 %collective-permute-done.9 = f32[2,3840]{1,0:T(2,128)S(1)} collective-permute-done((f32[2,3840]{1,0:T(2,128)S(1)}, f32[2,3840]{1,0:T(2,128)S(1)}, u32[]{:S(2)}, u32[]{:S(2)}) %collective-permute-start.9) | collective-permute-done | bytes 30752 | tf_op jit(solution)/shard_map/ppermute | solution.py:213
  59.8 10.6 %all-gather.3.cloned.1.call-done = bf16[1152,2304]{1,0:T(8,128)(2,1)} async-done(((bf16[72,2304]{1,0:T(8,128)(2,1)}), bf16[1152,2304]{1,0:T(8,128)(2,1)}) %all-gather.3.cloned.1.call-update) | async-done | bytes 5308432 | tf_op jit(solution)/shard_map/all_gather | solution.py:596
  70.4 5.0 %fusion.8 = f32[512,1728]{0,1:T(8,128)S(1)} fusion(bf16[1152,2304]{1,0:T(8,128)(2,1)} %all-gather.3.cloned.1.call-done, f32[1152]{0:T(1024)S(1)} %get-tuple-element.199, f32[1152]{0:T(1024)S(1)} %get-tuple-element.200, f32[1152]{0:T(1024)S(1)} %get-tuple-element.201, f32[1152]{0:T(1024)S(1)} %get-tuple-element.202, f32[512]{0:T(512)S(1)} %add_rsqrt_fusion, ...), kind=kOutput, calls=%fused_computation.14 | convolution fusion | flops 2044919808 | bytes 8868352 | tf_op jit(solution)/shard_map/dot_general | solution.py:655
  85.2 3.2 convolution_convert_fusion.2
  90.1 26.5 %collective-permute-done.13 = bf16[512,1152]{1,0:T(8,128)(2,1)S(1)} collective-permute-done((bf16[512,1152]{1,0:T(8,128)(2,1)S(1)}, bf16[512,1152]{1,0:T(8,128)(2,1)S(1)}, u32[]{:S(2)}, u32[]{:S(2)}) %collective-permute-start.13) | collective-permute-done | bytes 1179680 | tf_op jit(solution)/shard_map/ppermute | solution.py:218
  117.0 3.8 multiply_reduce_fusion.2
  128.1 32.4 %all-gather.5.cloned.1.call-done.held = bf16[1152,4608]{1,0:T(8,128)(2,1)} async-done(((bf16[72,4608]{1,0:T(8,128)(2,1)}), bf16[1152,4608]{1,0:T(8,128)(2,1)}) %all-gather.5.cloned.1.call-update) | async-done | bytes 10616848 | tf_op jit(solution)/shard_map/all_gather | solution.py:598
  160.4 19.0 %shard_map.454 = (bf16[512,1152]{1,0:T(8,128)(2,1)}, bf16[512,1152]{1,0:T(8,128)(2,1)}, bf16[512,4608]{1,0:T(8,128)(2,1)}) custom-call(bf16[512,1152]{1,0:T(8,128)(2,1)} %get-tuple-element.128.rows_ref, bf16[512,1152]{1,0:T(8,128)(2,1)} %get-tuple-element.129.grad_ref, bf16[1152,4608]{1,0:T(8,128)(2,1)} %all-gather.5.cloned.1.call-done.held), custom_call_target="tpu_custom_call" | custom-call | flops 10871635968 | bytes 10616832 | tf_op jit(solution)/shard_map/pallas_call | solution.py:385
  183.5 11.2 %shard_map.455 = bf16[1152,4608]{1,0:T(8,128)(2,1)} custom-call(bf16[1152,512]{1,0:T(8,128)(2,1)} %bitcast.198, bf16[1152,512]{1,0:T(8,128)(2,1)} %bitcast.199, bf16[512,4608]{1,0:T(8,128)(2,1)} %get-tuple-element.155.refs_0_), custom_call_target="tpu_custom_call" | custom-call | flops 5435817984 | bytes 10616832 | tf_op jit(solution)/shard_map/pallas_call | solution.py:422
  194.7 13.2 %collective-permute-done.15 = bf16[512,1152]{1,0:T(8,128)(2,1)} collective-permute-done((bf16[512,1152]{1,0:T(8,128)(2,1)}, bf16[512,1152]{1,0:T(8,128)(2,1)}, u32[]{:S(2)}, u32[]{:S(2)}) %collective-permute-start.15) | collective-permute-done | bytes 1179680 | tf_op jit(solution)/shard_map/ppermute | solution.py:218
  210.4 3.5 fusion.14
  214.0 4.0 %convolution_convert_fusion.3 = bf16[512,576]{0,1:T(8,128)(2,1)S(1)} fusion(bf16[512,1152]{1,0:T(8,128)(2,1)S(1)} %get-tuple-element.140, bf16[1152,2304]{1,0:T(8,128)(2,1)} %all-gather.3.cloned.1.call-done), kind=kOutput, calls=%fused_computation.52 | convolution fusion | flops 679772160 | bytes 3244032 | tf_op jit(solution)/shard_map/gd,dc->gc/dot_general | solution.py:693
  220.3 2.8 multiply_convert_fusion
  233.8 2.9 convolution_convert_fusion
  254.9 7.5 %collective-permute-done.19 = bf16[256,1152]{1,0:T(8,128)(2,1)} collective-permute-done((bf16[256,1152]{1,0:T(8,128)(2,1)S(1)}, bf16[256,1152]{1,0:T(8,128)(2,1)}, u32[]{:S(2)}, u32[]{:S(2)}) %collective-permute-start.19) | collective-permute-done | bytes 589856 | tf_op jit(solution)/shard_map/ppermute | solution.py:218
  263.9 18.0 %collective-permute-done.18 = bf16[4,72,1728]{2,1,0:T(8,128)(2,1)} collective-permute-done((bf16[4,72,1728]{2,1,0:T(8,128)(2,1)}, bf16[4,72,1728]{2,1,0:T(8,128)(2,1)}, u32[]{:S(2)}, u32[]{:S(2)}) %collective-permute-start.18) | collective-permute-done | bytes 995360 | tf_op jit(solution)/shard_map/ppermute | solution.py:213
  289.1 5.1 %select_reduce_fusion.3 = (f32[1152]{0:T(1024)S(1)}, f32[1152]{0:T(1024)S(1)}, f32[1152]{0:T(1024)S(1)}, f32[1152]{0:T(1024)S(1)}, bf16[256,1152]{1,0:T(8,128)(2...) fusion(pred[256]{0:T(512)(128)(4,1)S(1)} %copy-done.107, ...), kind=kLoop, calls=%fused_computation.71 | loop fusion | flops 11782400 | bytes 12453376 | tf_op jit(solution)/shard_map/reduce_sum | solution.py:648
  311.6 17.1 %collective-permute-done.30 = bf16[72,1728]{1,0:T(8,128)(2,1)} collective-permute-done((bf16[72,1728]{1,0:T(8,128)(2,1)}, bf16[72,1728]{1,0:T(8,128)(2,1)}, u32[]{:S(2)}, u32[]{:S(2)}) %collective-permute-start.30) | collective-permute-done | bytes 248864 | tf_op jit(solution)/shard_map/ppermute | solution.py:213
  331.7 2.6 collective-permute-start.32
  337.7 4.9 %collective-permute-done.33 = bf16[72,576]{1,0:T(8,128)(2,1)S(1)} collective-permute-done((bf16[72,576]{1,0:T(8,128)(2,1)}, bf16[72,576]{1,0:T(8,128)(2,1)S(1)}, u32[]{:S(2)}, u32[]{:S(2)}) %collective-permute-start.33) | collective-permute-done | bytes 82976 | tf_op jit(solution)/shard_map/ppermute | solution.py:213
  372.6 11.8 %shard_map.456 = (f32[6,72,576]{2,1,0:T(8,128)}, f32[6,72,576]{2,1,0:T(8,128)}, f32[6,72,576]{2,1,0:T(8,128)}, f32[6,1152]{1,0:T(8,128)}, f32[6,1152]{1,0:T(8,12...) custom-call(f32[1,1]{1,0:T(1,128)} %bitcast.50.clip_ref, ...), custom_call_target="tpu_custom_call" | custom-call | tf_op jit(solution)/shard_map/pallas_call | solution.py:535
  (501 shorter events, 150.3 us)
Async XLA Ops:
  7.2 63.1 %all-gather.3.cloned.1.call-start = ((), (), s32[]{:S(2)}) async-start(), calls=%async_computation.1 | async-start | bytes 5640192 | tf_op jit(solution)/shard_map/all_gather | solution.py:596
  9.4 151.0 %all-gather.5.cloned.1.call-start = ((), (), s32[]{:S(2)}) async-start(), calls=%async_computation.2 | async-start | bytes 11280384 | tf_op jit(solution)/shard_map/all_gather | solution.py:598
  12.8 336.1 %reduce-scatter.2.cloned.1.call-start = ((), (), s32[]{:S(2)}) async-start(), calls=%async_computation.3 | async-start | bytes 11280384 | tf_op jit(solution)/shard_map/reduce_scatter | solution.py:682
  12.9 9.8 %collective-permute-start.1 = (s32[1,2,2]{2,1,0:T(2,128)S(1)}, s32[1,2,2]{2,1,0:T(2,128)S(1)}, u32[]{:S(2)}, u32[]{:S(2)}) collective-permute-start(s32[1,2,2]{2,1,0:T(2,128)S(1)} %add_bitcast_fusion.1), channel_id=1, source_target_pairs={{0,8},{2,10},{4,12},{6,14},{8,16},{10,18},{12,20},{14,22},{16,24},... | collective-permute-start | bytes 56 | tf_op jit(solution)/shard_map/ppermute | solution.py:213
  20.0 37.3 %collective-permute-start = (bf16[256,1152]{1,0:T(8,128)(2,1)S(1)}, bf16[256,1152]{1,0:T(8,128)(2,1)S(1)}, u32[]{:S(2)}, u32[]{:S(2)}) collective-permute-start(bf16[256,1152]{1,0:T(8,128)(2,1)S(1)} %copy-done.11), channel_id=1, source_target_pairs={{0,1},{1,0},{2,3},{3,2},{4,5},{5,4},{6,7},{7,6},{8,9},{9,8},{10,11... | collective-permute-start | bytes 1769480 | tf_op jit(solution)/shard_map/ppermute | solution.py:218
  21.5 36.1 %collective-permute-start.12 = (bf16[256,1152]{1,0:T(8,128)(2,1)}, bf16[256,1152]{1,0:T(8,128)(2,1)}, u32[]{:S(2)}, u32[]{:S(2)}) collective-permute-start(bf16[256,1152]{1,0:T(8,128)(2,1)} %param.29), channel_id=1, source_target_pairs={{0,1},{1,0},{2,3},{3,2},{4,5},{5,4},{6,7},{7,6},{8,9},{9,8},{10,11... | collective-permute-start | bytes 1769480 | tf_op jit(solution)/shard_map/ppermute | solution.py:218
  88.4 28.2 %collective-permute-start.13 = (bf16[512,1152]{1,0:T(8,128)(2,1)S(1)}, bf16[512,1152]{1,0:T(8,128)(2,1)S(1)}, u32[]{:S(2)}, u32[]{:S(2)}) collective-permute-start(bf16[512,1152]{1,0:T(8,128)(2,1)S(1)} %convolution_convert_fusion.2), channel_id=1, source_target_pairs={{0,1},{1,0},{2,3},{3,2},{4,5},{5,4},{6,7},{7,6},{8,9},{9,8},{10,11... | collective-permute-start | bytes 3538952 | tf_op jit(solution)/shard_map/ppermute | solution.py:218
  179.5 28.4 %collective-permute-start.15 = (bf16[512,1152]{1,0:T(8,128)(2,1)}, bf16[512,1152]{1,0:T(8,128)(2,1)}, u32[]{:S(2)}, u32[]{:S(2)}) collective-permute-start(bf16[512,1152]{1,0:T(8,128)(2,1)} %get-tuple-element.131), channel_id=1, source_target_pairs={{0,1},{1,0},{2,3},{3,2},{4,5},{5,4},{6,7},{7,6},{8,9},{9,8},{10,11... | collective-permute-start | bytes 3538952 | tf_op jit(solution)/shard_map/ppermute | solution.py:218
  245.4 7.0 %collective-permute-start.20 = (bf16[4,72,576]{2,1,0:T(8,128)(2,1)}, bf16[4,72,576]{2,1,0:T(8,128)(2,1)S(1)}, u32[]{:S(2)}, u32[]{:S(2)}) collective-permute-start(bf16[4,72,576]{2,1,0:T(8,128)(2,1)} %get-tuple-element.239), channel_id=1, source_target_pairs={{0,2},{2,0},{4,6},{6,4},{8,10},{10,8},{12,14},{14,12},{16,18},{18,... | collective-permute-start | bytes 995336 | tf_op jit(solution)/shard_map/ppermute | solution.py:213
  245.6 6.9 %collective-permute-start.21 = (bf16[4,72,576]{2,1,0:T(8,128)(2,1)}, bf16[4,72,576]{2,1,0:T(8,128)(2,1)}, u32[]{:S(2)}, u32[]{:S(2)}) collective-permute-start(bf16[4,72,576]{2,1,0:T(8,128)(2,1)} %get-tuple-element.238), channel_id=1, source_target_pairs={{0,2},{2,0},{4,6},{6,4},{8,10},{10,8},{12,14},{14,12},{16,18},{18,... | collective-permute-start | bytes 995336 | tf_op jit(solution)/shard_map/ppermute | solution.py:213
  246.0 16.4 %collective-permute-start.19 = (bf16[256,1152]{1,0:T(8,128)(2,1)S(1)}, bf16[256,1152]{1,0:T(8,128)(2,1)}, u32[]{:S(2)}, u32[]{:S(2)}) collective-permute-start(bf16[256,1152]{1,0:T(8,128)(2,1)S(1)} %slice.298), channel_id=1, source_target_pairs={{0,1},{1,0},{2,3},{3,2},{4,5},{5,4},{6,7},{7,6},{8,9},{9,8},{10,11... | collective-permute-start | bytes 1769480 | tf_op jit(solution)/shard_map/ppermute | solution.py:218
  247.7 34.3 %collective-permute-start.18 = (bf16[4,72,1728]{2,1,0:T(8,128)(2,1)}, bf16[4,72,1728]{2,1,0:T(8,128)(2,1)}, u32[]{:S(2)}, u32[]{:S(2)}) collective-permute-start(bf16[4,72,1728]{2,1,0:T(8,128)(2,1)} %get-tuple-element.138), channel_id=1, source_target_pairs={{0,4},{2,6},{4,0},{6,2},{8,12},{10,14},{12,8},{14,10},{16,20},{18,... | collective-permute-start | bytes 2985992 | tf_op jit(solution)/shard_map/ppermute | solution.py:213
  251.1 37.9 %collective-permute-start.14 = (bf16[256,1152]{1,0:T(8,128)(2,1)}, bf16[256,1152]{1,0:T(8,128)(2,1)}, u32[]{:S(2)}, u32[]{:S(2)}) collective-permute-start(bf16[256,1152]{1,0:T(8,128)(2,1)} %slice.293), channel_id=1, source_target_pairs={{0,1},{1,0},{2,3},{3,2},{4,5},{5,4},{6,7},{7,6},{8,9},{9,8},{10,11... | collective-permute-start | bytes 1769480 | tf_op jit(solution)/shard_map/ppermute | solution.py:218
  284.9 26.4 %collective-permute-start.29 = (bf16[72,1728]{1,0:T(8,128)(2,1)}, bf16[72,1728]{1,0:T(8,128)(2,1)}, u32[]{:S(2)}, u32[]{:S(2)}) collective-permute-start(bf16[72,1728]{1,0:T(8,128)(2,1)} %get-tuple-element.146), channel_id=1, source_target_pairs={{0,24},{2,26},{4,28},{6,30},{8,0},{10,2},{12,4},{14,6},{16,8},{18,... | collective-permute-start | bytes 746504 | tf_op jit(solution)/shard_map/ppermute | solution.py:213
  286.3 42.3 %collective-permute-start.30 = (bf16[72,1728]{1,0:T(8,128)(2,1)}, bf16[72,1728]{1,0:T(8,128)(2,1)}, u32[]{:S(2)}, u32[]{:S(2)}) collective-permute-start(bf16[72,1728]{1,0:T(8,128)(2,1)} %get-tuple-element.147), channel_id=1, source_target_pairs={{0,16},{2,18},{4,20},{6,22},{8,24},{10,26},{12,28},{14,30},{16,0},... | collective-permute-start | bytes 746504 | tf_op jit(solution)/shard_map/ppermute | solution.py:213
  287.7 41.0 %collective-permute-start.31 = (bf16[72,1728]{1,0:T(8,128)(2,1)}, bf16[72,1728]{1,0:T(8,128)(2,1)}, u32[]{:S(2)}, u32[]{:S(2)}) collective-permute-start(bf16[72,1728]{1,0:T(8,128)(2,1)} %get-tuple-element.148), channel_id=1, source_target_pairs={{0,8},{2,10},{4,12},{6,14},{8,16},{10,18},{12,20},{14,22},{16,24},... | collective-permute-start | bytes 746504 | tf_op jit(solution)/shard_map/ppermute | solution.py:213
  288.0 12.4 %collective-permute-start.22 = (bf16[4,72,576]{2,1,0:T(8,128)(2,1)}, bf16[4,72,576]{2,1,0:T(8,128)(2,1)}, u32[]{:S(2)}, u32[]{:S(2)}) collective-permute-start(bf16[4,72,576]{2,1,0:T(8,128)(2,1)} %get-tuple-element.143), channel_id=1, source_target_pairs={{0,4},{2,6},{4,0},{6,2},{8,12},{10,14},{12,8},{14,10},{16,20},{18,... | collective-permute-start | bytes 995336 | tf_op jit(solution)/shard_map/ppermute | solution.py:213
  307.5 23.2 %collective-permute-start.24 = (f32[2,3840]{1,0:T(2,128)S(1)}, f32[2,3840]{1,0:T(2,128)S(1)}, u32[]{:S(2)}, u32[]{:S(2)}) collective-permute-start(f32[2,3840]{1,0:T(2,128)S(1)} %bitcast.204), channel_id=1, source_target_pairs={{0,8},{2,10},{4,12},{6,14},{8,16},{10,18},{12,20},{14,22},{16,24},... | collective-permute-start | bytes 92168 | tf_op jit(solution)/shard_map/ppermute | solution.py:213
  309.1 21.5 %collective-permute-start.25 = (f32[2,3840]{1,0:T(2,128)S(1)}, f32[2,3840]{1,0:T(2,128)S(1)}, u32[]{:S(2)}, u32[]{:S(2)}) collective-permute-start(f32[2,3840]{1,0:T(2,128)S(1)} %bitcast.205), channel_id=1, source_target_pairs={{0,16},{2,18},{4,20},{6,22},{8,24},{10,26},{12,28},{14,30},{16,0},... | collective-permute-start | bytes 92168 | tf_op jit(solution)/shard_map/ppermute | solution.py:213
  311.3 19.3 %collective-permute-start.26 = (f32[2,3840]{1,0:T(2,128)S(1)}, f32[2,3840]{1,0:T(2,128)S(1)}, u32[]{:S(2)}, u32[]{:S(2)}) collective-permute-start(f32[2,3840]{1,0:T(2,128)S(1)} %bitcast.206), channel_id=1, source_target_pairs={{0,24},{2,26},{4,28},{6,30},{8,0},{10,2},{12,4},{14,6},{16,8},{18,... | collective-permute-start | bytes 92168 | tf_op jit(solution)/shard_map/ppermute | solution.py:213
  334.3 8.3 %collective-permute-start.33 = (bf16[72,576]{1,0:T(8,128)(2,1)}, bf16[72,576]{1,0:T(8,128)(2,1)S(1)}, u32[]{:S(2)}, u32[]{:S(2)}) collective-permute-start(bf16[72,576]{1,0:T(8,128)(2,1)} %get-tuple-element.151), channel_id=1, source_target_pairs={{0,16},{2,18},{4,20},{6,22},{8,24},{10,26},{12,28},{14,30},{16,0},... | collective-permute-start | bytes 248840 | tf_op jit(solution)/shard_map/ppermute | solution.py:213
  334.3 8.3 %collective-permute-start.34 = (bf16[72,576]{1,0:T(8,128)(2,1)}, bf16[72,576]{1,0:T(8,128)(2,1)S(1)}, u32[]{:S(2)}, u32[]{:S(2)}) collective-permute-start(bf16[72,576]{1,0:T(8,128)(2,1)} %get-tuple-element.152), channel_id=1, source_target_pairs={{0,8},{2,10},{4,12},{6,14},{8,16},{10,18},{12,20},{14,22},{16,24},... | collective-permute-start | bytes 248840 | tf_op jit(solution)/shard_map/ppermute | solution.py:213
  335.8 8.2 %collective-permute-start.28 = (f32[16,3840]{1,0:T(8,128)S(1)}, f32[16,3840]{1,0:T(8,128)S(1)}, u32[]{:S(2)}, u32[]{:S(2)}) collective-permute-start(f32[16,3840]{1,0:T(8,128)S(1)} %concatenate.71), channel_id=1, source_target_pairs={{0,2},{2,0},{4,6},{6,4},{8,10},{10,8},{12,14},{14,12},{16,18},{18,... | collective-permute-start | bytes 737288 | tf_op jit(solution)/shard_map/ppermute | solution.py:213
  344.7 9.5 %collective-permute-start.40 = (f32[6,576]{1,0:T(8,128)S(1)}, f32[6,576]{1,0:T(8,128)S(1)}, u32[]{:S(2)}, u32[]{:S(2)}) collective-permute-start(f32[6,576]{1,0:T(8,128)S(1)} %get-tuple-element.215), channel_id=1, source_target_pairs={{0,1},{1,0},{2,3},{3,2},{4,5},{5,4},{6,7},{7,6},{8,9},{9,8},{10,11... | collective-permute-start | bytes 41480 | tf_op jit(solution)/shard_map/ppermute | solution.py:218
  (140 other events, 1208.3 us)
Sparse Core Ops, SparseCore 0:
  10.8 59.5 all-gather.2
  73.2 87.1 all-gather.4
  194.8 137.8 reduce-scatter.1

commit v4 on v3

--- a/solution.py
+++ b/solution.py
@@ -530,11 +530,24 @@
         lax.fori_loop(0, rows // tall, step, 0)
 
 
-def adam_all(clip, grads, states, rates):
-    vmem = pl.BlockSpec(memory_space=pltpu.VMEM)
+def adam_all(clip, grads, states, rates, row_share):
+    steps = 3 if row_share % 24 == 0 else 1
+
+    def spec_of(values):
+        shape = values.shape
+        if row_share not in shape[:-1]:
+            return pl.BlockSpec(shape, lambda i: (0,) * len(shape))
+        dim = shape.index(row_share)
+        block = tuple(size // steps if at == dim else size for at, size in enumerate(shape))
+        return pl.BlockSpec(
+            block, lambda i: tuple(i if at == dim else 0 for at in range(len(shape)))
+        )
+
     return pl.pallas_call(
         partial(adam_kernel, rates),
-        in_specs=[pl.BlockSpec(memory_space=pltpu.SMEM)] + [vmem] * (len(grads) + len(states)),
+        grid=(steps,),
+        in_specs=[pl.BlockSpec(memory_space=pltpu.SMEM)] + [spec_of(x) for x in grads + states],
+        out_specs=[spec_of(x) for x in states],
         out_shape=[jax.ShapeDtypeStruct(x.shape, x.dtype) for x in states],
         compiler_params=pltpu.CompilerParams(vmem_limit_bytes=60 * 1024 * 1024),
     )(clip.reshape(1, 1), *grads, *states)
@@ -809,7 +822,7 @@
         gain_total,
     ]
     states = [view(x) for group, view, _ in views for x in group]
-    updated = adam_all(clip, grads, states, rates)
+    updated = adam_all(clip, grads, states, rates, row_share)
     updated = [
         back(updated[3 * index + slot])
         for index, (_, _, back) in enumerate(views)

time: 396 us -> 395 us (level)
  no operation moved by 1% of the time
where the time goes in v4:
time: 395 us; the launch traced here: 391 us
  waiting for transfers between devices  156 us (39%)
  other arithmetic  60 us (15%)
  Pallas kernels  47.6 us (12%)
  starting transfers between devices  43.5 us (11%)
  local copies, waits for them, and re-layouts  32.5 us (8%)
  matrix products  30 us (8%)
  between operations  22 us (6%)
    ppermute x27, waiting for transfers between devices, send(): return lax.ppermute(values, 'dp', shift_pairs(count, dim, amount))  56.1 us
    ppermute x9, waiting for transfers between devices, tensor_send(): lax.ppermute(values, 'tensor', [(r, (r + amount) % count) for r in range(...  51.1 us
    all_gather x1, waiting for transfers between devices, local(): full_mlp = lax.all_gather(mlp_shard, 'dp', axis=0, tiled=True)  32.4 us
    ppermute x27, starting transfers between devices, send(): return lax.ppermute(values, 'dp', shift_pairs(count, dim, amount))  28.8 us
    pallas_call x1, Pallas kernels, mlp_part(): pl.pallas_call(mlp_kernel, grid=(blocks,), in_specs=[whole, whole, across...  19 us
    pallas_call x1, Pallas kernels, grad_part(): pl.pallas_call(grad_kernel, grid=(blocks,), in_specs=[whole, whole] + [pl...  11.2 us
    pallas_call x1, Pallas kernels, adam_all(): pl.pallas_call(partial(adam_kernel, rates), grid=(steps,), in_specs=[pl.B...  10.7 us
    all_gather x1, waiting for transfers between devices, local(): full_attn = lax.all_gather(attn_shard, 'dp', axis=0, tiled=True)  10.6 us
  transfers between devices with their start and end apart: 44, of which 23 were waited for; matrix products, arithmetic and copies ran while one was open for 29% of the time, Pallas kernels for 4%

profile of v4, /device:TPU:0, one launch (start us, length us, event | category | flops | bytes accessed | tf_op | source)
XLA Modules:
  0.0 391.2 jit_solution(3869295352897582448)
XLA Ops:
  12.9 3.1 collective-permute-start.1
  37.5 3.9 %collective-permute-done.7 = f32[8,3840]{1,0:T(8,128)S(1)} collective-permute-done((f32[8,3840]{1,0:T(8,128)S(1)}, f32[8,3840]{1,0:T(8,128)S(1)}, u32[]{:S(2)}, u32[]{:S(2)}) %collective-permute-start.7) | collective-permute-done | bytes 122912 | tf_op jit(solution)/shard_map/ppermute | solution.py:213
  42.1 3.8 collective-permute-start.8
  48.2 4.2 %collective-permute-done.9 = f32[2,3840]{1,0:T(2,128)S(1)} collective-permute-done((f32[2,3840]{1,0:T(2,128)S(1)}, f32[2,3840]{1,0:T(2,128)S(1)}, u32[]{:S(2)}, u32[]{:S(2)}) %collective-permute-start.9) | collective-permute-done | bytes 30752 | tf_op jit(solution)/shard_map/ppermute | solution.py:213
  59.8 10.6 %all-gather.3.cloned.1.call-done = bf16[1152,2304]{1,0:T(8,128)(2,1)} async-done(((bf16[72,2304]{1,0:T(8,128)(2,1)}), bf16[1152,2304]{1,0:T(8,128)(2,1)}) %all-gather.3.cloned.1.call-update) | async-done | bytes 5308432 | tf_op jit(solution)/shard_map/all_gather | solution.py:609
  70.4 5.0 %fusion.8 = f32[512,1728]{0,1:T(8,128)S(1)} fusion(bf16[1152,2304]{1,0:T(8,128)(2,1)} %all-gather.3.cloned.1.call-done, f32[1152]{0:T(1024)S(1)} %get-tuple-element.199, f32[1152]{0:T(1024)S(1)} %get-tuple-element.200, f32[1152]{0:T(1024)S(1)} %get-tuple-element.201, f32[1152]{0:T(1024)S(1)} %get-tuple-element.202, f32[512]{0:T(512)S(1)} %add_rsqrt_fusion, ...), kind=kOutput, calls=%fused_computation.14 | convolution fusion | flops 2044919808 | bytes 8868352 | tf_op jit(solution)/shard_map/dot_general | solution.py:668
  85.2 3.2 convolution_convert_fusion.2
  90.1 26.5 %collective-permute-done.13 = bf16[512,1152]{1,0:T(8,128)(2,1)S(1)} collective-permute-done((bf16[512,1152]{1,0:T(8,128)(2,1)S(1)}, bf16[512,1152]{1,0:T(8,128)(2,1)S(1)}, u32[]{:S(2)}, u32[]{:S(2)}) %collective-permute-start.13) | collective-permute-done | bytes 1179680 | tf_op jit(solution)/shard_map/ppermute | solution.py:218
  117.0 3.8 multiply_reduce_fusion.2
  128.1 32.4 %all-gather.5.cloned.1.call-done.held = bf16[1152,4608]{1,0:T(8,128)(2,1)} async-done(((bf16[72,4608]{1,0:T(8,128)(2,1)}), bf16[1152,4608]{1,0:T(8,128)(2,1)}) %all-gather.5.cloned.1.call-update) | async-done | bytes 10616848 | tf_op jit(solution)/shard_map/all_gather | solution.py:611
  160.4 19.0 %shard_map.454 = (bf16[512,1152]{1,0:T(8,128)(2,1)}, bf16[512,1152]{1,0:T(8,128)(2,1)}, bf16[512,4608]{1,0:T(8,128)(2,1)}) custom-call(bf16[512,1152]{1,0:T(8,128)(2,1)} %get-tuple-element.128.rows_ref, bf16[512,1152]{1,0:T(8,128)(2,1)} %get-tuple-element.129.grad_ref, bf16[1152,4608]{1,0:T(8,128)(2,1)} %all-gather.5.cloned.1.call-done.held), custom_call_target="tpu_custom_call" | custom-call | flops 10871635968 | bytes 10616832 | tf_op jit(solution)/shard_map/pallas_call | solution.py:385
  183.5 11.2 %shard_map.455 = bf16[1152,4608]{1,0:T(8,128)(2,1)} custom-call(bf16[1152,512]{1,0:T(8,128)(2,1)} %bitcast.198, bf16[1152,512]{1,0:T(8,128)(2,1)} %bitcast.199, bf16[512,4608]{1,0:T(8,128)(2,1)} %get-tuple-element.155.refs_0_), custom_call_target="tpu_custom_call" | custom-call | flops 5435817984 | bytes 10616832 | tf_op jit(solution)/shard_map/pallas_call | solution.py:422
  194.7 13.2 %collective-permute-done.15 = bf16[512,1152]{1,0:T(8,128)(2,1)} collective-permute-done((bf16[512,1152]{1,0:T(8,128)(2,1)}, bf16[512,1152]{1,0:T(8,128)(2,1)}, u32[]{:S(2)}, u32[]{:S(2)}) %collective-permute-start.15) | collective-permute-done | bytes 1179680 | tf_op jit(solution)/shard_map/ppermute | solution.py:218
  210.4 3.5 fusion.14
  214.0 4.0 %convolution_convert_fusion.3 = bf16[512,576]{0,1:T(8,128)(2,1)S(1)} fusion(bf16[512,1152]{1,0:T(8,128)(2,1)S(1)} %get-tuple-element.140, bf16[1152,2304]{1,0:T(8,128)(2,1)} %all-gather.3.cloned.1.call-done), kind=kOutput, calls=%fused_computation.52 | convolution fusion | flops 679772160 | bytes 3244032 | tf_op jit(solution)/shard_map/gd,dc->gc/dot_general | solution.py:706
  220.3 2.8 multiply_convert_fusion
  233.8 2.9 convolution_convert_fusion
  254.9 7.5 %collective-permute-done.19 = bf16[256,1152]{1,0:T(8,128)(2,1)} collective-permute-done((bf16[256,1152]{1,0:T(8,128)(2,1)S(1)}, bf16[256,1152]{1,0:T(8,128)(2,1)}, u32[]{:S(2)}, u32[]{:S(2)}) %collective-permute-start.19) | collective-permute-done | bytes 589856 | tf_op jit(solution)/shard_map/ppermute | solution.py:218
  263.9 18.0 %collective-permute-done.18 = bf16[4,72,1728]{2,1,0:T(8,128)(2,1)} collective-permute-done((bf16[4,72,1728]{2,1,0:T(8,128)(2,1)}, bf16[4,72,1728]{2,1,0:T(8,128)(2,1)}, u32[]{:S(2)}, u32[]{:S(2)}) %collective-permute-start.18) | collective-permute-done | bytes 995360 | tf_op jit(solution)/shard_map/ppermute | solution.py:213
  289.1 5.1 %select_reduce_fusion.3 = (f32[1152]{0:T(1024)S(1)}, f32[1152]{0:T(1024)S(1)}, f32[1152]{0:T(1024)S(1)}, f32[1152]{0:T(1024)S(1)}, bf16[256,1152]{1,0:T(8,128)(2...) fusion(pred[256]{0:T(512)(128)(4,1)S(1)} %copy-done.107, ...), kind=kLoop, calls=%fused_computation.71 | loop fusion | flops 11782400 | bytes 12453376 | tf_op jit(solution)/shard_map/reduce_sum | solution.py:661
  311.6 17.1 %collective-permute-done.30 = bf16[72,1728]{1,0:T(8,128)(2,1)} collective-permute-done((bf16[72,1728]{1,0:T(8,128)(2,1)}, bf16[72,1728]{1,0:T(8,128)(2,1)}, u32[]{:S(2)}, u32[]{:S(2)}) %collective-permute-start.30) | collective-permute-done | bytes 248864 | tf_op jit(solution)/shard_map/ppermute | solution.py:213
  331.7 2.6 collective-permute-start.32
  337.7 4.9 %collective-permute-done.33 = bf16[72,576]{1,0:T(8,128)(2,1)S(1)} collective-permute-done((bf16[72,576]{1,0:T(8,128)(2,1)}, bf16[72,576]{1,0:T(8,128)(2,1)S(1)}, u32[]{:S(2)}, u32[]{:S(2)}) %collective-permute-start.33) | collective-permute-done | bytes 82976 | tf_op jit(solution)/shard_map/ppermute | solution.py:213
  372.6 10.7 %shard_map.456 = (f32[6,72,576]{2,1,0:T(8,128)}, f32[6,72,576]{2,1,0:T(8,128)}, f32[6,72,576]{2,1,0:T(8,128)}, f32[6,1152]{1,0:T(8,128)}, f32[6,1152]{1,0:T(8,12...) custom-call(f32[1,1]{1,0:T(1,128)} %bitcast.50.clip_ref, ...), custom_call_target="tpu_custom_call" | custom-call | tf_op jit(solution)/shard_map/pallas_call | solution.py:546
  (501 shorter events, 150.3 us)
Async XLA Ops:
  7.2 63.1 %all-gather.3.cloned.1.call-start = ((), (), s32[]{:S(2)}) async-start(), calls=%async_computation.1 | async-start | bytes 5640192 | tf_op jit(solution)/shard_map/all_gather | solution.py:609
  9.4 151.0 %all-gather.5.cloned.1.call-start = ((), (), s32[]{:S(2)}) async-start(), calls=%async_computation.2 | async-start | bytes 11280384 | tf_op jit(solution)/shard_map/all_gather | solution.py:611
  12.8 336.1 %reduce-scatter.2.cloned.1.call-start = ((), (), s32[]{:S(2)}) async-start(), calls=%async_computation.3 | async-start | bytes 11280384 | tf_op jit(solution)/shard_map/reduce_scatter | solution.py:695
  12.9 9.8 %collective-permute-start.1 = (s32[1,2,2]{2,1,0:T(2,128)S(1)}, s32[1,2,2]{2,1,0:T(2,128)S(1)}, u32[]{:S(2)}, u32[]{:S(2)}) collective-permute-start(s32[1,2,2]{2,1,0:T(2,128)S(1)} %add_bitcast_fusion.1), channel_id=1, source_target_pairs={{0,8},{2,10},{4,12},{6,14},{8,16},{10,18},{12,20},{14,22},{16,24},... | collective-permute-start | bytes 56 | tf_op jit(solution)/shard_map/ppermute | solution.py:213
  20.0 37.3 %collective-permute-start = (bf16[256,1152]{1,0:T(8,128)(2,1)S(1)}, bf16[256,1152]{1,0:T(8,128)(2,1)S(1)}, u32[]{:S(2)}, u32[]{:S(2)}) collective-permute-start(bf16[256,1152]{1,0:T(8,128)(2,1)S(1)} %copy-done.11), channel_id=1, source_target_pairs={{0,1},{1,0},{2,3},{3,2},{4,5},{5,4},{6,7},{7,6},{8,9},{9,8},{10,11... | collective-permute-start | bytes 1769480 | tf_op jit(solution)/shard_map/ppermute | solution.py:218
  21.5 36.1 %collective-permute-start.12 = (bf16[256,1152]{1,0:T(8,128)(2,1)}, bf16[256,1152]{1,0:T(8,128)(2,1)}, u32[]{:S(2)}, u32[]{:S(2)}) collective-permute-start(bf16[256,1152]{1,0:T(8,128)(2,1)} %param.29), channel_id=1, source_target_pairs={{0,1},{1,0},{2,3},{3,2},{4,5},{5,4},{6,7},{7,6},{8,9},{9,8},{10,11... | collective-permute-start | bytes 1769480 | tf_op jit(solution)/shard_map/ppermute | solution.py:218
  88.4 28.2 %collective-permute-start.13 = (bf16[512,1152]{1,0:T(8,128)(2,1)S(1)}, bf16[512,1152]{1,0:T(8,128)(2,1)S(1)}, u32[]{:S(2)}, u32[]{:S(2)}) collective-permute-start(bf16[512,1152]{1,0:T(8,128)(2,1)S(1)} %convolution_convert_fusion.2), channel_id=1, source_target_pairs={{0,1},{1,0},{2,3},{3,2},{4,5},{5,4},{6,7},{7,6},{8,9},{9,8},{10,11... | collective-permute-start | bytes 3538952 | tf_op jit(solution)/shard_map/ppermute | solution.py:218
  179.5 28.4 %collective-permute-start.15 = (bf16[512,1152]{1,0:T(8,128)(2,1)}, bf16[512,1152]{1,0:T(8,128)(2,1)}, u32[]{:S(2)}, u32[]{:S(2)}) collective-permute-start(bf16[512,1152]{1,0:T(8,128)(2,1)} %get-tuple-element.131), channel_id=1, source_target_pairs={{0,1},{1,0},{2,3},{3,2},{4,5},{5,4},{6,7},{7,6},{8,9},{9,8},{10,11... | collective-permute-start | bytes 3538952 | tf_op jit(solution)/shard_map/ppermute | solution.py:218
  245.4 7.0 %collective-permute-start.20 = (bf16[4,72,576]{2,1,0:T(8,128)(2,1)}, bf16[4,72,576]{2,1,0:T(8,128)(2,1)S(1)}, u32[]{:S(2)}, u32[]{:S(2)}) collective-permute-start(bf16[4,72,576]{2,1,0:T(8,128)(2,1)} %get-tuple-element.239), channel_id=1, source_target_pairs={{0,2},{2,0},{4,6},{6,4},{8,10},{10,8},{12,14},{14,12},{16,18},{18,... | collective-permute-start | bytes 995336 | tf_op jit(solution)/shard_map/ppermute | solution.py:213
  245.6 6.9 %collective-permute-start.21 = (bf16[4,72,576]{2,1,0:T(8,128)(2,1)}, bf16[4,72,576]{2,1,0:T(8,128)(2,1)}, u32[]{:S(2)}, u32[]{:S(2)}) collective-permute-start(bf16[4,72,576]{2,1,0:T(8,128)(2,1)} %get-tuple-element.238), channel_id=1, source_target_pairs={{0,2},{2,0},{4,6},{6,4},{8,10},{10,8},{12,14},{14,12},{16,18},{18,... | collective-permute-start | bytes 995336 | tf_op jit(solution)/shard_map/ppermute | solution.py:213
  246.0 16.4 %collective-permute-start.19 = (bf16[256,1152]{1,0:T(8,128)(2,1)S(1)}, bf16[256,1152]{1,0:T(8,128)(2,1)}, u32[]{:S(2)}, u32[]{:S(2)}) collective-permute-start(bf16[256,1152]{1,0:T(8,128)(2,1)S(1)} %slice.298), channel_id=1, source_target_pairs={{0,1},{1,0},{2,3},{3,2},{4,5},{5,4},{6,7},{7,6},{8,9},{9,8},{10,11... | collective-permute-start | bytes 1769480 | tf_op jit(solution)/shard_map/ppermute | solution.py:218
  247.7 34.3 %collective-permute-start.18 = (bf16[4,72,1728]{2,1,0:T(8,128)(2,1)}, bf16[4,72,1728]{2,1,0:T(8,128)(2,1)}, u32[]{:S(2)}, u32[]{:S(2)}) collective-permute-start(bf16[4,72,1728]{2,1,0:T(8,128)(2,1)} %get-tuple-element.138), channel_id=1, source_target_pairs={{0,4},{2,6},{4,0},{6,2},{8,12},{10,14},{12,8},{14,10},{16,20},{18,... | collective-permute-start | bytes 2985992 | tf_op jit(solution)/shard_map/ppermute | solution.py:213
  251.1 37.9 %collective-permute-start.14 = (bf16[256,1152]{1,0:T(8,128)(2,1)}, bf16[256,1152]{1,0:T(8,128)(2,1)}, u32[]{:S(2)}, u32[]{:S(2)}) collective-permute-start(bf16[256,1152]{1,0:T(8,128)(2,1)} %slice.293), channel_id=1, source_target_pairs={{0,1},{1,0},{2,3},{3,2},{4,5},{5,4},{6,7},{7,6},{8,9},{9,8},{10,11... | collective-permute-start | bytes 1769480 | tf_op jit(solution)/shard_map/ppermute | solution.py:218
  284.9 26.4 %collective-permute-start.29 = (bf16[72,1728]{1,0:T(8,128)(2,1)}, bf16[72,1728]{1,0:T(8,128)(2,1)}, u32[]{:S(2)}, u32[]{:S(2)}) collective-permute-start(bf16[72,1728]{1,0:T(8,128)(2,1)} %get-tuple-element.146), channel_id=1, source_target_pairs={{0,24},{2,26},{4,28},{6,30},{8,0},{10,2},{12,4},{14,6},{16,8},{18,... | collective-permute-start | bytes 746504 | tf_op jit(solution)/shard_map/ppermute | solution.py:213
  286.3 42.3 %collective-permute-start.30 = (bf16[72,1728]{1,0:T(8,128)(2,1)}, bf16[72,1728]{1,0:T(8,128)(2,1)}, u32[]{:S(2)}, u32[]{:S(2)}) collective-permute-start(bf16[72,1728]{1,0:T(8,128)(2,1)} %get-tuple-element.147), channel_id=1, source_target_pairs={{0,16},{2,18},{4,20},{6,22},{8,24},{10,26},{12,28},{14,30},{16,0},... | collective-permute-start | bytes 746504 | tf_op jit(solution)/shard_map/ppermute | solution.py:213
  287.7 41.0 %collective-permute-start.31 = (bf16[72,1728]{1,0:T(8,128)(2,1)}, bf16[72,1728]{1,0:T(8,128)(2,1)}, u32[]{:S(2)}, u32[]{:S(2)}) collective-permute-start(bf16[72,1728]{1,0:T(8,128)(2,1)} %get-tuple-element.148), channel_id=1, source_target_pairs={{0,8},{2,10},{4,12},{6,14},{8,16},{10,18},{12,20},{14,22},{16,24},... | collective-permute-start | bytes 746504 | tf_op jit(solution)/shard_map/ppermute | solution.py:213
  288.0 12.4 %collective-permute-start.22 = (bf16[4,72,576]{2,1,0:T(8,128)(2,1)}, bf16[4,72,576]{2,1,0:T(8,128)(2,1)}, u32[]{:S(2)}, u32[]{:S(2)}) collective-permute-start(bf16[4,72,576]{2,1,0:T(8,128)(2,1)} %get-tuple-element.143), channel_id=1, source_target_pairs={{0,4},{2,6},{4,0},{6,2},{8,12},{10,14},{12,8},{14,10},{16,20},{18,... | collective-permute-start | bytes 995336 | tf_op jit(solution)/shard_map/ppermute | solution.py:213
  307.5 23.2 %collective-permute-start.24 = (f32[2,3840]{1,0:T(2,128)S(1)}, f32[2,3840]{1,0:T(2,128)S(1)}, u32[]{:S(2)}, u32[]{:S(2)}) collective-permute-start(f32[2,3840]{1,0:T(2,128)S(1)} %bitcast.204), channel_id=1, source_target_pairs={{0,8},{2,10},{4,12},{6,14},{8,16},{10,18},{12,20},{14,22},{16,24},... | collective-permute-start | bytes 92168 | tf_op jit(solution)/shard_map/ppermute | solution.py:213
  309.1 21.5 %collective-permute-start.25 = (f32[2,3840]{1,0:T(2,128)S(1)}, f32[2,3840]{1,0:T(2,128)S(1)}, u32[]{:S(2)}, u32[]{:S(2)}) collective-permute-start(f32[2,3840]{1,0:T(2,128)S(1)} %bitcast.205), channel_id=1, source_target_pairs={{0,16},{2,18},{4,20},{6,22},{8,24},{10,26},{12,28},{14,30},{16,0},... | collective-permute-start | bytes 92168 | tf_op jit(solution)/shard_map/ppermute | solution.py:213
  311.3 19.3 %collective-permute-start.26 = (f32[2,3840]{1,0:T(2,128)S(1)}, f32[2,3840]{1,0:T(2,128)S(1)}, u32[]{:S(2)}, u32[]{:S(2)}) collective-permute-start(f32[2,3840]{1,0:T(2,128)S(1)} %bitcast.206), channel_id=1, source_target_pairs={{0,24},{2,26},{4,28},{6,30},{8,0},{10,2},{12,4},{14,6},{16,8},{18,... | collective-permute-start | bytes 92168 | tf_op jit(solution)/shard_map/ppermute | solution.py:213
  334.3 8.3 %collective-permute-start.33 = (bf16[72,576]{1,0:T(8,128)(2,1)}, bf16[72,576]{1,0:T(8,128)(2,1)S(1)}, u32[]{:S(2)}, u32[]{:S(2)}) collective-permute-start(bf16[72,576]{1,0:T(8,128)(2,1)} %get-tuple-element.151), channel_id=1, source_target_pairs={{0,16},{2,18},{4,20},{6,22},{8,24},{10,26},{12,28},{14,30},{16,0},... | collective-permute-start | bytes 248840 | tf_op jit(solution)/shard_map/ppermute | solution.py:213
  334.3 8.3 %collective-permute-start.34 = (bf16[72,576]{1,0:T(8,128)(2,1)}, bf16[72,576]{1,0:T(8,128)(2,1)S(1)}, u32[]{:S(2)}, u32[]{:S(2)}) collective-permute-start(bf16[72,576]{1,0:T(8,128)(2,1)} %get-tuple-element.152), channel_id=1, source_target_pairs={{0,8},{2,10},{4,12},{6,14},{8,16},{10,18},{12,20},{14,22},{16,24},... | collective-permute-start | bytes 248840 | tf_op jit(solution)/shard_map/ppermute | solution.py:213
  335.8 8.2 %collective-permute-start.28 = (f32[16,3840]{1,0:T(8,128)S(1)}, f32[16,3840]{1,0:T(8,128)S(1)}, u32[]{:S(2)}, u32[]{:S(2)}) collective-permute-start(f32[16,3840]{1,0:T(8,128)S(1)} %concatenate.71), channel_id=1, source_target_pairs={{0,2},{2,0},{4,6},{6,4},{8,10},{10,8},{12,14},{14,12},{16,18},{18,... | collective-permute-start | bytes 737288 | tf_op jit(solution)/shard_map/ppermute | solution.py:213
  344.7 9.5 %collective-permute-start.40 = (f32[6,576]{1,0:T(8,128)S(1)}, f32[6,576]{1,0:T(8,128)S(1)}, u32[]{:S(2)}, u32[]{:S(2)}) collective-permute-start(f32[6,576]{1,0:T(8,128)S(1)} %get-tuple-element.215), channel_id=1, source_target_pairs={{0,1},{1,0},{2,3},{3,2},{4,5},{5,4},{6,7},{7,6},{8,9},{9,8},{10,11... | collective-permute-start | bytes 41480 | tf_op jit(solution)/shard_map/ppermute | solution.py:218
  (140 other events, 1207.3 us)
Sparse Core Ops, SparseCore 0:
  10.8 59.5 all-gather.2
  73.2 87.1 all-gather.4
  194.8 137.8 reduce-scatter.1
